TPU v7x, 128 devices: a whole 4x4x4 slice. The times are simulated.
128 devices in a mesh: dp: 8 (over x, y_hi), expert: 16 (over z, y_lo, core).
Axes of the slice: x: 4, y: 4 (y_hi: 2, y_lo: 2; y = y_hi * 2 + y_lo), z: 4, core: 2. Of those that a mesh axis runs over, the one named last changes fastest.
Arguments:
- tokens: bfloat16 [16384, 4096], P(('dp', 'expert')), may hold values from -6 to 6
- cotangent: bfloat16 [16384, 4096], P(('dp', 'expert')), may hold values from -3 to 3
- expert_ids: int32 [16384, 8, 2], P(('dp', 'expert')), may hold values from 0 to 31, as said below
- slot_ids: int32 [16384, 8, 2], P(('dp', 'expert')), may hold values from 0 to 63, as said below
- route_probs: bfloat16 [16384, 8, 2], P(('dp', 'expert')), may hold values from 0.099609375 to 1
- weights_in: bfloat16 [32, 2, 1792, 512], P('expert', None, 'dp'), may hold values from -0.25 to 0.25
- weights_out: bfloat16 [32, 1792, 512], P('expert', 'dp'), may hold values from -0.125 to 0.125
Outputs:
- grad_tokens: bfloat16 [16384, 4096], P(('dp', 'expert'))
- grad_probs: float32 [16384, 8, 2], P(('dp', 'expert'))
- grad_in: bfloat16 [32, 2, 1792, 512], P('expert', None, 'dp')
- grad_out: bfloat16 [32, 1792, 512], P('expert', 'dp')
Inputs may be any that keep to these rules, and one draw needn't show every extreme that they name: `expert_ids`: each sub-token names 2 different experts. On each device the experts fall into two sets of 16, and the two ids of a sub-token come one from each set. Every expert is named by exactly 64 sub-tokens of every device. `slot_ids`: for each device and expert, the sub-tokens of that device that name the expert carry distinct slot numbers at the matching position.
All inputs are finite; a program needn't handle non-finite values.
Results may differ from a plain program's by a relative error of at most 0.012.
Values may be sent and summed in bfloat16 or wider, within the bound.
No kernel may reach another device: no remote copies, remote signals or barrier semaphores. Data moves between devices by JAX's collectives and lax.ppermute only.
A program may use at most 192 MiB of HBM per device.

v0:
```python
import functools

import jax
import jax.numpy as jnp
from jax import lax
from jax.experimental import pallas as pl
from jax.experimental.pallas import tpu as pltpu
from jax.sharding import Mesh
from jax.sharding import PartitionSpec as P

H = 8
DS = 512
PEERS = 32
SLOTS = (40, 24)
GROUP = 8
SUBS = 1024
EXTRA = 8
SH = 224
F32 = jnp.float32
BF = jnp.bfloat16
AXES = ("x", "yh", "z", "yl", "core")
PLANE = ("yh", "z", "yl", "core")


def contract(a, b, ca, cb):
    return lax.dot_general(a, b, (((ca,), (cb,)), ((), ())), preferred_element_type=F32)


def in_hbm(a):
    return pltpu.with_memory_space_constraint(a, pltpu.HBM)


def params(mib=24):
    return pltpu.CompilerParams(vmem_limit_bytes=mib * 2**20)


def dispatch_kernel(table, tok, cot, out, *, part):
    slots = SLOTS[part]
    base = part * PEERS * SLOTS[0]
    x = jnp.concatenate([tok[:, h * DS : (h + 1) * DS] for h in range(H)], axis=0)
    c = jnp.concatenate([cot[:, h * DS : (h + 1) * DS] for h in range(H)], axis=0)
    code0 = table[0:1, :].astype(jnp.int32)
    code1 = table[1:2, :].astype(jnp.int32)
    prob0 = table[2:3, :]
    prob1 = table[3:4, :]
    block = GROUP * slots
    row = lax.broadcasted_iota(jnp.int32, (block, SUBS), 0) + (base + pl.program_id(0) * block)
    hit0 = row == code0
    hit1 = row == code1
    scale = jnp.where(hit0, prob0, jnp.where(hit1, prob1, 0.0)).astype(BF)
    pick = jnp.where(hit0 | hit1, 1.0, 0.0).astype(BF)
    out[:, 0:slots, :] = contract(pick, x, 1, 0).astype(BF).reshape(GROUP, slots, DS)
    out[:, slots : 2 * slots, :] = contract(scale, c, 1, 0).astype(BF).reshape(GROUP, slots, DS)


def dispatch(table, tok, cot, part):
    slots = SLOTS[part]
    fixed = lambda b: (0, 0)
    return pl.pallas_call(
        functools.partial(dispatch_kernel, part=part),
        grid=(PEERS // GROUP,),
        in_specs=[
            pl.BlockSpec((8, SUBS), fixed),
            pl.BlockSpec((SUBS // H, H * DS), fixed),
            pl.BlockSpec((SUBS // H, H * DS), fixed),
        ],
        out_specs=pl.BlockSpec((GROUP, 2 * slots, DS), lambda b: (b, 0, 0)),
        out_shape=pltpu.HBM((PEERS, 2 * slots, DS), BF),
        compiler_params=params(),
    )(table, tok, cot)


def expert_block(z, slots, wg, wu, wo):
    hidden = wg.shape[0]
    rows = PEERS * slots
    x = z[:, 0:slots, :].reshape(rows, DS)
    s = z[:, slots : 2 * slots, :].reshape(rows, DS)
    g = contract(wg, x, 1, 1)
    u = contract(wu, x, 1, 1)
    dh = contract(wo, s, 1, 1)
    sig = 0.5 * jnp.tanh(0.5 * g) + 0.5
    act = g * sig
    hid = (act * u).astype(BF)
    dhu = dh * u
    du = (dh * act).astype(BF)
    dg = (dhu * (sig + act * (1.0 - sig))).astype(BF)
    router = jnp.sum((dhu * act).reshape(hidden // 8, 8, rows), axis=0)
    dw = (contract(dg, x, 1, 0), contract(du, x, 1, 0), contract(hid, s, 1, 0))
    dx = contract(dg, wg, 0, 0) + contract(du, wu, 0, 0)
    return dw, dx, router


HBM = pl.BlockSpec(memory_space=pltpu.HBM)
WHOLE = pl.BlockSpec(memory_space=pltpu.VMEM)


def first_kernel(z_in, *refs):
    weights, (dw, dxo, router, z, wbuf, acc, stage, zsem, wsem, osem) = refs[:8], refs[8:]
    rows_in = pltpu.make_async_copy(z_in, z, zsem)
    rows_in.start()

    def fetch(k, slot):
        here = pl.ds(pl.multiple_of(slot * SH, SH), SH)
        return pltpu.make_async_copy(weights[k], wbuf.at[:, here, :], wsem.at[slot])

    def flush(j, slot):
        here = pl.ds(pl.multiple_of(j * 2 * SH, 2 * SH), 2 * SH)
        return pltpu.make_async_copy(stage.at[slot], dw.at[:, here, :], osem.at[slot])

    for k in range(8):
        fetch(k, k).start()
    acc[...] = jnp.zeros_like(acc)
    router[...] = jnp.zeros_like(router)
    rows_in.wait()

    def block(j, carry):
        fetch(0, 2 * j).wait()
        fetch(1, 2 * j + 1).wait()
        here = pl.ds(pl.multiple_of(j * 2 * SH, 2 * SH), 2 * SH)
        parts, dx, r = expert_block(
            z, SLOTS[0], wbuf[0, here, :], wbuf[1, here, :], wbuf[2, here, :]
        )
        slot = j % 2

        @pl.when(j >= 2)
        def _():
            flush(j - 2, slot).wait()

        for k in range(3):
            stage[slot, k] = parts[k]
        acc[...] += dx
        router[...] += r
        flush(j, slot).start()
        return carry

    lax.fori_loop(0, 4, block, 0)
    dxo[...] = acc[...].astype(BF).reshape(PEERS, SLOTS[0], DS)
    flush(2, 0).wait()
    flush(3, 1).wait()


def first_part(z, weights):
    rows = PEERS * SLOTS[0]
    return pl.pallas_call(
        first_kernel,
        in_specs=[HBM] * 9,
        out_specs=[HBM, WHOLE, WHOLE],
        out_shape=[
            pltpu.HBM((3, 8 * SH, DS), F32),
            pltpu.HBM((PEERS, SLOTS[0], DS), BF),
            jax.ShapeDtypeStruct((8, rows), F32),
        ],
        scratch_shapes=[
            pltpu.VMEM((PEERS, 2 * SLOTS[0], DS), BF),
            pltpu.VMEM((3, 8 * SH, DS), BF),
            pltpu.VMEM((rows, DS), F32),
            pltpu.VMEM((2, 3, 2 * SH, DS), F32),
            pltpu.SemaphoreType.DMA,
            pltpu.SemaphoreType.DMA((8,)),
            pltpu.SemaphoreType.DMA((2,)),
        ],
        compiler_params=params(40),
        name="first_part",
    )(*[in_hbm(a) for a in (z, *weights)])


def second_kernel(*refs, pairs, first, begin, end):
    n = 2 * pairs
    slots = SLOTS[1]
    z = refs[0]
    weights = refs[1 : 1 + n]
    before = refs[1 + n]
    pos = 2 + n
    if not begin:
        acc_in, router_in = refs[pos : pos + 2]
        pos += 2
    if end:
        router_first = refs[pos]
        pos += 1
    outs = refs[pos : pos + n]
    pos += n
    if end:
        back, router, acc, wbuf, stage, obuf, asem, wsem, bsem, ssem = refs[pos:]
    else:
        acc_out, router, acc, wbuf, stage, obuf, asem, wsem, bsem, ssem = refs[pos:]

    def fetch(k, slot):
        half = k % 2
        return pltpu.make_async_copy(
            weights[k], wbuf.at[slot, :, half * SH : (half + 1) * SH, :], wsem.at[slot, half]
        )

    def load(p):
        here = pl.ds(pl.multiple_of((first + p) * 2 * SH, 2 * SH), 2 * SH)
        return pltpu.make_async_copy(before.at[:, here, :], stage.at[p], bsem.at[p])

    def store(p, half):
        return pltpu.make_async_copy(
            obuf.at[p, :, half * SH : (half + 1) * SH, :], outs[2 * p + half], ssem.at[p, half]
        )

    for k in range(n):
        fetch(k, k // 2).start()
    for p in range(pairs):
        load(p).start()
    if begin:
        router[...] = jnp.zeros_like(router)
        acc[...] = jnp.zeros_like(acc)
    else:
        acc_load = pltpu.make_async_copy(acc_in, acc, asem)
        acc_load.start()
        router[...] = router_in[...]

    def block(p, carry):
        fetch(0, p).wait()
        fetch(1, p).wait()
        parts, dx, r = expert_block(z, slots, wbuf[p, 0], wbuf[p, 1], wbuf[p, 2])
        load(p).wait()
        for k in range(3):
            obuf[p, k] = (parts[k] + stage[p, k]).astype(BF)
        for q in range(pairs):

            @pl.when(p == q)
            def _():
                for half in range(2):
                    store(q, half).start()

        if not begin:

            @pl.when(p == 0)
            def _():
                acc_load.wait()

        acc[...] += dx
        router[...] += r
        return carry

    if pairs == 1:
        block(0, 0)
    else:
        lax.fori_loop(0, pairs, block, 0)

    def drain():
        for p in range(pairs):
            for half in range(2):
                store(p, half).wait()

    if not end:
        acc_save = pltpu.make_async_copy(acc, acc_out, asem)
        acc_save.start()
        drain()
        acc_save.wait()
        return
    back[:, 0:slots, :] = acc[...].astype(BF).reshape(PEERS, slots, DS)
    table = jnp.zeros((PEERS, 128), F32)
    for part, value in ((0, router_first[...]), (1, router[...])):
        count = SLOTS[part]
        total = PEERS * count
        source = lax.broadcasted_iota(jnp.int32, (PEERS, total), 0) * count
        row = lax.broadcasted_iota(jnp.int32, (PEERS, total), 1)
        flat = jnp.sum(value, axis=0, keepdims=True)
        spread = jnp.where((row >= source) & (row < source + count), flat, 0.0).astype(BF)
        slot = lax.broadcasted_iota(jnp.int32, (total, 128), 0) % count + part * SLOTS[0]
        lane = lax.broadcasted_iota(jnp.int32, (total, 128), 1)
        place = jnp.where(slot == lane, 1.0, 0.0).astype(BF)
        table = table + contract(spread, place, 1, 0)
    back[:, slots : slots + EXTRA, 0:128] = jnp.broadcast_to(
        table.astype(BF)[:, None, :], (PEERS, EXTRA, 128)
    )
    back[:, slots : slots + EXTRA, 128:DS] = jnp.zeros((PEERS, EXTRA, DS - 128), BF)
    drain()


def second_part(z, weights, before, first, carry=None, router_first=None):
    n = len(weights)
    end = router_first is not None
    rows = PEERS * SLOTS[1]
    args = [z, *[in_hbm(a) for a in (*weights, before)]]
    in_specs = [WHOLE] + [HBM] * (n + 1)
    if carry is not None:
        args += [in_hbm(carry[0]), carry[1]]
        in_specs += [HBM, WHOLE]
    if end:
        args += [router_first]
        in_specs += [WHOLE]
    out_shape = [pltpu.HBM((3, SH, DS), BF)] * n
    scratch = []
    if end:
        out_shape += [pltpu.HBM((PEERS, SLOTS[1] + EXTRA, DS), BF)]
        scratch += [pltpu.VMEM((8, rows), F32)]
        out_specs = [HBM] * n + [WHOLE]
    else:
        out_shape += [pltpu.HBM((rows, DS), F32), jax.ShapeDtypeStruct((8, rows), F32)]
        out_specs = [HBM] * (n + 1) + [WHOLE]
    scratch += [pltpu.VMEM((rows, DS), F32)]
    scratch += [
        pltpu.VMEM((n // 2, 3, 2 * SH, DS), BF),
        pltpu.VMEM((n // 2, 3, 2 * SH, DS), F32),
        pltpu.VMEM((n // 2, 3, 2 * SH, DS), BF),
        pltpu.SemaphoreType.DMA,
        pltpu.SemaphoreType.DMA((n // 2, 2)),
        pltpu.SemaphoreType.DMA((n // 2,)),
        pltpu.SemaphoreType.DMA((n // 2, 2)),
    ]
    return pl.pallas_call(
        functools.partial(
            second_kernel, pairs=n // 2, first=first, begin=carry is None, end=end
        ),
        in_specs=in_specs,
        out_specs=out_specs,
        out_shape=out_shape,
        scratch_shapes=scratch,
        compiler_params=params(30),
    )(*args)


def picks(codes, part, start, count):
    rows = PEERS * SLOTS[part]
    row = lax.broadcasted_iota(jnp.int32, (count, rows), 1) + part * PEERS * SLOTS[0]
    code0, code1 = (c[start : start + count] for c in codes)
    return jnp.where((row == code0) | (row == code1), 1.0, 0.0).astype(BF)


def columns(table):
    cols = jnp.transpose(table[...])
    whole = lambda k: cols[:, k : k + 1].astype(jnp.int32)
    return (whole(0), whole(1)), (cols[:, 2:3], cols[:, 3:4]), (whole(4), whole(5)), (whole(6), whole(7))


def combine_first_kernel(table, back, out):
    codes = columns(table)[0]
    rows = back[...].reshape(PEERS * SLOTS[0], DS)
    count = 256
    for b in range(SUBS // count):
        out[b * count : (b + 1) * count, :] = contract(
            picks(codes, 0, b * count, count), rows, 1, 0
        )


def combine_last_kernel(table, part, back, out, probs):
    codes, weight, peer, slot = columns(table)
    rows = back[:, 0 : SLOTS[1], :].reshape(PEERS * SLOTS[1], DS)
    count = 256
    n = count // 128
    for b in range(SUBS // count):
        got = contract(picks(codes, 1, b * count, count), rows, 1, 0)
        got = (got + part[b * count : (b + 1) * count, :]).astype(BF)
        for k in range(n):
            h = b * n + k
            out[:, h * DS : (h + 1) * DS] = got[k * 128 : (k + 1) * 128]
    routers = back[:, SLOTS[1] : SLOTS[1] + EXTRA, 0:128].reshape(PEERS * EXTRA, 128)
    source = lax.broadcasted_iota(jnp.int32, (SUBS, PEERS * EXTRA), 1)
    lane = lax.broadcasted_iota(jnp.int32, (SUBS, 128), 1)
    found = []
    for k in range(2):
        pick = jnp.where(source == peer[k] * EXTRA, 1.0, 0.0).astype(BF)
        line = contract(pick, routers, 1, 0)
        value = jnp.sum(jnp.where(lane == slot[k], line, 0.0), axis=1, keepdims=True)
        found.append(value / weight[k])
    both = jnp.where(lane == 0, found[0], jnp.where(lane == 1, found[1], 0.0))
    probs[...] = jnp.transpose(both)[0:8, :]


def combine_first(table, back):
    return pl.pallas_call(
        combine_first_kernel,
        out_shape=jax.ShapeDtypeStruct((SUBS, DS), F32),
        compiler_params=params(),
        name="combine_first",
    )(table, back)


def combine_last(table, part, back):
    return pl.pallas_call(
        combine_last_kernel,
        out_shape=[
            jax.ShapeDtypeStruct((SUBS // H, H * DS), BF),
            jax.ShapeDtypeStruct((8, SUBS), F32),
        ],
        compiler_params=params(),
        name="combine_last",
    )(table, part, back)


def final_kernel(which, own0, own1, own2, other, grad_in, grad_out):
    a = which[0]
    b = 1 - a
    for k in range(3):
        total = own0[k].astype(F32) + own1[k].astype(F32) + own2[k].astype(F32)
        total = total.astype(BF)
        if k < 2:
            grad_in[a, k] = total
            grad_in[b, k] = other[k]
        else:
            grad_out[a] = total
            grad_out[b] = other[k]


def final(which, own, other):
    vmem = pl.BlockSpec(memory_space=pltpu.VMEM)
    return pl.pallas_call(
        final_kernel,
        in_specs=[pl.BlockSpec(memory_space=pltpu.SMEM)] + [vmem] * 4,
        out_shape=[
            jax.ShapeDtypeStruct((2, 2, SH, DS), BF),
            jax.ShapeDtypeStruct((2, SH, DS), BF),
        ],
        compiler_params=params(),
        name="final",
    )(which, *own, other)


def ring(a, step):
    return lax.ppermute(a, "x", [(i, (i + step) % 4) for i in range(4)])


def swap(a):
    return lax.ppermute(a, "yh", [(0, 1), (1, 0)])


def exchange(a):
    return lax.all_to_all(a, PLANE, 0, 0, tiled=True)


def add(*arrays):
    return sum(a.astype(F32) for a in arrays).astype(BF)


def layer(tokens, cotangent, expert_ids, slot_ids, route_probs, weights_in, weights_out):
    yh = lax.axis_index("yh")
    both = jnp.concatenate([weights_in, weights_out[:, None]], axis=1)
    theirs = jnp.where(yh == 0, both[1], both[0])
    w_o = jnp.where(yh == 0, both[0], both[1])
    w_p = swap(theirs)
    w_o_m = ring(w_o, 1)
    w_o_p = ring(w_o, -1)
    w_p_m = ring(w_p, 1)
    w_p_p = ring(w_p, -1)
    w_o_2 = ring(w_o_m, 1)
    w_p_2 = ring(w_p_p, -1)

    dest = expert_ids % 2 * (PEERS // 2) + expert_ids // 2
    code = jnp.where(
        slot_ids < SLOTS[0],
        dest * SLOTS[0] + slot_ids,
        PEERS * SLOTS[0] + dest * SLOTS[1] + slot_ids - SLOTS[0],
    )
    table = [code, route_probs, dest, slot_ids]
    table = jnp.concatenate([t.astype(F32) for t in table], axis=2)
    table = jnp.transpose(table, (2, 1, 0)).reshape(8, SUBS)

    z1 = exchange(dispatch(table, tokens, cotangent, 0))
    z2 = exchange(dispatch(table, tokens, cotangent, 1))

    weights = [w_o_2, w_p_2, w_o_p, w_p_p, w_o_m, w_p_m, w_o, w_p]
    dw_first, back1, router1 = first_part(z1, weights)
    back1 = exchange(back1)
    o_2, p_2, *carry = second_part(z2, weights[0:2], dw_first, 0)
    o_2 = ring(o_2, 1)
    p_2 = ring(p_2, -1)
    o_p, p_p, o_m, p_m, *carry = second_part(z2, weights[2:6], dw_first, 1, carry)
    p_p = ring(p_p, 1)
    p_m = ring(add(p_m, p_2), -1)
    o_p = ring(add(o_p, o_2), 1)
    o_m = ring(o_m, -1)
    o_0, p_0, back2 = second_part(z2, weights[6:8], dw_first, 3, carry, router1)
    back2 = exchange(back2)

    other = swap(add(p_0, p_p, p_m))
    grad_in, grad_out = final(yh.astype(jnp.int32).reshape(1), (o_0, o_p, o_m), other)

    part = combine_first(table, back1)
    grad_tokens, probs = combine_last(table, part, back2)
    grad_probs = jnp.transpose(probs[0:2].reshape(2, H, SUBS // H), (2, 1, 0))
    return grad_tokens, grad_probs, grad_in, grad_out


def solution(mesh):
    wide = Mesh(mesh.devices.reshape(4, 2, 4, 2, 2), AXES)
    dp = ("x", "yh")
    expert = ("z", "yl", "core")
    rows2 = P(AXES, None)
    rows3 = P(AXES, None, None)
    w_in = P(expert, None, dp, None)
    w_out = P(expert, dp, None)
    return jax.shard_map(
        layer,
        mesh=wide,
        in_specs=(rows2, rows2, rows3, rows3, rows3, w_in, w_out),
        out_specs=(rows2, rows3, w_in, w_out),
        check_vma=False,
    )
```

profile of v0, /device:TPU:0, one launch (start us, length us, event | category | flops | bytes accessed | tf_op | source)
XLA Modules:
  0.0 225.9 jit_solution(11805303170138351136)
XLA Ops:
  0.6 0.8 fusion.1
  1.5 0.7 convert_element_type.43
  2.2 1.2 copy-done
  3.4 1.2 copy-done.2
  4.6 4.3 %shard_map.102 = bf16[32,80,512]{2,1,0:T(8,128)(2,1)} custom-call(f32[8,1024]{1,0:T(8,128)S(1)} %maximum_bitcast_fusion.table, bf16[128,4096]{1,0:T(8,128)(2,1)S(1)} %copy-done, bf16[128,4096]{1,0:T(8,128)(2,1)S(1)} %copy-done.2), custom_call_target="tpu_custom_call" | custom-call | tf_op jit(solution)/shard_map/pallas_call | solution.py:59
  8.9 8.4 %all-to-all-start = ((bf16[32,80,512]{2,1,0:T(8,128)(2,1)}), bf16[32,80,512]{2,1,0:T(8,128)(2,1)S(1)}, u32[]{:S(2)}, u32[]{:S(2)}) async-start(bf16[32,80,512]{2,1,0:T(8,128)(2,1)} %shard_map.102), calls=%async_computation | async-start | bytes 5242880 | tf_op jit(solution)/shard_map/all_to_all | solution.py:422
  17.4 2.7 %select_bitcast_fusion = (bf16[3,224,512]{2,1,0:T(8,128)(2,1)}, bf16[3,224,512]{2,1,0:T(8,128)(2,1)S(1)}) fusion(pred[]{:T(512)S(6)} %eq.6, bf16[2,1,224,512]{3,2,1,0:T(8,128)(2,1)} %bitcast.14, bf16[2,2,224,512]{3,2,1,0:T(8,128)(2,1)} %param.12), kind=kLoop, calls=%fused_computation.7 | loop fusion | flops 1720320 | bytes 2752513 | tf_op jit(solution)/shard_map/jit(_where)/select_n | solution.py:432
  20.1 3.3 %collective-permute-start.2 = (bf16[3,224,512]{2,1,0:T(8,128)(2,1)}, bf16[3,224,512]{2,1,0:T(8,128)(2,1)}, u32[]{:S(2)}, u32[]{:S(2)}) collective-permute-start(bf16[3,224,512]{2,1,0:T(8,128)(2,1)} %get-tuple-element.46), channel_id=1, source_target_pairs={{0,16},{16,0},{1,17},{17,1},{2,18},{18,2},{3,19},{19,3},{4,20},{20... | collective-permute-start | bytes 2064392 | tf_op jit(solution)/shard_map/ppermute | solution.py:418
  23.4 3.2 %shard_map.103 = bf16[32,48,512]{2,1,0:T(8,128)(2,1)} custom-call(f32[8,1024]{1,0:T(8,128)S(1)} %maximum_bitcast_fusion.table, bf16[128,4096]{1,0:T(8,128)(2,1)S(1)} %copy-done.1, bf16[128,4096]{1,0:T(8,128)(2,1)S(1)} %copy-done.3), custom_call_target="tpu_custom_call" | custom-call | tf_op jit(solution)/shard_map/pallas_call | solution.py:59
  26.7 24.2 %all-to-all-done.z_in = bf16[32,80,512]{2,1,0:T(8,128)(2,1)S(1)} async-done(((bf16[32,80,512]{2,1,0:T(8,128)(2,1)}), bf16[32,80,512]{2,1,0:T(8,128)(2,1)S(1)}, u32[]{:S(2)}, u32[]{:S(2)}) %all-to-all-start) | async-done | bytes 2621472 | tf_op jit(solution)/shard_map/all_to_all | solution.py:422
  50.9 1.5 copy-done.5
  52.4 7.4 %all-to-all-start.2 = ((bf16[32,48,512]{2,1,0:T(8,128)(2,1)}), bf16[32,48,512]{2,1,0:T(8,128)(2,1)S(1)}, u32[]{:S(2)}, u32[]{:S(2)}) async-start(bf16[32,48,512]{2,1,0:T(8,128)(2,1)} %shard_map.103), calls=%async_computation.2 | async-start | bytes 3145728 | tf_op jit(solution)/shard_map/all_to_all | solution.py:422
  59.8 1.6 collective-permute-start
  61.4 4.2 %collective-permute-done.2.refs_7_.refs_2_ = bf16[3,224,512]{2,1,0:T(8,128)(2,1)} collective-permute-done((bf16[3,224,512]{2,1,0:T(8,128)(2,1)}, bf16[3,224,512]{2,1,0:T(8,128)(2,1)}, u32[]{:S(2)}, u32[]{:S(2)}) %collective-permute-start.2) | collective-permute-done | bytes 688160 | tf_op jit(solution)/shard_map/ppermute | solution.py:418
  65.6 2.8 %collective-permute-start.3 = (bf16[3,224,512]{2,1,0:T(8,128)(2,1)}, bf16[3,224,512]{2,1,0:T(8,128)(2,1)S(1)}, u32[]{:S(2)}, u32[]{:S(2)}) collective-permute-start(bf16[3,224,512]{2,1,0:T(8,128)(2,1)} %collective-permute-done.2.refs_7_.refs_2_), channel_id=1, source_target_pairs={{0,96},{32,0},{64,32},{96,64},{1,97},{33,1},{65,33},{97,65},{2,98}... | collective-permute-start | bytes 2064392 | tf_op jit(solution)/shard_map/ppermute | solution.py:414
  68.4 0.8 collective-permute-start.5
  69.2 1.2 collective-permute-start.6
  70.4 9.0 %collective-permute-done.refs_4_.refs_3_ = bf16[3,224,512]{2,1,0:T(8,128)(2,1)S(1)} collective-permute-done((bf16[3,224,512]{2,1,0:T(8,128)(2,1)S(1)}, bf16[3,224,512]{2,1,0:T(8,128)(2,1)S(1)}, u32[]{:S(2)}, u32[]{:S(2)}) %collective-permute-start) | collective-permute-done | bytes 688160 | tf_op jit(solution)/shard_map/ppermute | solution.py:414
  79.4 0.3 collective-permute-start.1
  79.7 4.8 %collective-permute-done.3.refs_3_.refs_2_ = bf16[3,224,512]{2,1,0:T(8,128)(2,1)S(1)} collective-permute-done((bf16[3,224,512]{2,1,0:T(8,128)(2,1)}, bf16[3,224,512]{2,1,0:T(8,128)(2,1)S(1)}, u32[]{:S(2)}, u32[]{:S(2)}) %collective-permute-start.3) | collective-permute-done | bytes 688160 | tf_op jit(solution)/shard_map/ppermute | solution.py:414
  84.5 3.6 %collective-permute-start.4 = (bf16[3,224,512]{2,1,0:T(8,128)(2,1)S(1)}, bf16[3,224,512]{2,1,0:T(8,128)(2,1)S(1)}, u32[]{:S(2)}, u32[]{:S(2)}) collective-permute-start(bf16[3,224,512]{2,1,0:T(8,128)(2,1)S(1)} %collective-permute-done.3.refs_3_.refs_2_), channel_id=1, source_target_pairs={{0,96},{32,0},{64,32},{96,64},{1,97},{33,1},{65,33},{97,65},{2,98}... | collective-permute-start | bytes 2064392 | tf_op jit(solution)/shard_map/ppermute | solution.py:414
  88.1 11.1 %collective-permute-done.5.refs_2_.refs_1_ = bf16[3,224,512]{2,1,0:T(8,128)(2,1)S(1)} collective-permute-done((bf16[3,224,512]{2,1,0:T(8,128)(2,1)S(1)}, bf16[3,224,512]{2,1,0:T(8,128)(2,1)S(1)}, u32[]{:S(2)}, u32[]{:S(2)}) %collective-permute-start.5) | collective-permute-done | bytes 688160 | tf_op jit(solution)/shard_map/ppermute | solution.py:414
  99.2 9.0 %collective-permute-done.1.refs_0_.refs_1_ = bf16[3,224,512]{2,1,0:T(8,128)(2,1)S(1)} collective-permute-done((bf16[3,224,512]{2,1,0:T(8,128)(2,1)S(1)}, bf16[3,224,512]{2,1,0:T(8,128)(2,1)S(1)}, u32[]{:S(2)}, u32[]{:S(2)}) %collective-permute-start.1) | collective-permute-done | bytes 688160 | tf_op jit(solution)/shard_map/ppermute | solution.py:414
  108.2 3.6 %collective-permute-done.4.refs_1_.refs_2_ = bf16[3,224,512]{2,1,0:T(8,128)(2,1)S(1)} collective-permute-done((bf16[3,224,512]{2,1,0:T(8,128)(2,1)S(1)}, bf16[3,224,512]{2,1,0:T(8,128)(2,1)S(1)}, u32[]{:S(2)}, u32[]{:S(2)}) %collective-permute-start.4) | collective-permute-done | bytes 688160 | tf_op jit(solution)/shard_map/ppermute | solution.py:414
  111.9 0.8 copy-done.12
  112.7 29.1 %first_part.1 = (f32[3,1792,512]{2,1,0:T(8,128)}, bf16[32,40,512]{2,1,0:T(8,128)(2,1)}, f32[8,1280]{1,0:T(8,128)S(1)}) custom-call(bf16[32,80,512]{2,1,0:T(8,128)(2,1)} %copy-done.5, bf16[3,224,512]{2,1,0:T(8,128)(2,1)} %copy-done.11, bf16[3,224,512]{2,1,0:T(8,128)(2,1)} %copy-done.12, bf16[3,224,512]{2,1,0:T(8,128)(2,1)} %copy-done.9, ...), custom_call_target="tpu_custom_call" | custom-call | tf_op jit(solution)/shard_map/first_part/pallas_call | solution.py:144
  141.9 6.6 %shard_map.104 = (bf16[3,224,512]{2,1,0:T(8,128)(2,1)}, bf16[3,224,512]{2,1,0:T(8,128)(2,1)}, f32[768,512]{1,0:T(8,128)}, f32[8,768]{1,0:T(8,128)S(1)}) custom-call(bf16[32,48,512]{2,1,0:T(8,128)(2,1)S(1)} %all-to-all-done.2.refs_0_, bf16[3,224,512]{2,1,0:T(8,128)(2,1)} %copy-done.11, bf16[3,224,512]{2,1,0:T(8,128)(2,1)} %copy-done.12, ...), custom_call_target="tpu_custom_call" | custom-call | tf_op jit(solution)/shard_map/pallas_call | solution.py:305
  148.5 3.8 %collective-permute-start.11 = (bf16[3,224,512]{2,1,0:T(8,128)(2,1)}, bf16[3,224,512]{2,1,0:T(8,128)(2,1)}, u32[]{:S(2)}, u32[]{:S(2)}) collective-permute-start(bf16[3,224,512]{2,1,0:T(8,128)(2,1)} %get-tuple-element.41), channel_id=1, source_target_pairs={{0,96},{32,0},{64,32},{96,64},{1,97},{33,1},{65,33},{97,65},{2,98}... | collective-permute-start | bytes 2064392 | tf_op jit(solution)/shard_map/ppermute | solution.py:414
  152.2 7.6 %all-to-all-start.1 = ((bf16[32,40,512]{2,1,0:T(8,128)(2,1)}), bf16[32,40,512]{2,1,0:T(8,128)(2,1)S(1)}, u32[]{:S(2)}, u32[]{:S(2)}) async-start(bf16[32,40,512]{2,1,0:T(8,128)(2,1)} %get-tuple-element.24), calls=%async_computation.1 | async-start | bytes 2621440 | tf_op jit(solution)/shard_map/all_to_all | solution.py:422
  159.8 0.3 collective-permute-start.7
  160.2 10.2 %shard_map.105 = (bf16[3,224,512]{2,1,0:T(8,128)(2,1)}, bf16[3,224,512]{2,1,0:T(8,128)(2,1)}, bf16[3,224,512]{2,1,0:T(8,128)(2,1)}, bf16[3,224,512]{2,1,0:T(8,12...) custom-call(bf16[32,48,512]{2,1,0:T(8,128)(2,1)S(1)} %all-to-all-done.2.refs_0_, bf16[3,224,512]{2,1,0:T(8,128)(2,1)} %copy-done.9, ...), custom_call_target="tpu_custom_call" | custom-call | tf_op jit(solution)/shard_map/pallas_call | solution.py:305
  170.4 0.1 collective-permute-start.10
  170.4 2.4 %add_convert_fusion.1 = bf16[3,224,512]{2,1,0:T(8,128)(2,1)} fusion(bf16[3,224,512]{2,1,0:T(8,128)(2,1)} %collective-permute-done.11, bf16[3,224,512]{2,1,0:T(8,128)(2,1)} %get-tuple-element.40), kind=kLoop, calls=%fused_computation.3 | loop fusion | flops 1376256 | bytes 2064384 | tf_op jit(solution)/shard_map/convert_element_type | solution.py:426
  172.8 3.2 %collective-permute-start.12 = (bf16[3,224,512]{2,1,0:T(8,128)(2,1)}, bf16[3,224,512]{2,1,0:T(8,128)(2,1)}, u32[]{:S(2)}, u32[]{:S(2)}) collective-permute-start(bf16[3,224,512]{2,1,0:T(8,128)(2,1)} %add_convert_fusion.1), channel_id=1, source_target_pairs={{0,96},{32,0},{64,32},{96,64},{1,97},{33,1},{65,33},{97,65},{2,98}... | collective-permute-start | bytes 2064392 | tf_op jit(solution)/shard_map/ppermute | solution.py:414
  176.0 2.0 collective-permute-start.9
  178.0 7.0 %shard_map.106 = (bf16[3,224,512]{2,1,0:T(8,128)(2,1)}, bf16[3,224,512]{2,1,0:T(8,128)(2,1)}, bf16[32,32,512]{2,1,0:T(8,128)(2,1)}) custom-call(bf16[32,48,512]{2,1,0:T(8,128)(2,1)S(1)} %all-to-all-done.2.refs_0_, bf16[3,224,512]{2,1,0:T(8,128)(2,1)} %copy-done.6, bf16[3,224,512]{2,1,0:T(8,128)(2,1)} %collective-permute-done.2.refs_7_.refs_2_, ...), custom_call_target="tpu_custom_call" | custom-call | tf_op jit(solution)/shard_map/pallas_call | solution.py:305
  185.1 7.7 %all-to-all-start.3 = ((bf16[32,32,512]{2,1,0:T(8,128)(2,1)}), bf16[32,32,512]{2,1,0:T(8,128)(2,1)}, u32[]{:S(2)}, u32[]{:S(2)}) async-start(bf16[32,32,512]{2,1,0:T(8,128)(2,1)} %get-tuple-element.31), calls=%async_computation.3 | async-start | bytes 2097152 | tf_op jit(solution)/shard_map/all_to_all | solution.py:422
  192.8 2.2 add_convert_fusion.2
  195.0 0.0 collective-permute-start.8
  195.0 2.4 %add_convert_fusion = bf16[3,224,512]{2,1,0:T(8,128)(2,1)} fusion(bf16[3,224,512]{2,1,0:T(8,128)(2,1)} %collective-permute-done.12, bf16[3,224,512]{2,1,0:T(8,128)(2,1)} %collective-permute-done.10, bf16[3,224,512]{2,1,0:T(8,128)(2,1)S(1)} %copy-done.14), kind=kLoop, calls=%fused_computation.2 | loop fusion | flops 2064384 | bytes 2752512 | tf_op jit(solution)/shard_map/convert_element_type | solution.py:426
  197.5 3.2 %collective-permute-start.13 = (bf16[3,224,512]{2,1,0:T(8,128)(2,1)}, bf16[3,224,512]{2,1,0:T(8,128)(2,1)}, u32[]{:S(2)}, u32[]{:S(2)}) collective-permute-start(bf16[3,224,512]{2,1,0:T(8,128)(2,1)} %add_convert_fusion), channel_id=1, source_target_pairs={{0,16},{16,0},{1,17},{17,1},{2,18},{18,2},{3,19},{19,3},{4,20},{20... | collective-permute-start | bytes 2064392 | tf_op jit(solution)/shard_map/ppermute | solution.py:418
  200.7 1.8 combine_first.1.part
  202.5 7.2 %all-to-all-done.3.back = bf16[32,32,512]{2,1,0:T(8,128)(2,1)} async-done(((bf16[32,32,512]{2,1,0:T(8,128)(2,1)}), bf16[32,32,512]{2,1,0:T(8,128)(2,1)}, u32[]{:S(2)}, u32[]{:S(2)}) %all-to-all-start.3) | async-done | bytes 1048608 | tf_op jit(solution)/shard_map/all_to_all | solution.py:422
  209.7 3.6 %combine_last.1 = (bf16[128,4096]{1,0:T(8,128)(2,1)}, f32[8,1024]{1,0:T(8,128)S(1)}) custom-call(f32[8,1024]{1,0:T(8,128)S(1)} %maximum_bitcast_fusion.table, f32[1024,512]{1,0:T(8,128)S(1)} %combine_first.1.part, bf16[32,32,512]{2,1,0:T(8,128)(2,1)} %all-to-all-done.3.back), custom_call_target="tpu_custom_call" | custom-call | tf_op jit(solution)/shard_map/combine_last/pallas_call | solution.py:374
  213.2 0.6 slice_bitcast_fusion
  213.8 0.2 collective-permute-done.8.own1
  214.0 9.0 %collective-permute-done.13.other = bf16[3,224,512]{2,1,0:T(8,128)(2,1)} collective-permute-done((bf16[3,224,512]{2,1,0:T(8,128)(2,1)}, bf16[3,224,512]{2,1,0:T(8,128)(2,1)}, u32[]{:S(2)}, u32[]{:S(2)}) %collective-permute-start.13) | collective-permute-done | bytes 688160 | tf_op jit(solution)/shard_map/ppermute | solution.py:418
  223.1 2.8 %final.1 = (bf16[2,2,224,512]{3,2,1,0:T(8,128)(2,1)}, bf16[2,224,512]{2,1,0:T(8,128)(2,1)}) custom-call(s32[1]{0:T(128)} %bitcast.8.which, bf16[3,224,512]{2,1,0:T(8,128)(2,1)S(1)} %copy-done.4, bf16[3,224,512]{2,1,0:T(8,128)(2,1)} %collective-permute-done.8.own1, bf16[3,224,512]{2,1,0:T(8,128)(2,1)} %collective-permute-done.9.own2, ...), custom_call_target="tpu_custom_call" | custom-call | tf_op jit(solution)/shard_map/final/pallas_call | solution.py:401
  (36 shorter events, 0.1 us)
Async XLA Ops:
  2.2 1.2 copy-start
  3.4 1.2 copy-start.2
  8.9 41.9 %all-to-all-start = ((bf16[32,80,512]{2,1,0:T(8,128)(2,1)}), bf16[32,80,512]{2,1,0:T(8,128)(2,1)S(1)}, u32[]{:S(2)}, u32[]{:S(2)}) async-start(bf16[32,80,512]{2,1,0:T(8,128)(2,1)} %shard_map.102), calls=%async_computation | async-start | bytes 5242880 | tf_op jit(solution)/shard_map/all_to_all | solution.py:422
  17.4 6.0 %copy-start.1 = (bf16[128,4096]{1,0:T(8,128)(2,1)S(1)}, bf16[128,4096]{1,0:T(8,128)(2,1)}, u32[]{:S(2)}) copy-start(bf16[128,4096]{1,0:T(8,128)(2,1)} %tok.3) | copy-start | bytes 3145732
  17.4 6.0 %copy-start.3 = (bf16[128,4096]{1,0:T(8,128)(2,1)S(1)}, bf16[128,4096]{1,0:T(8,128)(2,1)}, u32[]{:S(2)}) copy-start(bf16[128,4096]{1,0:T(8,128)(2,1)} %cot.3) | copy-start | bytes 3145732
  20.1 48.3 %copy-start.6 = (bf16[3,224,512]{2,1,0:T(8,128)(2,1)}, bf16[3,224,512]{2,1,0:T(8,128)(2,1)S(1)}, u32[]{:S(2)}) copy-start(bf16[3,224,512]{2,1,0:T(8,128)(2,1)S(1)} %get-tuple-element.47.refs_6_.refs_1_) | copy-start | bytes 2064388
  20.1 45.5 %collective-permute-start.2 = (bf16[3,224,512]{2,1,0:T(8,128)(2,1)}, bf16[3,224,512]{2,1,0:T(8,128)(2,1)}, u32[]{:S(2)}, u32[]{:S(2)}) collective-permute-start(bf16[3,224,512]{2,1,0:T(8,128)(2,1)} %get-tuple-element.46), channel_id=1, source_target_pairs={{0,16},{16,0},{1,17},{17,1},{2,18},{18,2},{3,19},{19,3},{4,20},{20... | collective-permute-start | bytes 2064392 | tf_op jit(solution)/shard_map/ppermute | solution.py:418
  50.9 1.5 copy-start.5
  52.4 89.5 %all-to-all-start.2 = ((bf16[32,48,512]{2,1,0:T(8,128)(2,1)}), bf16[32,48,512]{2,1,0:T(8,128)(2,1)S(1)}, u32[]{:S(2)}, u32[]{:S(2)}) async-start(bf16[32,48,512]{2,1,0:T(8,128)(2,1)} %shard_map.103), calls=%async_computation.2 | async-start | bytes 3145728 | tf_op jit(solution)/shard_map/all_to_all | solution.py:422
  59.8 19.6 %collective-permute-start = (bf16[3,224,512]{2,1,0:T(8,128)(2,1)S(1)}, bf16[3,224,512]{2,1,0:T(8,128)(2,1)S(1)}, u32[]{:S(2)}, u32[]{:S(2)}) collective-permute-start(bf16[3,224,512]{2,1,0:T(8,128)(2,1)S(1)} %get-tuple-element.47.refs_6_.refs_1_), channel_id=1, source_target_pairs={{0,32},{32,64},{64,96},{96,0},{1,33},{33,65},{65,97},{97,1},{2,34}... | collective-permute-start | bytes 2064392 | tf_op jit(solution)/shard_map/ppermute | solution.py:414
  65.6 18.9 %collective-permute-start.3 = (bf16[3,224,512]{2,1,0:T(8,128)(2,1)}, bf16[3,224,512]{2,1,0:T(8,128)(2,1)S(1)}, u32[]{:S(2)}, u32[]{:S(2)}) collective-permute-start(bf16[3,224,512]{2,1,0:T(8,128)(2,1)} %collective-permute-done.2.refs_7_.refs_2_), channel_id=1, source_target_pairs={{0,96},{32,0},{64,32},{96,64},{1,97},{33,1},{65,33},{97,65},{2,98}... | collective-permute-start | bytes 2064392 | tf_op jit(solution)/shard_map/ppermute | solution.py:414
  68.4 30.8 %collective-permute-start.5 = (bf16[3,224,512]{2,1,0:T(8,128)(2,1)S(1)}, bf16[3,224,512]{2,1,0:T(8,128)(2,1)S(1)}, u32[]{:S(2)}, u32[]{:S(2)}) collective-permute-start(bf16[3,224,512]{2,1,0:T(8,128)(2,1)S(1)} %get-tuple-element.47.refs_6_.refs_1_), channel_id=1, source_target_pairs={{0,96},{32,0},{64,32},{96,64},{1,97},{33,1},{65,33},{97,65},{2,98}... | collective-permute-start | bytes 2064392 | tf_op jit(solution)/shard_map/ppermute | solution.py:414
  69.2 39.0 %collective-permute-start.6 = (bf16[3,224,512]{2,1,0:T(8,128)(2,1)}, bf16[3,224,512]{2,1,0:T(8,128)(2,1)S(1)}, u32[]{:S(2)}, u32[]{:S(2)}) collective-permute-start(bf16[3,224,512]{2,1,0:T(8,128)(2,1)} %collective-permute-done.2.refs_7_.refs_2_), channel_id=1, source_target_pairs={{0,32},{32,64},{64,96},{96,0},{1,33},{33,65},{65,97},{97,1},{2,34}... | collective-permute-start | bytes 2064392 | tf_op jit(solution)/shard_map/ppermute | solution.py:414
  79.4 32.5 %copy-start.7 = (bf16[3,224,512]{2,1,0:T(8,128)(2,1)}, bf16[3,224,512]{2,1,0:T(8,128)(2,1)S(1)}, u32[]{:S(2)}) copy-start(bf16[3,224,512]{2,1,0:T(8,128)(2,1)S(1)} %collective-permute-done.refs_4_.refs_3_) | copy-start | bytes 2064388
  79.4 28.8 %collective-permute-start.1 = (bf16[3,224,512]{2,1,0:T(8,128)(2,1)S(1)}, bf16[3,224,512]{2,1,0:T(8,128)(2,1)S(1)}, u32[]{:S(2)}, u32[]{:S(2)}) collective-permute-start(bf16[3,224,512]{2,1,0:T(8,128)(2,1)S(1)} %collective-permute-done.refs_4_.refs_3_), channel_id=1, source_target_pairs={{0,32},{32,64},{64,96},{96,0},{1,33},{33,65},{65,97},{97,1},{2,34}... | collective-permute-start | bytes 2064392 | tf_op jit(solution)/shard_map/ppermute | solution.py:414
  84.5 27.3 %copy-start.8 = (bf16[3,224,512]{2,1,0:T(8,128)(2,1)}, bf16[3,224,512]{2,1,0:T(8,128)(2,1)S(1)}, u32[]{:S(2)}) copy-start(bf16[3,224,512]{2,1,0:T(8,128)(2,1)S(1)} %collective-permute-done.3.refs_3_.refs_2_) | copy-start | bytes 2064388
  84.5 27.3 %collective-permute-start.4 = (bf16[3,224,512]{2,1,0:T(8,128)(2,1)S(1)}, bf16[3,224,512]{2,1,0:T(8,128)(2,1)S(1)}, u32[]{:S(2)}, u32[]{:S(2)}) collective-permute-start(bf16[3,224,512]{2,1,0:T(8,128)(2,1)S(1)} %collective-permute-done.3.refs_3_.refs_2_), channel_id=1, source_target_pairs={{0,96},{32,0},{64,32},{96,64},{1,97},{33,1},{65,33},{97,65},{2,98}... | collective-permute-start | bytes 2064392 | tf_op jit(solution)/shard_map/ppermute | solution.py:414
  99.2 12.7 %copy-start.9 = (bf16[3,224,512]{2,1,0:T(8,128)(2,1)}, bf16[3,224,512]{2,1,0:T(8,128)(2,1)S(1)}, u32[]{:S(2)}) copy-start(bf16[3,224,512]{2,1,0:T(8,128)(2,1)S(1)} %collective-permute-done.5.refs_2_.refs_1_) | copy-start | bytes 2064388
  108.2 3.7 %copy-start.11 = (bf16[3,224,512]{2,1,0:T(8,128)(2,1)}, bf16[3,224,512]{2,1,0:T(8,128)(2,1)S(1)}, u32[]{:S(2)}) copy-start(bf16[3,224,512]{2,1,0:T(8,128)(2,1)S(1)} %collective-permute-done.1.refs_0_.refs_1_) | copy-start | bytes 2064388
  108.2 3.7 %copy-start.10 = (bf16[3,224,512]{2,1,0:T(8,128)(2,1)}, bf16[3,224,512]{2,1,0:T(8,128)(2,1)S(1)}, u32[]{:S(2)}) copy-start(bf16[3,224,512]{2,1,0:T(8,128)(2,1)S(1)} %collective-permute-done.6.refs_5_.refs_4_) | copy-start | bytes 2064388
  111.9 0.8 copy-start.12
  148.5 22.0 %collective-permute-start.11 = (bf16[3,224,512]{2,1,0:T(8,128)(2,1)}, bf16[3,224,512]{2,1,0:T(8,128)(2,1)}, u32[]{:S(2)}, u32[]{:S(2)}) collective-permute-start(bf16[3,224,512]{2,1,0:T(8,128)(2,1)} %get-tuple-element.41), channel_id=1, source_target_pairs={{0,96},{32,0},{64,32},{96,64},{1,97},{33,1},{65,33},{97,65},{2,98}... | collective-permute-start | bytes 2064392 | tf_op jit(solution)/shard_map/ppermute | solution.py:414
  152.2 32.8 %all-to-all-start.1 = ((bf16[32,40,512]{2,1,0:T(8,128)(2,1)}), bf16[32,40,512]{2,1,0:T(8,128)(2,1)S(1)}, u32[]{:S(2)}, u32[]{:S(2)}) async-start(bf16[32,40,512]{2,1,0:T(8,128)(2,1)} %get-tuple-element.24), calls=%async_computation.1 | async-start | bytes 2621440 | tf_op jit(solution)/shard_map/all_to_all | solution.py:422
  159.8 32.9 %collective-permute-start.7 = (bf16[3,224,512]{2,1,0:T(8,128)(2,1)}, bf16[3,224,512]{2,1,0:T(8,128)(2,1)}, u32[]{:S(2)}, u32[]{:S(2)}) collective-permute-start(bf16[3,224,512]{2,1,0:T(8,128)(2,1)} %get-tuple-element.36), channel_id=1, source_target_pairs={{0,32},{32,64},{64,96},{96,0},{1,33},{33,65},{65,97},{97,1},{2,34}... | collective-permute-start | bytes 2064392 | tf_op jit(solution)/shard_map/ppermute | solution.py:414
  170.4 24.6 %collective-permute-start.10 = (bf16[3,224,512]{2,1,0:T(8,128)(2,1)}, bf16[3,224,512]{2,1,0:T(8,128)(2,1)}, u32[]{:S(2)}, u32[]{:S(2)}) collective-permute-start(bf16[3,224,512]{2,1,0:T(8,128)(2,1)} %get-tuple-element.39), channel_id=1, source_target_pairs={{0,32},{32,64},{64,96},{96,0},{1,33},{33,65},{65,97},{97,1},{2,34}... | collective-permute-start | bytes 2064392 | tf_op jit(solution)/shard_map/ppermute | solution.py:414
  172.8 22.2 %collective-permute-start.12 = (bf16[3,224,512]{2,1,0:T(8,128)(2,1)}, bf16[3,224,512]{2,1,0:T(8,128)(2,1)}, u32[]{:S(2)}, u32[]{:S(2)}) collective-permute-start(bf16[3,224,512]{2,1,0:T(8,128)(2,1)} %add_convert_fusion.1), channel_id=1, source_target_pairs={{0,96},{32,0},{64,32},{96,64},{1,97},{33,1},{65,33},{97,65},{2,98}... | collective-permute-start | bytes 2064392 | tf_op jit(solution)/shard_map/ppermute | solution.py:414
  176.0 37.8 %collective-permute-start.9 = (bf16[3,224,512]{2,1,0:T(8,128)(2,1)}, bf16[3,224,512]{2,1,0:T(8,128)(2,1)}, u32[]{:S(2)}, u32[]{:S(2)}) collective-permute-start(bf16[3,224,512]{2,1,0:T(8,128)(2,1)} %get-tuple-element.37), channel_id=1, source_target_pairs={{0,96},{32,0},{64,32},{96,64},{1,97},{33,1},{65,33},{97,65},{2,98}... | collective-permute-start | bytes 2064392 | tf_op jit(solution)/shard_map/ppermute | solution.py:414
  185.0 7.7 %copy-start.13 = (bf16[3,224,512]{2,1,0:T(8,128)(2,1)S(1)}, bf16[3,224,512]{2,1,0:T(8,128)(2,1)}, u32[]{:S(2)}) copy-start(bf16[3,224,512]{2,1,0:T(8,128)(2,1)} %get-tuple-element.35) | copy-start | bytes 2064388
  185.1 24.6 %all-to-all-start.3 = ((bf16[32,32,512]{2,1,0:T(8,128)(2,1)}), bf16[32,32,512]{2,1,0:T(8,128)(2,1)}, u32[]{:S(2)}, u32[]{:S(2)}) async-start(bf16[32,32,512]{2,1,0:T(8,128)(2,1)} %get-tuple-element.31), calls=%async_computation.3 | async-start | bytes 2097152 | tf_op jit(solution)/shard_map/all_to_all | solution.py:422
  192.8 2.3 copy-start.14
  195.0 19.1 %collective-permute-start.8 = (bf16[3,224,512]{2,1,0:T(8,128)(2,1)}, bf16[3,224,512]{2,1,0:T(8,128)(2,1)}, u32[]{:S(2)}, u32[]{:S(2)}) collective-permute-start(bf16[3,224,512]{2,1,0:T(8,128)(2,1)} %add_convert_fusion.2), channel_id=1, source_target_pairs={{0,32},{32,64},{64,96},{96,0},{1,33},{33,65},{65,97},{97,1},{2,34}... | collective-permute-start | bytes 2064392 | tf_op jit(solution)/shard_map/ppermute | solution.py:414
  197.5 25.6 %collective-permute-start.13 = (bf16[3,224,512]{2,1,0:T(8,128)(2,1)}, bf16[3,224,512]{2,1,0:T(8,128)(2,1)}, u32[]{:S(2)}, u32[]{:S(2)}) collective-permute-start(bf16[3,224,512]{2,1,0:T(8,128)(2,1)} %add_convert_fusion), channel_id=1, source_target_pairs={{0,16},{16,0},{1,17},{17,1},{2,18},{18,2},{3,19},{19,3},{4,20},{20... | collective-permute-start | bytes 2064392 | tf_op jit(solution)/shard_map/ppermute | solution.py:418
  202.5 20.6 %copy-start.4 = (bf16[3,224,512]{2,1,0:T(8,128)(2,1)S(1)}, bf16[3,224,512]{2,1,0:T(8,128)(2,1)}, u32[]{:S(2)}) copy-start(bf16[3,224,512]{2,1,0:T(8,128)(2,1)} %get-tuple-element.34.own0) | copy-start | bytes 2064388
where the time goes:
time: 227 us; the launch traced here: 226 us
  waiting for transfers between devices  82.4 us (36%)
  Pallas kernels  68.6 us (30%)
  starting transfers between devices  57.3 us (25%)
  other arithmetic  11.2 us (5%)
  local copies, waits for them, and re-layouts  5.46 us (2%)
    ppermute x12, waiting for transfers between devices, ring(): return lax.ppermute(a, 'x', [(i, (i + step) % 4) for i in range(4)])  37.8 us
    all_to_all x4, waiting for transfers between devices, exchange(): return lax.all_to_all(a, PLANE, 0, 0, tiled=True)  31.4 us
    all_to_all x4, starting transfers between devices, exchange(): return lax.all_to_all(a, PLANE, 0, 0, tiled=True)  31.2 us
    pallas_call x1, Pallas kernels, first_part(): pl.pallas_call(first_kernel, in_specs=[HBM] * 9, out_specs=[HBM, WHOLE, W...  29.1 us
    pallas_call x3, Pallas kernels, second_part(): pl.pallas_call(functools.partial(second_kernel, pairs=n // 2, first=first...  23.8 us
    ppermute x12, starting transfers between devices, ring(): return lax.ppermute(a, 'x', [(i, (i + step) % 4) for i in range(4)])  19.6 us
    ppermute x2, waiting for transfers between devices, swap(): return lax.ppermute(a, 'yh', [(0, 1), (1, 0)])  13.3 us
    pallas_call x2, Pallas kernels, dispatch(): pl.pallas_call(functools.partial(dispatch_kernel, part=part), grid=(PEERS...  7.53 us
  transfers between devices with their start and end apart: 18, of which 10 were waited for; matrix products, arithmetic and copies ran while one was open for 5% of the time, Pallas kernels for 24%

commit v1 on v0

--- a/solution.py
+++ b/solution.py
@@ -11,7 +11,7 @@
 H = 8
 DS = 512
 PEERS = 32
-SLOTS = (40, 24)
+SLOTS = (32, 32)
 GROUP = 8
 SUBS = 1024
 EXTRA = 8
@@ -92,168 +92,12 @@
 
 HBM = pl.BlockSpec(memory_space=pltpu.HBM)
 WHOLE = pl.BlockSpec(memory_space=pltpu.VMEM)
-
-
-def first_kernel(z_in, *refs):
-    weights, (dw, dxo, router, z, wbuf, acc, stage, zsem, wsem, osem) = refs[:8], refs[8:]
-    rows_in = pltpu.make_async_copy(z_in, z, zsem)
-    rows_in.start()
-
-    def fetch(k, slot):
-        here = pl.ds(pl.multiple_of(slot * SH, SH), SH)
-        return pltpu.make_async_copy(weights[k], wbuf.at[:, here, :], wsem.at[slot])
-
-    def flush(j, slot):
-        here = pl.ds(pl.multiple_of(j * 2 * SH, 2 * SH), 2 * SH)
-        return pltpu.make_async_copy(stage.at[slot], dw.at[:, here, :], osem.at[slot])
-
-    for k in range(8):
-        fetch(k, k).start()
-    acc[...] = jnp.zeros_like(acc)
-    router[...] = jnp.zeros_like(router)
-    rows_in.wait()
-
-    def block(j, carry):
-        fetch(0, 2 * j).wait()
-        fetch(1, 2 * j + 1).wait()
-        here = pl.ds(pl.multiple_of(j * 2 * SH, 2 * SH), 2 * SH)
-        parts, dx, r = expert_block(
-            z, SLOTS[0], wbuf[0, here, :], wbuf[1, here, :], wbuf[2, here, :]
-        )
-        slot = j % 2
-
-        @pl.when(j >= 2)
-        def _():
-            flush(j - 2, slot).wait()
-
-        for k in range(3):
-            stage[slot, k] = parts[k]
-        acc[...] += dx
-        router[...] += r
-        flush(j, slot).start()
-        return carry
-
-    lax.fori_loop(0, 4, block, 0)
-    dxo[...] = acc[...].astype(BF).reshape(PEERS, SLOTS[0], DS)
-    flush(2, 0).wait()
-    flush(3, 1).wait()
-
-
-def first_part(z, weights):
-    rows = PEERS * SLOTS[0]
-    return pl.pallas_call(
-        first_kernel,
-        in_specs=[HBM] * 9,
-        out_specs=[HBM, WHOLE, WHOLE],
-        out_shape=[
-            pltpu.HBM((3, 8 * SH, DS), F32),
-            pltpu.HBM((PEERS, SLOTS[0], DS), BF),
-            jax.ShapeDtypeStruct((8, rows), F32),
-        ],
-        scratch_shapes=[
-            pltpu.VMEM((PEERS, 2 * SLOTS[0], DS), BF),
-            pltpu.VMEM((3, 8 * SH, DS), BF),
-            pltpu.VMEM((rows, DS), F32),
-            pltpu.VMEM((2, 3, 2 * SH, DS), F32),
-            pltpu.SemaphoreType.DMA,
-            pltpu.SemaphoreType.DMA((8,)),
-            pltpu.SemaphoreType.DMA((2,)),
-        ],
-        compiler_params=params(40),
-        name="first_part",
-    )(*[in_hbm(a) for a in (z, *weights)])
-
-
-def second_kernel(*refs, pairs, first, begin, end):
-    n = 2 * pairs
-    slots = SLOTS[1]
-    z = refs[0]
-    weights = refs[1 : 1 + n]
-    before = refs[1 + n]
-    pos = 2 + n
-    if not begin:
-        acc_in, router_in = refs[pos : pos + 2]
-        pos += 2
-    if end:
-        router_first = refs[pos]
-        pos += 1
-    outs = refs[pos : pos + n]
-    pos += n
-    if end:
-        back, router, acc, wbuf, stage, obuf, asem, wsem, bsem, ssem = refs[pos:]
-    else:
-        acc_out, router, acc, wbuf, stage, obuf, asem, wsem, bsem, ssem = refs[pos:]
-
-    def fetch(k, slot):
-        half = k % 2
-        return pltpu.make_async_copy(
-            weights[k], wbuf.at[slot, :, half * SH : (half + 1) * SH, :], wsem.at[slot, half]
-        )
-
-    def load(p):
-        here = pl.ds(pl.multiple_of((first + p) * 2 * SH, 2 * SH), 2 * SH)
-        return pltpu.make_async_copy(before.at[:, here, :], stage.at[p], bsem.at[p])
-
-    def store(p, half):
-        return pltpu.make_async_copy(
-            obuf.at[p, :, half * SH : (half + 1) * SH, :], outs[2 * p + half], ssem.at[p, half]
-        )
-
-    for k in range(n):
-        fetch(k, k // 2).start()
-    for p in range(pairs):
-        load(p).start()
-    if begin:
-        router[...] = jnp.zeros_like(router)
-        acc[...] = jnp.zeros_like(acc)
-    else:
-        acc_load = pltpu.make_async_copy(acc_in, acc, asem)
-        acc_load.start()
-        router[...] = router_in[...]
-
-    def block(p, carry):
-        fetch(0, p).wait()
-        fetch(1, p).wait()
-        parts, dx, r = expert_block(z, slots, wbuf[p, 0], wbuf[p, 1], wbuf[p, 2])
-        load(p).wait()
-        for k in range(3):
-            obuf[p, k] = (parts[k] + stage[p, k]).astype(BF)
-        for q in range(pairs):
-
-            @pl.when(p == q)
-            def _():
-                for half in range(2):
-                    store(q, half).start()
-
-        if not begin:
-
-            @pl.when(p == 0)
-            def _():
-                acc_load.wait()
-
-        acc[...] += dx
-        router[...] += r
-        return carry
-
-    if pairs == 1:
-        block(0, 0)
-    else:
-        lax.fori_loop(0, pairs, block, 0)
-
-    def drain():
-        for p in range(pairs):
-            for half in range(2):
-                store(p, half).wait()
-
-    if not end:
-        acc_save = pltpu.make_async_copy(acc, acc_out, asem)
-        acc_save.start()
-        drain()
-        acc_save.wait()
-        return
-    back[:, 0:slots, :] = acc[...].astype(BF).reshape(PEERS, slots, DS)
+UNITS = 2 * SH
+
+
+def router_rows(back, slots, router_first, router):
     table = jnp.zeros((PEERS, 128), F32)
-    for part, value in ((0, router_first[...]), (1, router[...])):
+    for part, value in ((0, router_first), (1, router)):
         count = SLOTS[part]
         total = PEERS * count
         source = lax.broadcasted_iota(jnp.int32, (PEERS, total), 0) * count
@@ -268,49 +112,147 @@
         table.astype(BF)[:, None, :], (PEERS, EXTRA, 128)
     )
     back[:, slots : slots + EXTRA, 128:DS] = jnp.zeros((PEERS, EXTRA, DS - 128), BF)
-    drain()
-
-
-def second_part(z, weights, before, first, carry=None, router_first=None):
-    n = len(weights)
-    end = router_first is not None
-    rows = PEERS * SLOTS[1]
-    args = [z, *[in_hbm(a) for a in (*weights, before)]]
-    in_specs = [WHOLE] + [HBM] * (n + 1)
-    if carry is not None:
+
+
+def expert_kernel(*refs, part, end):
+    slots = SLOTS[part]
+    refs = list(refs)
+    take = lambda n: [refs.pop(0) for _ in range(n)]
+    (z,) = take(1)
+    weights = take(4)
+    before = take(1)[0] if part else None
+    acc_in, router_in = take(2) if end else (None, None)
+    router_first = take(1)[0] if part and end else None
+    outs = take(4 if part else 1)
+    (dx_out,) = take(1)
+    router_out = None if part and end else take(1)[0]
+    acc, wbuf, stage, obuf, asem, wsem, bsem, ssem = refs
+
+    def units(p):
+        return pl.ds(pl.multiple_of(p * UNITS, UNITS), UNITS)
+
+    def fetch(k, slot):
+        half = k % 2
+        return pltpu.make_async_copy(
+            weights[k], wbuf.at[slot, :, half * SH : (half + 1) * SH, :], wsem.at[slot, half]
+        )
+
+    def load(p):
+        return pltpu.make_async_copy(before.at[:, units(p), :], stage.at[p], bsem.at[p])
+
+    def store_wide(p):
+        return pltpu.make_async_copy(stage.at[p], outs[0].at[:, units(p), :], bsem.at[p])
+
+    def store(p, half):
+        return pltpu.make_async_copy(
+            obuf.at[p, :, half * SH : (half + 1) * SH, :], outs[2 * p + half], ssem.at[p, half]
+        )
+
+    for k in range(4):
+        fetch(k, k // 2).start()
+    if part:
+        for p in range(2):
+            load(p).start()
+    if end:
+        acc_load = pltpu.make_async_copy(acc_in, acc, asem)
+        acc_load.start()
+    else:
+        acc[...] = jnp.zeros_like(acc)
+    router = jnp.zeros((8, PEERS * slots), F32) if not end else router_in[...]
+
+    def block(p, router):
+        fetch(0, p).wait()
+        fetch(1, p).wait()
+        parts, dx, r = expert_block(z, slots, wbuf[p, 0], wbuf[p, 1], wbuf[p, 2])
+        if part:
+            load(p).wait()
+            for k in range(3):
+                obuf[p, k] = (parts[k] + stage[p, k]).astype(BF)
+            for q in range(2):
+
+                @pl.when(p == q)
+                def _():
+                    for half in range(2):
+                        store(q, half).start()
+        else:
+            for k in range(3):
+                stage[p, k] = parts[k]
+            store_wide(p).start()
+        if end:
+
+            @pl.when(p == 0)
+            def _():
+                acc_load.wait()
+
+        acc[...] += dx
+        return router + r
+
+    router = lax.fori_loop(0, 2, block, router)
+    if end:
+        dx_out[:, 0:slots, :] = acc[...].astype(BF).reshape(PEERS, slots, DS)
+    else:
+        acc_save = pltpu.make_async_copy(acc, dx_out, asem)
+        acc_save.start()
+    if router_out is None:
+        router_rows(dx_out, slots, router_first[...], router)
+    else:
+        router_out[...] = router
+    for p in range(2):
+        if part:
+            store(p, 0).wait()
+            store(p, 1).wait()
+        else:
+            store_wide(p).wait()
+    if not end:
+        acc_save.wait()
+
+
+def expert_part(part, z, weights, before=None, carry=None, router_first=None):
+    end = carry is not None
+    slots = SLOTS[part]
+    rows = PEERS * slots
+    args = [z, *[in_hbm(w) for w in weights]]
+    in_specs = [WHOLE] + [HBM] * 4
+    if part:
+        args += [in_hbm(before)]
+        in_specs += [HBM]
+    if end:
         args += [in_hbm(carry[0]), carry[1]]
         in_specs += [HBM, WHOLE]
-    if end:
+    if part and end:
         args += [router_first]
         in_specs += [WHOLE]
-    out_shape = [pltpu.HBM((3, SH, DS), BF)] * n
-    scratch = []
+    if part:
+        out_shape = [pltpu.HBM((3, SH, DS), BF)] * 4
+        out_specs = [HBM] * 4
+    else:
+        out_shape = [pltpu.HBM((3, 4 * SH, DS), F32)]
+        out_specs = [HBM]
     if end:
-        out_shape += [pltpu.HBM((PEERS, SLOTS[1] + EXTRA, DS), BF)]
-        scratch += [pltpu.VMEM((8, rows), F32)]
-        out_specs = [HBM] * n + [WHOLE]
+        out_shape += [pltpu.HBM((PEERS, slots + part * EXTRA, DS), BF)]
+        out_specs += [WHOLE]
     else:
-        out_shape += [pltpu.HBM((rows, DS), F32), jax.ShapeDtypeStruct((8, rows), F32)]
-        out_specs = [HBM] * (n + 1) + [WHOLE]
-    scratch += [pltpu.VMEM((rows, DS), F32)]
-    scratch += [
-        pltpu.VMEM((n // 2, 3, 2 * SH, DS), BF),
-        pltpu.VMEM((n // 2, 3, 2 * SH, DS), F32),
-        pltpu.VMEM((n // 2, 3, 2 * SH, DS), BF),
-        pltpu.SemaphoreType.DMA,
-        pltpu.SemaphoreType.DMA((n // 2, 2)),
-        pltpu.SemaphoreType.DMA((n // 2,)),
-        pltpu.SemaphoreType.DMA((n // 2, 2)),
-    ]
+        out_shape += [pltpu.HBM((rows, DS), F32)]
+        out_specs += [HBM]
+    if not (part and end):
+        out_shape += [jax.ShapeDtypeStruct((8, rows), F32)]
+        out_specs += [WHOLE]
     return pl.pallas_call(
-        functools.partial(
-            second_kernel, pairs=n // 2, first=first, begin=carry is None, end=end
-        ),
+        functools.partial(expert_kernel, part=part, end=end),
         in_specs=in_specs,
         out_specs=out_specs,
         out_shape=out_shape,
-        scratch_shapes=scratch,
-        compiler_params=params(30),
+        scratch_shapes=[
+            pltpu.VMEM((rows, DS), F32),
+            pltpu.VMEM((2, 3, UNITS, DS), BF),
+            pltpu.VMEM((2, 3, UNITS, DS), F32),
+            pltpu.VMEM((2, 3, UNITS, DS) if part else (8, 128), BF),
+            pltpu.SemaphoreType.DMA,
+            pltpu.SemaphoreType.DMA((2, 2)),
+            pltpu.SemaphoreType.DMA((2,)),
+            pltpu.SemaphoreType.DMA((2, 2)),
+        ],
+        compiler_params=params(36),
     )(*args)
 
 
@@ -436,8 +378,8 @@
     w_o_p = ring(w_o, -1)
     w_p_m = ring(w_p, 1)
     w_p_p = ring(w_p, -1)
-    w_o_2 = ring(w_o_m, 1)
-    w_p_2 = ring(w_p_p, -1)
+    w_o_2 = ring(w_o_p, -1)
+    w_p_2 = ring(w_p_m, 1)
 
     dest = expert_ids % 2 * (PEERS // 2) + expert_ids // 2
     code = jnp.where(
@@ -452,20 +394,20 @@
     z1 = exchange(dispatch(table, tokens, cotangent, 0))
     z2 = exchange(dispatch(table, tokens, cotangent, 1))
 
-    weights = [w_o_2, w_p_2, w_o_p, w_p_p, w_o_m, w_p_m, w_o, w_p]
-    dw_first, back1, router1 = first_part(z1, weights)
+    w_p = [w_p_2, w_p_p, w_p_m, w_p]
+    w_o = [w_o_2, w_o_p, w_o_m, w_o]
+    dw_p, *carry = expert_part(0, z1, w_p)
+    dw_o, back1, router1 = expert_part(0, z1, w_o, carry=carry)
     back1 = exchange(back1)
-    o_2, p_2, *carry = second_part(z2, weights[0:2], dw_first, 0)
-    o_2 = ring(o_2, 1)
-    p_2 = ring(p_2, -1)
-    o_p, p_p, o_m, p_m, *carry = second_part(z2, weights[2:6], dw_first, 1, carry)
-    p_p = ring(p_p, 1)
-    p_m = ring(add(p_m, p_2), -1)
-    o_p = ring(add(o_p, o_2), 1)
-    o_m = ring(o_m, -1)
-    o_0, p_0, back2 = second_part(z2, weights[6:8], dw_first, 3, carry, router1)
+    p_2, p_p, p_m, p_0, *carry = expert_part(1, z2, w_p, dw_p)
+    p_2 = ring(p_2, 1)
+    p_m = ring(p_m, -1)
+    o_2, o_p, o_m, o_0, back2 = expert_part(1, z2, w_o, dw_o, carry, router1)
     back2 = exchange(back2)
-
+    o_2 = ring(o_2, -1)
+    p_p = ring(add(p_p, p_2), 1)
+    o_p = ring(o_p, 1)
+    o_m = ring(add(o_m, o_2), -1)
     other = swap(add(p_0, p_p, p_m))
     grad_in, grad_out = final(yh.astype(jnp.int32).reshape(1), (o_0, o_p, o_m), other)
 

time: 227 us -> 223 us (0.982)
  waiting for transfers between devices: 82.4 us -> 69.8 us
  starting transfers between devices: 57.3 us -> 67.4 us
    all_to_all x4, waiting for transfers between devices: 31.4 us -> 18.1 us  [exchange(): return lax.all_to_all(a, PLANE, 0, 0, tiled=True)]
    all_to_all x4, starting transfers between devices: 31.2 us -> 42.9 us  [exchange(): return lax.all_to_all(a, PLANE, 0, 0, tiled=True)]
    ppermute x12, waiting for transfers between devices: 37.8 us -> 45.3 us  [ring(): return lax.ppermute(a, 'x', [(i, (i + step) % 4) for i in range(4)])]
    ppermute x2, waiting for transfers between devices: 13.3 us -> 6.4 us  [swap(): return lax.ppermute(a, 'yh', [(0, 1), (1, 0)])]
    unnamed x30 -> x28, local copies, waits for them, and re-layouts: 4.86 us -> 3.34 us
  transfers between devices with their start and end apart: 18 -> 18, of which waited for: 10 -> 8; matrix products, arithmetic and copies ran while one was open for 5% -> 5% of each run, Pallas kernels for 24% -> 28%
where the time goes in v1:
time: 223 us; the launch traced here: 222 us
  waiting for transfers between devices  69.8 us (31%)
  Pallas kernels  68.7 us (31%)
  starting transfers between devices  67.4 us (30%)
  other arithmetic  11 us (5%)
  local copies, waits for them, and re-layouts  3.96 us (2%)
    pallas_call x4, Pallas kernels, expert_part(): pl.pallas_call(functools.partial(expert_kernel, part=part, end=end), in_s...  53 us
    ppermute x12, waiting for transfers between devices, ring(): return lax.ppermute(a, 'x', [(i, (i + step) % 4) for i in range(4)])  45.3 us
    all_to_all x4, starting transfers between devices, exchange(): return lax.all_to_all(a, PLANE, 0, 0, tiled=True)  42.9 us
    all_to_all x4, waiting for transfers between devices, exchange(): return lax.all_to_all(a, PLANE, 0, 0, tiled=True)  18.1 us
    ppermute x12, starting transfers between devices, ring(): return lax.ppermute(a, 'x', [(i, (i + step) % 4) for i in range(4)])  17.9 us
    pallas_call x2, Pallas kernels, dispatch(): pl.pallas_call(functools.partial(dispatch_kernel, part=part), grid=(PEERS...  7.68 us
    convert_element_type x3, other arithmetic, add(): return sum((a.astype(F32) for a in arrays)).astype(BF)  7.03 us
    ppermute x2, starting transfers between devices, swap(): return lax.ppermute(a, 'yh', [(0, 1), (1, 0)])  6.61 us
  transfers between devices with their start and end apart: 18, of which 8 were waited for; matrix products, arithmetic and copies ran while one was open for 5% of the time, Pallas kernels for 28%

profile of v1, /device:TPU:0, one launch (start us, length us, event | category | flops | bytes accessed | tf_op | source)
XLA Modules:
  0.0 221.7 jit_solution(6629648769512739612)
XLA Ops:
  0.6 0.8 fusion.1
  1.5 0.7 convert_element_type.43
  2.2 0.0 copy-start.2
  2.2 1.2 copy-done.2
  3.4 1.2 copy-done.4
  4.6 3.8 %shard_map.102 = bf16[32,64,512]{2,1,0:T(8,128)(2,1)} custom-call(f32[8,1024]{1,0:T(8,128)S(1)} %maximum_bitcast_fusion.table, bf16[128,4096]{1,0:T(8,128)(2,1)S(1)} %copy-done.2, bf16[128,4096]{1,0:T(8,128)(2,1)S(1)} %copy-done.4), custom_call_target="tpu_custom_call" | custom-call | tf_op jit(solution)/shard_map/pallas_call | solution.py:59
  8.4 8.6 %all-to-all-start = ((bf16[32,64,512]{2,1,0:T(8,128)(2,1)}), bf16[32,64,512]{2,1,0:T(8,128)(2,1)S(1)}, u32[]{:S(2)}, u32[]{:S(2)}) async-start(bf16[32,64,512]{2,1,0:T(8,128)(2,1)} %shard_map.102), calls=%async_computation | async-start | bytes 4194304 | tf_op jit(solution)/shard_map/all_to_all | solution.py:364
  17.1 0.0 copy-start.3
  17.1 0.0 copy-start.5
  17.1 2.4 %select_bitcast_fusion = (bf16[3,224,512]{2,1,0:T(8,128)(2,1)}, bf16[3,224,512]{2,1,0:T(8,128)(2,1)S(1)}) fusion(pred[]{:T(512)S(6)} %eq.6, bf16[2,1,224,512]{3,2,1,0:T(8,128)(2,1)S(1)} %bitcast.14, bf16[2,2,224,512]{3,2,1,0:T(8,128)(2,1)} %param.12), kind=kLoop, calls=%fused_computation.7 | loop fusion | flops 1720320 | bytes 2752513 | tf_op jit(solution)/shard_map/jit(_where)/select_n | solution.py:374
  19.5 3.3 %collective-permute-start.3 = (bf16[3,224,512]{2,1,0:T(8,128)(2,1)}, bf16[3,224,512]{2,1,0:T(8,128)(2,1)}, u32[]{:S(2)}, u32[]{:S(2)}) collective-permute-start(bf16[3,224,512]{2,1,0:T(8,128)(2,1)} %get-tuple-element.48), channel_id=1, source_target_pairs={{0,16},{16,0},{1,17},{17,1},{2,18},{18,2},{3,19},{19,3},{4,20},{20... | collective-permute-start | bytes 2064392 | tf_op jit(solution)/shard_map/ppermute | solution.py:360
  22.8 3.9 %shard_map.105 = bf16[32,64,512]{2,1,0:T(8,128)(2,1)} custom-call(f32[8,1024]{1,0:T(8,128)S(1)} %maximum_bitcast_fusion.table, bf16[128,4096]{1,0:T(8,128)(2,1)S(1)} %copy-done.3, bf16[128,4096]{1,0:T(8,128)(2,1)S(1)} %copy-done.5), custom_call_target="tpu_custom_call" | custom-call | tf_op jit(solution)/shard_map/pallas_call | solution.py:59
  26.7 18.1 %all-to-all-done.refs_0_ = bf16[32,64,512]{2,1,0:T(8,128)(2,1)S(1)} async-done(((bf16[32,64,512]{2,1,0:T(8,128)(2,1)}), bf16[32,64,512]{2,1,0:T(8,128)(2,1)S(1)}, u32[]{:S(2)}, u32[]{:S(2)}) %all-to-all-start) | async-done | bytes 2097184 | tf_op jit(solution)/shard_map/all_to_all | solution.py:364
  44.8 19.7 %all-to-all-start.2 = ((bf16[32,64,512]{2,1,0:T(8,128)(2,1)}), bf16[32,64,512]{2,1,0:T(8,128)(2,1)}, u32[]{:S(2)}, u32[]{:S(2)}) async-start(bf16[32,64,512]{2,1,0:T(8,128)(2,1)} %shard_map.105), calls=%async_computation.2 | async-start | bytes 4194304 | tf_op jit(solution)/shard_map/all_to_all | solution.py:364
  64.5 1.5 collective-permute-start.4
  66.1 1.8 collective-permute-start
  67.8 1.5 collective-permute-start.6
  69.4 14.2 %collective-permute-done.4.refs_3_ = bf16[3,224,512]{2,1,0:T(8,128)(2,1)S(1)} collective-permute-done((bf16[3,224,512]{2,1,0:T(8,128)(2,1)}, bf16[3,224,512]{2,1,0:T(8,128)(2,1)S(1)}, u32[]{:S(2)}, u32[]{:S(2)}) %collective-permute-start.4) | collective-permute-done | bytes 688160 | tf_op jit(solution)/shard_map/ppermute | solution.py:356
  83.5 0.3 collective-permute-start.5
  83.8 1.5 collective-permute-start.2
  85.3 2.1 collective-permute-start.1
  87.4 11.7 %collective-permute-done.6.refs_2_ = bf16[3,224,512]{2,1,0:T(8,128)(2,1)S(1)} collective-permute-done((bf16[3,224,512]{2,1,0:T(8,128)(2,1)}, bf16[3,224,512]{2,1,0:T(8,128)(2,1)S(1)}, u32[]{:S(2)}, u32[]{:S(2)}) %collective-permute-start.6) | collective-permute-done | bytes 688160 | tf_op jit(solution)/shard_map/ppermute | solution.py:356
  99.1 3.9 %collective-permute-done.5.refs_1_ = bf16[3,224,512]{2,1,0:T(8,128)(2,1)S(1)} collective-permute-done((bf16[3,224,512]{2,1,0:T(8,128)(2,1)S(1)}, bf16[3,224,512]{2,1,0:T(8,128)(2,1)S(1)}, u32[]{:S(2)}, u32[]{:S(2)}) %collective-permute-start.5) | collective-permute-done | bytes 688160 | tf_op jit(solution)/shard_map/ppermute | solution.py:356
  103.1 0.8 copy-done.10
  103.9 11.7 %shard_map.103 = (f32[3,896,512]{2,1,0:T(8,128)}, f32[1024,512]{1,0:T(8,128)}, f32[8,1024]{1,0:T(8,128)S(1)}) custom-call(bf16[32,64,512]{2,1,0:T(8,128)(2,1)S(1)} %all-to-all-done.refs_0_, bf16[3,224,512]{2,1,0:T(8,128)(2,1)} %copy-done.10, bf16[3,224,512]{2,1,0:T(8,128)(2,1)} %copy-done.9, bf16[3,224,512]{2,1,0:T(8,128)(2,1)} %copy-done.8, ...), custom_call_target="tpu_custom_call" | custom-call | tf_op jit(solution)/shard_map/pallas_call | solution.py:240
  115.7 14.3 %shard_map.106 = (bf16[3,224,512]{2,1,0:T(8,128)(2,1)}, bf16[3,224,512]{2,1,0:T(8,128)(2,1)}, bf16[3,224,512]{2,1,0:T(8,128)(2,1)}, bf16[3,224,512]{2,1,0:T(8,12...) custom-call(bf16[32,64,512]{2,1,0:T(8,128)(2,1)} %all-to-all-done.2.refs_0_, bf16[3,224,512]{2,1,0:T(8,128)(2,1)} %copy-done.10, ...), custom_call_target="tpu_custom_call" | custom-call | tf_op jit(solution)/shard_map/pallas_call | solution.py:240
  130.0 0.1 collective-permute-start.10
  130.1 12.3 %shard_map.104 = (f32[3,896,512]{2,1,0:T(8,128)}, bf16[32,32,512]{2,1,0:T(8,128)(2,1)}, f32[8,1024]{1,0:T(8,128)S(1)}) custom-call(bf16[32,64,512]{2,1,0:T(8,128)(2,1)S(1)} %all-to-all-done.refs_0_, bf16[3,224,512]{2,1,0:T(8,128)(2,1)} %collective-permute-done.1.refs_1_, bf16[3,224,512]{2,1,0:T(8,128)(2,1)} %collective-permute-done.refs_2_, ...), custom_call_target="tpu_custom_call" | custom-call | tf_op jit(solution)/shard_map/pallas_call | solution.py:240
  142.4 7.3 %all-to-all-start.1 = ((bf16[32,32,512]{2,1,0:T(8,128)(2,1)}), bf16[32,32,512]{2,1,0:T(8,128)(2,1)S(1)}, u32[]{:S(2)}, u32[]{:S(2)}) async-start(bf16[32,32,512]{2,1,0:T(8,128)(2,1)} %get-tuple-element.27), calls=%async_computation.1 | async-start | bytes 2097152 | tf_op jit(solution)/shard_map/all_to_all | solution.py:364
  149.6 14.7 %shard_map.107 = (bf16[3,224,512]{2,1,0:T(8,128)(2,1)}, bf16[3,224,512]{2,1,0:T(8,128)(2,1)}, bf16[3,224,512]{2,1,0:T(8,128)(2,1)}, bf16[3,224,512]{2,1,0:T(8,128)(2,1)}, bf16[32,40,512]{2,1,0:T(8,128)(2,1)}) custom-call(bf16[32,64,512]{2,1,0:T(8,128)(2,1)} %all-to-all-done.2.refs_0_, bf16[3,224,512]{2,1,0:T(8,128)(2,1)} %collective-permute-done.1.refs_1_, ...), custom_call_target="tpu_custom_call" | custom-call | tf_op jit(solution)/shard_map/pallas_call | solution.py:240
  164.3 3.3 %collective-permute-start.8 = (bf16[3,224,512]{2,1,0:T(8,128)(2,1)}, bf16[3,224,512]{2,1,0:T(8,128)(2,1)}, u32[]{:S(2)}, u32[]{:S(2)}) collective-permute-start(bf16[3,224,512]{2,1,0:T(8,128)(2,1)} %get-tuple-element.39), channel_id=1, source_target_pairs={{0,96},{32,0},{64,32},{96,64},{1,97},{33,1},{65,33},{97,65},{2,98}... | collective-permute-start | bytes 2064392 | tf_op jit(solution)/shard_map/ppermute | solution.py:356
  167.6 0.1 collective-permute-start.12
  167.7 2.1 add_convert_fusion.1
  169.8 1.9 collective-permute-start.11
  171.8 7.4 %all-to-all-start.3 = ((bf16[32,40,512]{2,1,0:T(8,128)(2,1)}), bf16[32,40,512]{2,1,0:T(8,128)(2,1)S(1)}, u32[]{:S(2)}, u32[]{:S(2)}) async-start(bf16[32,40,512]{2,1,0:T(8,128)(2,1)} %get-tuple-element.33), calls=%async_computation.3 | async-start | bytes 2621440 | tf_op jit(solution)/shard_map/all_to_all | solution.py:364
  179.2 0.1 collective-permute-start.7
  179.3 4.5 %collective-permute-done.8 = bf16[3,224,512]{2,1,0:T(8,128)(2,1)} collective-permute-done((bf16[3,224,512]{2,1,0:T(8,128)(2,1)}, bf16[3,224,512]{2,1,0:T(8,128)(2,1)}, u32[]{:S(2)}, u32[]{:S(2)}) %collective-permute-start.8) | collective-permute-done | bytes 688160 | tf_op jit(solution)/shard_map/ppermute | solution.py:356
  183.7 2.3 %add_convert_fusion.2 = bf16[3,224,512]{2,1,0:T(8,128)(2,1)} fusion(bf16[3,224,512]{2,1,0:T(8,128)(2,1)} %collective-permute-done.8, bf16[3,224,512]{2,1,0:T(8,128)(2,1)} %get-tuple-element.38), kind=kLoop, calls=%fused_computation.4 | loop fusion | flops 1376256 | bytes 2064384 | tf_op jit(solution)/shard_map/convert_element_type | solution.py:368
  186.1 3.7 %collective-permute-start.9 = (bf16[3,224,512]{2,1,0:T(8,128)(2,1)}, bf16[3,224,512]{2,1,0:T(8,128)(2,1)}, u32[]{:S(2)}, u32[]{:S(2)}) collective-permute-start(bf16[3,224,512]{2,1,0:T(8,128)(2,1)} %add_convert_fusion.2), channel_id=1, source_target_pairs={{0,96},{32,0},{64,32},{96,64},{1,97},{33,1},{65,33},{97,65},{2,98}... | collective-permute-start | bytes 2064392 | tf_op jit(solution)/shard_map/ppermute | solution.py:356
  189.8 8.7 %collective-permute-done.12 = bf16[3,224,512]{2,1,0:T(8,128)(2,1)} collective-permute-done((bf16[3,224,512]{2,1,0:T(8,128)(2,1)}, bf16[3,224,512]{2,1,0:T(8,128)(2,1)}, u32[]{:S(2)}, u32[]{:S(2)}) %collective-permute-start.12) | collective-permute-done | bytes 688160 | tf_op jit(solution)/shard_map/ppermute | solution.py:356
  198.5 2.6 %add_convert_fusion = bf16[3,224,512]{2,1,0:T(8,128)(2,1)} fusion(bf16[3,224,512]{2,1,0:T(8,128)(2,1)} %collective-permute-done.12, bf16[3,224,512]{2,1,0:T(8,128)(2,1)} %collective-permute-done.11, bf16[3,224,512]{2,1,0:T(8,128)(2,1)S(1)} %copy-done.11), kind=kLoop, calls=%fused_computation.2 | loop fusion | flops 2064384 | bytes 2752512 | tf_op jit(solution)/shard_map/convert_element_type | solution.py:368
  201.1 3.3 %collective-permute-start.13 = (bf16[3,224,512]{2,1,0:T(8,128)(2,1)}, bf16[3,224,512]{2,1,0:T(8,128)(2,1)}, u32[]{:S(2)}, u32[]{:S(2)}) collective-permute-start(bf16[3,224,512]{2,1,0:T(8,128)(2,1)} %add_convert_fusion), channel_id=1, source_target_pairs={{0,16},{16,0},{1,17},{17,1},{2,18},{18,2},{3,19},{19,3},{4,20},{20... | collective-permute-start | bytes 2064392 | tf_op jit(solution)/shard_map/ppermute | solution.py:360
  204.4 1.5 combine_first.1.part
  205.9 3.7 %combine_last.1 = (bf16[128,4096]{1,0:T(8,128)(2,1)}, f32[8,1024]{1,0:T(8,128)S(1)}) custom-call(f32[8,1024]{1,0:T(8,128)S(1)} %maximum_bitcast_fusion.table, f32[1024,512]{1,0:T(8,128)S(1)} %combine_first.1.part, bf16[32,40,512]{2,1,0:T(8,128)(2,1)S(1)} %all-to-all-done.3.back), custom_call_target="tpu_custom_call" | custom-call | tf_op jit(solution)/shard_map/combine_last/pallas_call | solution.py:316
  209.6 0.6 slice_bitcast_fusion
  210.2 2.3 %collective-permute-done.9.own2 = bf16[3,224,512]{2,1,0:T(8,128)(2,1)} collective-permute-done((bf16[3,224,512]{2,1,0:T(8,128)(2,1)}, bf16[3,224,512]{2,1,0:T(8,128)(2,1)}, u32[]{:S(2)}, u32[]{:S(2)}) %collective-permute-start.9) | collective-permute-done | bytes 688160 | tf_op jit(solution)/shard_map/ppermute | solution.py:356
  212.5 6.4 %collective-permute-done.13.other = bf16[3,224,512]{2,1,0:T(8,128)(2,1)} collective-permute-done((bf16[3,224,512]{2,1,0:T(8,128)(2,1)}, bf16[3,224,512]{2,1,0:T(8,128)(2,1)}, u32[]{:S(2)}, u32[]{:S(2)}) %collective-permute-start.13) | collective-permute-done | bytes 688160 | tf_op jit(solution)/shard_map/ppermute | solution.py:360
  218.9 2.8 %final.1 = (bf16[2,2,224,512]{3,2,1,0:T(8,128)(2,1)}, bf16[2,224,512]{2,1,0:T(8,128)(2,1)}) custom-call(s32[1]{0:T(128)} %bitcast.8.which, bf16[3,224,512]{2,1,0:T(8,128)(2,1)S(1)} %copy-done.6, bf16[3,224,512]{2,1,0:T(8,128)(2,1)} %collective-permute-done.7.own1, bf16[3,224,512]{2,1,0:T(8,128)(2,1)} %collective-permute-done.9.own2, ...), custom_call_target="tpu_custom_call" | custom-call | tf_op jit(solution)/shard_map/final/pallas_call | solution.py:343
  (34 shorter events, 0.1 us)
Async XLA Ops:
  2.2 1.2 copy-start.2
  3.4 1.2 copy-start.4
  8.4 8.6 %copy-start.13 = (bf16[2,224,512]{2,1,0:T(8,128)(2,1)S(1)}, bf16[2,224,512]{2,1,0:T(8,128)(2,1)}, u32[]{:S(2)}) copy-start(bf16[2,224,512]{2,1,0:T(8,128)(2,1)} %param.13) | copy-start | bytes 1376260
  8.4 36.4 %all-to-all-start = ((bf16[32,64,512]{2,1,0:T(8,128)(2,1)}), bf16[32,64,512]{2,1,0:T(8,128)(2,1)S(1)}, u32[]{:S(2)}, u32[]{:S(2)}) async-start(bf16[32,64,512]{2,1,0:T(8,128)(2,1)} %shard_map.102), calls=%async_computation | async-start | bytes 4194304 | tf_op jit(solution)/shard_map/all_to_all | solution.py:364
  17.1 5.8 %copy-start.3 = (bf16[128,4096]{1,0:T(8,128)(2,1)S(1)}, bf16[128,4096]{1,0:T(8,128)(2,1)}, u32[]{:S(2)}) copy-start(bf16[128,4096]{1,0:T(8,128)(2,1)} %tok.3) | copy-start | bytes 3145732
  17.1 5.8 %copy-start.5 = (bf16[128,4096]{1,0:T(8,128)(2,1)S(1)}, bf16[128,4096]{1,0:T(8,128)(2,1)}, u32[]{:S(2)}) copy-start(bf16[128,4096]{1,0:T(8,128)(2,1)} %cot.3) | copy-start | bytes 3145732
  19.5 64.3 %copy-start.7 = (bf16[3,224,512]{2,1,0:T(8,128)(2,1)}, bf16[3,224,512]{2,1,0:T(8,128)(2,1)S(1)}, u32[]{:S(2)}) copy-start(bf16[3,224,512]{2,1,0:T(8,128)(2,1)S(1)} %get-tuple-element.49.refs_4_) | copy-start | bytes 2064388
  19.5 45.0 %collective-permute-start.3 = (bf16[3,224,512]{2,1,0:T(8,128)(2,1)}, bf16[3,224,512]{2,1,0:T(8,128)(2,1)}, u32[]{:S(2)}, u32[]{:S(2)}) collective-permute-start(bf16[3,224,512]{2,1,0:T(8,128)(2,1)} %get-tuple-element.48), channel_id=1, source_target_pairs={{0,16},{16,0},{1,17},{17,1},{2,18},{18,2},{3,19},{19,3},{4,20},{20... | collective-permute-start | bytes 2064392 | tf_op jit(solution)/shard_map/ppermute | solution.py:360
  44.8 70.8 %all-to-all-start.2 = ((bf16[32,64,512]{2,1,0:T(8,128)(2,1)}), bf16[32,64,512]{2,1,0:T(8,128)(2,1)}, u32[]{:S(2)}, u32[]{:S(2)}) async-start(bf16[32,64,512]{2,1,0:T(8,128)(2,1)} %shard_map.105), calls=%async_computation.2 | async-start | bytes 4194304 | tf_op jit(solution)/shard_map/all_to_all | solution.py:364
  64.5 19.0 %collective-permute-start.4 = (bf16[3,224,512]{2,1,0:T(8,128)(2,1)}, bf16[3,224,512]{2,1,0:T(8,128)(2,1)S(1)}, u32[]{:S(2)}, u32[]{:S(2)}) collective-permute-start(bf16[3,224,512]{2,1,0:T(8,128)(2,1)} %collective-permute-done.3.refs_4_), channel_id=1, source_target_pairs={{0,32},{32,64},{64,96},{96,0},{1,33},{33,65},{65,97},{97,1},{2,34}... | collective-permute-start | bytes 2064392 | tf_op jit(solution)/shard_map/ppermute | solution.py:356
  66.1 19.3 %collective-permute-start = (bf16[3,224,512]{2,1,0:T(8,128)(2,1)S(1)}, bf16[3,224,512]{2,1,0:T(8,128)(2,1)}, u32[]{:S(2)}, u32[]{:S(2)}) collective-permute-start(bf16[3,224,512]{2,1,0:T(8,128)(2,1)S(1)} %get-tuple-element.49.refs_4_), channel_id=1, source_target_pairs={{0,96},{32,0},{64,32},{96,64},{1,97},{33,1},{65,33},{97,65},{2,98}... | collective-permute-start | bytes 2064392 | tf_op jit(solution)/shard_map/ppermute | solution.py:356
  67.8 31.3 %collective-permute-start.6 = (bf16[3,224,512]{2,1,0:T(8,128)(2,1)}, bf16[3,224,512]{2,1,0:T(8,128)(2,1)S(1)}, u32[]{:S(2)}, u32[]{:S(2)}) collective-permute-start(bf16[3,224,512]{2,1,0:T(8,128)(2,1)} %collective-permute-done.3.refs_4_), channel_id=1, source_target_pairs={{0,96},{32,0},{64,32},{96,64},{1,97},{33,1},{65,33},{97,65},{2,98}... | collective-permute-start | bytes 2064392 | tf_op jit(solution)/shard_map/ppermute | solution.py:356
  83.5 19.5 %copy-start.8 = (bf16[3,224,512]{2,1,0:T(8,128)(2,1)}, bf16[3,224,512]{2,1,0:T(8,128)(2,1)S(1)}, u32[]{:S(2)}) copy-start(bf16[3,224,512]{2,1,0:T(8,128)(2,1)S(1)} %collective-permute-done.4.refs_3_) | copy-start | bytes 2064388
  83.5 19.5 %collective-permute-start.5 = (bf16[3,224,512]{2,1,0:T(8,128)(2,1)S(1)}, bf16[3,224,512]{2,1,0:T(8,128)(2,1)S(1)}, u32[]{:S(2)}, u32[]{:S(2)}) collective-permute-start(bf16[3,224,512]{2,1,0:T(8,128)(2,1)S(1)} %collective-permute-done.4.refs_3_), channel_id=1, source_target_pairs={{0,32},{32,64},{64,96},{96,0},{1,33},{33,65},{65,97},{97,1},{2,34}... | collective-permute-start | bytes 2064392 | tf_op jit(solution)/shard_map/ppermute | solution.py:356
  83.8 46.2 %collective-permute-start.2 = (bf16[3,224,512]{2,1,0:T(8,128)(2,1)S(1)}, bf16[3,224,512]{2,1,0:T(8,128)(2,1)}, u32[]{:S(2)}, u32[]{:S(2)}) collective-permute-start(bf16[3,224,512]{2,1,0:T(8,128)(2,1)S(1)} %get-tuple-element.49.refs_4_), channel_id=1, source_target_pairs={{0,32},{32,64},{64,96},{96,0},{1,33},{33,65},{65,97},{97,1},{2,34}... | collective-permute-start | bytes 2064392 | tf_op jit(solution)/shard_map/ppermute | solution.py:356
  85.3 44.7 %collective-permute-start.1 = (bf16[3,224,512]{2,1,0:T(8,128)(2,1)}, bf16[3,224,512]{2,1,0:T(8,128)(2,1)}, u32[]{:S(2)}, u32[]{:S(2)}) collective-permute-start(bf16[3,224,512]{2,1,0:T(8,128)(2,1)} %collective-permute-done.refs_2_), channel_id=1, source_target_pairs={{0,96},{32,0},{64,32},{96,64},{1,97},{33,1},{65,33},{97,65},{2,98}... | collective-permute-start | bytes 2064392 | tf_op jit(solution)/shard_map/ppermute | solution.py:356
  99.1 4.0 %copy-start.9 = (bf16[3,224,512]{2,1,0:T(8,128)(2,1)}, bf16[3,224,512]{2,1,0:T(8,128)(2,1)S(1)}, u32[]{:S(2)}) copy-start(bf16[3,224,512]{2,1,0:T(8,128)(2,1)S(1)} %collective-permute-done.6.refs_2_) | copy-start | bytes 2064388
  103.1 0.8 copy-start.10
  130.0 37.7 %collective-permute-start.10 = (bf16[3,224,512]{2,1,0:T(8,128)(2,1)}, bf16[3,224,512]{2,1,0:T(8,128)(2,1)}, u32[]{:S(2)}, u32[]{:S(2)}) collective-permute-start(bf16[3,224,512]{2,1,0:T(8,128)(2,1)} %get-tuple-element.42), channel_id=1, source_target_pairs={{0,32},{32,64},{64,96},{96,0},{1,33},{33,65},{65,97},{97,1},{2,34}... | collective-permute-start | bytes 2064392 | tf_op jit(solution)/shard_map/ppermute | solution.py:356
  142.4 29.4 %all-to-all-start.1 = ((bf16[32,32,512]{2,1,0:T(8,128)(2,1)}), bf16[32,32,512]{2,1,0:T(8,128)(2,1)S(1)}, u32[]{:S(2)}, u32[]{:S(2)}) async-start(bf16[32,32,512]{2,1,0:T(8,128)(2,1)} %get-tuple-element.27), calls=%async_computation.1 | async-start | bytes 2097152 | tf_op jit(solution)/shard_map/all_to_all | solution.py:364
  149.6 18.0 %copy-start.12 = (bf16[3,224,512]{2,1,0:T(8,128)(2,1)S(1)}, bf16[3,224,512]{2,1,0:T(8,128)(2,1)}, u32[]{:S(2)}) copy-start(bf16[3,224,512]{2,1,0:T(8,128)(2,1)} %get-tuple-element.41) | copy-start | bytes 2064388
  164.3 19.4 %collective-permute-start.8 = (bf16[3,224,512]{2,1,0:T(8,128)(2,1)}, bf16[3,224,512]{2,1,0:T(8,128)(2,1)}, u32[]{:S(2)}, u32[]{:S(2)}) collective-permute-start(bf16[3,224,512]{2,1,0:T(8,128)(2,1)} %get-tuple-element.39), channel_id=1, source_target_pairs={{0,96},{32,0},{64,32},{96,64},{1,97},{33,1},{65,33},{97,65},{2,98}... | collective-permute-start | bytes 2064392 | tf_op jit(solution)/shard_map/ppermute | solution.py:356
  167.6 30.9 %collective-permute-start.12 = (bf16[3,224,512]{2,1,0:T(8,128)(2,1)}, bf16[3,224,512]{2,1,0:T(8,128)(2,1)}, u32[]{:S(2)}, u32[]{:S(2)}) collective-permute-start(bf16[3,224,512]{2,1,0:T(8,128)(2,1)} %get-tuple-element.43), channel_id=1, source_target_pairs={{0,96},{32,0},{64,32},{96,64},{1,97},{33,1},{65,33},{97,65},{2,98}... | collective-permute-start | bytes 2064392 | tf_op jit(solution)/shard_map/ppermute | solution.py:356
  169.8 28.7 %collective-permute-start.11 = (bf16[3,224,512]{2,1,0:T(8,128)(2,1)}, bf16[3,224,512]{2,1,0:T(8,128)(2,1)}, u32[]{:S(2)}, u32[]{:S(2)}) collective-permute-start(bf16[3,224,512]{2,1,0:T(8,128)(2,1)} %add_convert_fusion.1), channel_id=1, source_target_pairs={{0,32},{32,64},{64,96},{96,0},{1,33},{33,65},{65,97},{97,1},{2,34}... | collective-permute-start | bytes 2064392 | tf_op jit(solution)/shard_map/ppermute | solution.py:356
  171.8 14.3 %copy-start = (bf16[32,32,512]{2,1,0:T(8,128)(2,1)}, bf16[32,32,512]{2,1,0:T(8,128)(2,1)S(1)}, u32[]{:S(2)}) copy-start(bf16[32,32,512]{2,1,0:T(8,128)(2,1)S(1)} %all-to-all-done.1.back) | copy-start | bytes 3145732
  171.8 34.1 %all-to-all-start.3 = ((bf16[32,40,512]{2,1,0:T(8,128)(2,1)}), bf16[32,40,512]{2,1,0:T(8,128)(2,1)S(1)}, u32[]{:S(2)}, u32[]{:S(2)}) async-start(bf16[32,40,512]{2,1,0:T(8,128)(2,1)} %get-tuple-element.33), calls=%async_computation.3 | async-start | bytes 2621440 | tf_op jit(solution)/shard_map/all_to_all | solution.py:364
  179.2 19.3 %copy-start.11 = (bf16[3,224,512]{2,1,0:T(8,128)(2,1)S(1)}, bf16[3,224,512]{2,1,0:T(8,128)(2,1)}, u32[]{:S(2)}) copy-start(bf16[3,224,512]{2,1,0:T(8,128)(2,1)} %get-tuple-element.40) | copy-start | bytes 2064388
  179.2 31.0 %collective-permute-start.7 = (bf16[3,224,512]{2,1,0:T(8,128)(2,1)}, bf16[3,224,512]{2,1,0:T(8,128)(2,1)}, u32[]{:S(2)}, u32[]{:S(2)}) collective-permute-start(bf16[3,224,512]{2,1,0:T(8,128)(2,1)} %get-tuple-element.37), channel_id=1, source_target_pairs={{0,32},{32,64},{64,96},{96,0},{1,33},{33,65},{65,97},{97,1},{2,34}... | collective-permute-start | bytes 2064392 | tf_op jit(solution)/shard_map/ppermute | solution.py:356
  186.1 26.4 %collective-permute-start.9 = (bf16[3,224,512]{2,1,0:T(8,128)(2,1)}, bf16[3,224,512]{2,1,0:T(8,128)(2,1)}, u32[]{:S(2)}, u32[]{:S(2)}) collective-permute-start(bf16[3,224,512]{2,1,0:T(8,128)(2,1)} %add_convert_fusion.2), channel_id=1, source_target_pairs={{0,96},{32,0},{64,32},{96,64},{1,97},{33,1},{65,33},{97,65},{2,98}... | collective-permute-start | bytes 2064392 | tf_op jit(solution)/shard_map/ppermute | solution.py:356
  198.5 5.9 %copy-start.1 = (bf16[32,32,512]{2,1,0:T(8,128)(2,1)S(1)}, bf16[32,32,512]{2,1,0:T(8,128)(2,1)}, u32[]{:S(2)}) copy-start(bf16[32,32,512]{2,1,0:T(8,128)(2,1)} %copy-done) | copy-start | bytes 3145732
  201.1 17.9 %collective-permute-start.13 = (bf16[3,224,512]{2,1,0:T(8,128)(2,1)}, bf16[3,224,512]{2,1,0:T(8,128)(2,1)}, u32[]{:S(2)}, u32[]{:S(2)}) collective-permute-start(bf16[3,224,512]{2,1,0:T(8,128)(2,1)} %add_convert_fusion), channel_id=1, source_target_pairs={{0,16},{16,0},{1,17},{17,1},{2,18},{18,2},{3,19},{19,3},{4,20},{20... | collective-permute-start | bytes 2064392 | tf_op jit(solution)/shard_map/ppermute | solution.py:360
  205.9 13.0 %copy-start.6 = (bf16[3,224,512]{2,1,0:T(8,128)(2,1)S(1)}, bf16[3,224,512]{2,1,0:T(8,128)(2,1)}, u32[]{:S(2)}) copy-start(bf16[3,224,512]{2,1,0:T(8,128)(2,1)} %get-tuple-element.36.own0) | copy-start | bytes 2064388

commit v2 on v1

--- a/solution.py
+++ b/solution.py
@@ -70,11 +70,14 @@
     )(table, tok, cot)
 
 
-def expert_block(z, slots, wg, wu, wo):
-    hidden = wg.shape[0]
-    rows = PEERS * slots
-    x = z[:, 0:slots, :].reshape(rows, DS)
-    s = z[:, slots : 2 * slots, :].reshape(rows, DS)
+HBM = pl.BlockSpec(memory_space=pltpu.HBM)
+WHOLE = pl.BlockSpec(memory_space=pltpu.VMEM)
+UNITS = 2 * SH
+STEPS = 2
+
+
+def expert_block(x, s, wg, wu, wo):
+    hidden, rows = wg.shape[0], x.shape[0]
     g = contract(wg, x, 1, 1)
     u = contract(wu, x, 1, 1)
     dh = contract(wo, s, 1, 1)
@@ -88,11 +91,6 @@
     dw = (contract(dg, x, 1, 0), contract(du, x, 1, 0), contract(hid, s, 1, 0))
     dx = contract(dg, wg, 0, 0) + contract(du, wu, 0, 0)
     return dw, dx, router
-
-
-HBM = pl.BlockSpec(memory_space=pltpu.HBM)
-WHOLE = pl.BlockSpec(memory_space=pltpu.VMEM)
-UNITS = 2 * SH
 
 
 def router_rows(back, slots, router_first, router):
@@ -114,19 +112,24 @@
     back[:, slots : slots + EXTRA, 128:DS] = jnp.zeros((PEERS, EXTRA, DS - 128), BF)
 
 
-def expert_kernel(*refs, part, end):
+def expert_kernel(*refs, part, pairs, first, begin, end):
     slots = SLOTS[part]
+    step_peers = PEERS // STEPS
+    step_rows = step_peers * slots
+    last = part == 1 and end
     refs = list(refs)
     take = lambda n: [refs.pop(0) for _ in range(n)]
-    (z,) = take(1)
-    weights = take(4)
+    (z_in,) = take(1)
+    weights = take(2 * pairs)
     before = take(1)[0] if part else None
-    acc_in, router_in = take(2) if end else (None, None)
-    router_first = take(1)[0] if part and end else None
-    outs = take(4 if part else 1)
+    acc_in, router_in = (None, None) if begin else take(2)
+    router_first = take(1)[0] if last else None
+    outs = take(2 * pairs if part else 1)
     (dx_out,) = take(1)
-    router_out = None if part and end else take(1)[0]
-    acc, wbuf, stage, obuf, asem, wsem, bsem, ssem = refs
+    router = None if last else take(1)[0]
+    if last:
+        router = refs.pop()
+    z, acc, wbuf, stage, obuf, zsem, asem, wsem, bsem, ssem = refs
 
     def units(p):
         return pl.ds(pl.multiple_of(p * UNITS, UNITS), UNITS)
@@ -138,7 +141,7 @@
         )
 
     def load(p):
-        return pltpu.make_async_copy(before.at[:, units(p), :], stage.at[p], bsem.at[p])
+        return pltpu.make_async_copy(before.at[:, units(first + p), :], stage.at[p], bsem.at[p])
 
     def store_wide(p):
         return pltpu.make_async_copy(stage.at[p], outs[0].at[:, units(p), :], bsem.at[p])
@@ -148,56 +151,79 @@
             obuf.at[p, :, half * SH : (half + 1) * SH, :], outs[2 * p + half], ssem.at[p, half]
         )
 
-    for k in range(4):
+    z_load = pltpu.make_async_copy(z_in, z, zsem)
+    z_load.start()
+    for k in range(2 * pairs):
         fetch(k, k // 2).start()
     if part:
-        for p in range(2):
+        for p in range(pairs):
             load(p).start()
-    if end:
+    else:
+        stage[...] = jnp.zeros_like(stage)
+    if begin:
+        acc[...] = jnp.zeros_like(acc)
+        router[...] = jnp.zeros_like(router)
+    else:
         acc_load = pltpu.make_async_copy(acc_in, acc, asem)
         acc_load.start()
-    else:
-        acc[...] = jnp.zeros_like(acc)
-    router = jnp.zeros((8, PEERS * slots), F32) if not end else router_in[...]
-
-    def block(p, router):
-        fetch(0, p).wait()
-        fetch(1, p).wait()
-        parts, dx, r = expert_block(z, slots, wbuf[p, 0], wbuf[p, 1], wbuf[p, 2])
+        router[...] = router_in[...]
+    z_load.wait()
+
+    def block(i, carry):
+        p = i // STEPS
+        b = i % STEPS
+
+        @pl.when(b == 0)
+        def _():
+            fetch(0, p).wait()
+            fetch(1, p).wait()
+
+        here = pl.ds(b * step_peers, step_peers)
+        x = z[here, 0:slots, :].reshape(step_rows, DS)
+        s = z[here, slots : 2 * slots, :].reshape(step_rows, DS)
+        parts, dx, r = expert_block(x, s, wbuf[p, 0], wbuf[p, 1], wbuf[p, 2])
         if part:
-            load(p).wait()
-            for k in range(3):
-                obuf[p, k] = (parts[k] + stage[p, k]).astype(BF)
-            for q in range(2):
-
-                @pl.when(p == q)
-                def _():
-                    for half in range(2):
-                        store(q, half).start()
-        else:
-            for k in range(3):
-                stage[p, k] = parts[k]
-            store_wide(p).start()
-        if end:
-
-            @pl.when(p == 0)
+
+            @pl.when(b == 0)
+            def _():
+                load(p).wait()
+
+        if not begin:
+
+            @pl.when(i == 0)
             def _():
                 acc_load.wait()
 
-        acc[...] += dx
-        return router + r
-
-    router = lax.fori_loop(0, 2, block, router)
+        for k in range(3):
+            stage[p, k] += parts[k]
+        acc[b] += dx
+        router[b] += r
+
+        @pl.when(b == STEPS - 1)
+        def _():
+            if part:
+                obuf[p] = stage[p].astype(BF)
+                for q in range(pairs):
+
+                    @pl.when(p == q)
+                    def _():
+                        store(q, 0).start()
+                        store(q, 1).start()
+            else:
+                store_wide(p).start()
+
+        return carry
+
+    lax.fori_loop(0, pairs * STEPS, block, 0)
     if end:
         dx_out[:, 0:slots, :] = acc[...].astype(BF).reshape(PEERS, slots, DS)
     else:
         acc_save = pltpu.make_async_copy(acc, dx_out, asem)
         acc_save.start()
-    if router_out is None:
-        router_rows(dx_out, slots, router_first[...], router)
-    else:
-        router_out[...] = router
-    for p in range(2):
+    if last:
+        flat = [jnp.concatenate([r[b] for b in range(STEPS)], axis=1) for r in (router_first, router)]
+        router_rows(dx_out, slots, *flat)
+    for p in range(pairs):
         if part:
             store(p, 0).wait()
             store(p, 1).wait()
@@ -207,50 +233,55 @@
         acc_save.wait()
 
 
-def expert_part(part, z, weights, before=None, carry=None, router_first=None):
-    end = carry is not None
+def expert_part(part, z, weights, before=None, first=0, carry=None, end=False, router_first=None):
+    pairs = len(weights) // 2
     slots = SLOTS[part]
-    rows = PEERS * slots
+    step_rows = PEERS // STEPS * slots
+    last = part == 1 and end
     args = [z, *[in_hbm(w) for w in weights]]
-    in_specs = [WHOLE] + [HBM] * 4
+    in_specs = [pl.BlockSpec(memory_space=pl.ANY)] + [HBM] * len(weights)
     if part:
         args += [in_hbm(before)]
         in_specs += [HBM]
-    if end:
+    if carry is not None:
         args += [in_hbm(carry[0]), carry[1]]
         in_specs += [HBM, WHOLE]
-    if part and end:
+    if last:
         args += [router_first]
         in_specs += [WHOLE]
     if part:
-        out_shape = [pltpu.HBM((3, SH, DS), BF)] * 4
-        out_specs = [HBM] * 4
+        out_shape = [pltpu.HBM((3, SH, DS), BF)] * (2 * pairs)
     else:
-        out_shape = [pltpu.HBM((3, 4 * SH, DS), F32)]
-        out_specs = [HBM]
+        out_shape = [pltpu.HBM((3, pairs * UNITS, DS), F32)]
+    out_specs = [HBM] * len(out_shape)
     if end:
         out_shape += [pltpu.HBM((PEERS, slots + part * EXTRA, DS), BF)]
         out_specs += [WHOLE]
     else:
-        out_shape += [pltpu.HBM((rows, DS), F32)]
+        out_shape += [pltpu.HBM((STEPS, step_rows, DS), F32)]
         out_specs += [HBM]
-    if not (part and end):
-        out_shape += [jax.ShapeDtypeStruct((8, rows), F32)]
+    if not last:
+        out_shape += [jax.ShapeDtypeStruct((STEPS, 8, step_rows), F32)]
         out_specs += [WHOLE]
     return pl.pallas_call(
-        functools.partial(expert_kernel, part=part, end=end),
+        functools.partial(
+            expert_kernel, part=part, pairs=pairs, first=first, begin=carry is None, end=end
+        ),
         in_specs=in_specs,
         out_specs=out_specs,
         out_shape=out_shape,
         scratch_shapes=[
-            pltpu.VMEM((rows, DS), F32),
-            pltpu.VMEM((2, 3, UNITS, DS), BF),
-            pltpu.VMEM((2, 3, UNITS, DS), F32),
-            pltpu.VMEM((2, 3, UNITS, DS) if part else (8, 128), BF),
+            pltpu.VMEM((PEERS, 2 * slots, DS), BF),
+            pltpu.VMEM((STEPS, step_rows, DS), F32),
+            pltpu.VMEM((pairs, 3, UNITS, DS), BF),
+            pltpu.VMEM((pairs, 3, UNITS, DS), F32),
+            pltpu.VMEM((pairs, 3, UNITS, DS) if part else (8, 128), BF),
             pltpu.SemaphoreType.DMA,
-            pltpu.SemaphoreType.DMA((2, 2)),
-            pltpu.SemaphoreType.DMA((2,)),
-            pltpu.SemaphoreType.DMA((2, 2)),
+            pltpu.SemaphoreType.DMA,
+            pltpu.SemaphoreType.DMA((pairs, 2)),
+            pltpu.SemaphoreType.DMA((pairs,)),
+            pltpu.SemaphoreType.DMA((pairs, 2)),
+            *([pltpu.VMEM((STEPS, 8, step_rows), F32)] if last else []),
         ],
         compiler_params=params(36),
     )(*args)
@@ -324,32 +355,55 @@
     )(table, part, back)
 
 
-def final_kernel(which, own0, own1, own2, other, grad_in, grad_out):
+def final_own_kernel(which, own0, own1, own2, grad_in, grad_out, total, sems):
     a = which[0]
-    b = 1 - a
     for k in range(3):
-        total = own0[k].astype(F32) + own1[k].astype(F32) + own2[k].astype(F32)
-        total = total.astype(BF)
-        if k < 2:
-            grad_in[a, k] = total
-            grad_in[b, k] = other[k]
-        else:
-            grad_out[a] = total
-            grad_out[b] = other[k]
+        value = own0[k].astype(F32) + own1[k].astype(F32) + own2[k].astype(F32)
+        total[k] = value.astype(BF)
+    copies = (
+        pltpu.make_async_copy(total.at[0:2], grad_in.at[a], sems.at[0]),
+        pltpu.make_async_copy(total.at[2], grad_out.at[a], sems.at[1]),
+    )
+    for c in copies:
+        c.start()
+    for c in copies:
+        c.wait()
+
+
+def final_other_kernel(which, other, _in, _out, grad_in, grad_out, sems):
+    b = 1 - which[0]
+    copies = (
+        pltpu.make_async_copy(other.at[0:2], grad_in.at[b], sems.at[0]),
+        pltpu.make_async_copy(other.at[2], grad_out.at[b], sems.at[1]),
+    )
+    for c in copies:
+        c.start()
+    for c in copies:
+        c.wait()
 
 
 def final(which, own, other):
-    vmem = pl.BlockSpec(memory_space=pltpu.VMEM)
+    smem = pl.BlockSpec(memory_space=pltpu.SMEM)
+    out_shape = [pltpu.HBM((2, 2, SH, DS), BF), pltpu.HBM((2, SH, DS), BF)]
+    grads = pl.pallas_call(
+        final_own_kernel,
+        in_specs=[smem] + [WHOLE] * 3,
+        out_specs=[HBM, HBM],
+        out_shape=out_shape,
+        scratch_shapes=[pltpu.VMEM((3, SH, DS), BF), pltpu.SemaphoreType.DMA((2,))],
+        compiler_params=params(),
+        name="final_own",
+    )(which, *own)
     return pl.pallas_call(
-        final_kernel,
-        in_specs=[pl.BlockSpec(memory_space=pltpu.SMEM)] + [vmem] * 4,
-        out_shape=[
-            jax.ShapeDtypeStruct((2, 2, SH, DS), BF),
-            jax.ShapeDtypeStruct((2, SH, DS), BF),
-        ],
+        final_other_kernel,
+        in_specs=[smem] + [HBM] * 3,
+        out_specs=[HBM, HBM],
+        out_shape=out_shape,
+        input_output_aliases={2: 0, 3: 1},
+        scratch_shapes=[pltpu.SemaphoreType.DMA((2,))],
         compiler_params=params(),
-        name="final",
-    )(which, *own, other)
+        name="final_other",
+    )(which, in_hbm(other), *[in_hbm(g) for g in grads])
 
 
 def ring(a, step):
@@ -371,9 +425,8 @@
 def layer(tokens, cotangent, expert_ids, slot_ids, route_probs, weights_in, weights_out):
     yh = lax.axis_index("yh")
     both = jnp.concatenate([weights_in, weights_out[:, None]], axis=1)
-    theirs = jnp.where(yh == 0, both[1], both[0])
+    w_p = swap(jnp.where(yh == 0, both[1], both[0]))
     w_o = jnp.where(yh == 0, both[0], both[1])
-    w_p = swap(theirs)
     w_o_m = ring(w_o, 1)
     w_o_p = ring(w_o, -1)
     w_p_m = ring(w_p, 1)
@@ -394,20 +447,22 @@
     z1 = exchange(dispatch(table, tokens, cotangent, 0))
     z2 = exchange(dispatch(table, tokens, cotangent, 1))
 
-    w_p = [w_p_2, w_p_p, w_p_m, w_p]
-    w_o = [w_o_2, w_o_p, w_o_m, w_o]
-    dw_p, *carry = expert_part(0, z1, w_p)
-    dw_o, back1, router1 = expert_part(0, z1, w_o, carry=carry)
+    near = [w_p_p, w_p_m, w_o_p, w_o_m]
+    far = [w_p_2, w_o_2]
+    own = [w_p, w_o]
+    dw_near, *carry = expert_part(0, z1, near)
+    dw_rest, back1, router1 = expert_part(0, z1, far + own, carry=carry, end=True)
     back1 = exchange(back1)
-    p_2, p_p, p_m, p_0, *carry = expert_part(1, z2, w_p, dw_p)
+    p_2, o_2, *carry = expert_part(1, z2, far, dw_rest)
     p_2 = ring(p_2, 1)
+    o_2 = ring(o_2, -1)
+    p_p, p_m, o_p, o_m, *carry = expert_part(1, z2, near, dw_near, 0, carry)
     p_m = ring(p_m, -1)
-    o_2, o_p, o_m, o_0, back2 = expert_part(1, z2, w_o, dw_o, carry, router1)
+    p_p = ring(add(p_p, p_2), 1)
+    o_m = ring(add(o_m, o_2), -1)
+    o_p = ring(o_p, 1)
+    p_0, o_0, back2 = expert_part(1, z2, own, dw_rest, 1, carry, True, router1)
     back2 = exchange(back2)
-    o_2 = ring(o_2, -1)
-    p_p = ring(add(p_p, p_2), 1)
-    o_p = ring(o_p, 1)
-    o_m = ring(add(o_m, o_2), -1)
     other = swap(add(p_0, p_p, p_m))
     grad_in, grad_out = final(yh.astype(jnp.int32).reshape(1), (o_0, o_p, o_m), other)
 

time: 223 us -> 248 us (1.11)
  Pallas kernels: 68.7 us -> 97.2 us
  waiting for transfers between devices: 69.8 us -> 59.3 us
  local copies, waits for them, and re-layouts: 3.96 us -> 9.76 us
    pallas_call x5 -> x7, Pallas kernels: 55.8 us -> 84.4 us  [the longest x5 60 us: expert_part(): pl.pallas_call(functools.partial(expert_kernel, part=part, pairs=pairs, f...]
    ppermute x12, waiting for transfers between devices: 45.3 us -> 27.5 us  [ring(): return lax.ppermute(a, 'x', [(i, (i + step) % 4) for i in range(4)])]
    all_to_all x4, waiting for transfers between devices: 18.1 us -> 24.7 us  [exchange(): return lax.all_to_all(a, PLANE, 0, 0, tiled=True)]
    unnamed x28 -> x38, local copies, waits for them, and re-layouts: 3.34 us -> 9.14 us
  transfers between devices with their start and end apart: 18 -> 18, of which waited for: 8 -> 6; matrix products, arithmetic and copies ran while one was open for 5% -> 4% of each run, Pallas kernels for 28% -> 25%
where the time goes in v2:
time: 248 us; the launch traced here: 247 us
  Pallas kernels  97.2 us (39%)
  starting transfers between devices  68.3 us (28%)
  waiting for transfers between devices  59.3 us (24%)
  other arithmetic  11.1 us (4%)
  local copies, waits for them, and re-layouts  9.76 us (4%)
    pallas_call x5, Pallas kernels, expert_part(): pl.pallas_call(functools.partial(expert_kernel, part=part, pairs=pairs, f...  60 us
    all_to_all x4, starting transfers between devices, exchange(): return lax.all_to_all(a, PLANE, 0, 0, tiled=True)  43 us
    ppermute x12, waiting for transfers between devices, ring(): return lax.ppermute(a, 'x', [(i, (i + step) % 4) for i in range(4)])  27.5 us
    all_to_all x4, waiting for transfers between devices, exchange(): return lax.all_to_all(a, PLANE, 0, 0, tiled=True)  24.7 us
    pallas_call x1, Pallas kernels, final(): pl.pallas_call(final_other_kernel, in_specs=[smem] + [HBM] * 3, out_specs...  22 us
    ppermute x12, starting transfers between devices, ring(): return lax.ppermute(a, 'x', [(i, (i + step) % 4) for i in range(4)])  18.7 us
    unnamed x38, local copies, waits for them, and re-layouts  9.14 us
    pallas_call x2, Pallas kernels, dispatch(): pl.pallas_call(functools.partial(dispatch_kernel, part=part), grid=(PEERS...  7.63 us
  transfers between devices with their start and end apart: 18, of which 6 were waited for; matrix products, arithmetic and copies ran while one was open for 4% of the time, Pallas kernels for 25%

profile of v2, /device:TPU:0, one launch (start us, length us, event | category | flops | bytes accessed | tf_op | source)
XLA Modules:
  0.0 246.7 jit_solution(856181780336189806)
XLA Ops:
  0.6 0.8 fusion.1
  1.5 0.7 convert_element_type.43
  2.2 1.2 copy-done.4
  3.4 1.2 copy-done.6
  4.6 3.8 %shard_map.102 = bf16[32,64,512]{2,1,0:T(8,128)(2,1)} custom-call(f32[8,1024]{1,0:T(8,128)S(1)} %maximum_bitcast_fusion.table, bf16[128,4096]{1,0:T(8,128)(2,1)S(1)} %copy-done.4, bf16[128,4096]{1,0:T(8,128)(2,1)S(1)} %copy-done.6), custom_call_target="tpu_custom_call" | custom-call | tf_op jit(solution)/shard_map/pallas_call | solution.py:59
  8.5 8.6 %all-to-all-start = ((bf16[32,64,512]{2,1,0:T(8,128)(2,1)}), bf16[32,64,512]{2,1,0:T(8,128)(2,1)S(1)}, u32[]{:S(2)}, u32[]{:S(2)}) async-start(bf16[32,64,512]{2,1,0:T(8,128)(2,1)} %shard_map.102), calls=%async_computation | async-start | bytes 4194304 | tf_op jit(solution)/shard_map/all_to_all | solution.py:418
  17.1 2.4 select_bitcast_fusion
  19.5 3.3 %collective-permute-start = (bf16[3,224,512]{2,1,0:T(8,128)(2,1)}, bf16[3,224,512]{2,1,0:T(8,128)(2,1)}, u32[]{:S(2)}, u32[]{:S(2)}) collective-permute-start(bf16[3,224,512]{2,1,0:T(8,128)(2,1)} %get-tuple-element.57), channel_id=1, source_target_pairs={{0,16},{16,0},{1,17},{17,1},{2,18},{18,2},{3,19},{19,3},{4,20},{20... | collective-permute-start | bytes 2064392 | tf_op jit(solution)/shard_map/ppermute | solution.py:414
  22.8 3.8 %shard_map.105 = bf16[32,64,512]{2,1,0:T(8,128)(2,1)} custom-call(f32[8,1024]{1,0:T(8,128)S(1)} %maximum_bitcast_fusion.table, bf16[128,4096]{1,0:T(8,128)(2,1)S(1)} %copy-done.5, bf16[128,4096]{1,0:T(8,128)(2,1)S(1)} %copy-done.7), custom_call_target="tpu_custom_call" | custom-call | tf_op jit(solution)/shard_map/pallas_call | solution.py:59
  26.6 18.2 %all-to-all-done.refs_0_ = bf16[32,64,512]{2,1,0:T(8,128)(2,1)S(1)} async-done(((bf16[32,64,512]{2,1,0:T(8,128)(2,1)}), bf16[32,64,512]{2,1,0:T(8,128)(2,1)S(1)}, u32[]{:S(2)}, u32[]{:S(2)}) %all-to-all-start) | async-done | bytes 2097184 | tf_op jit(solution)/shard_map/all_to_all | solution.py:418
  44.8 1.3 copy-done
  46.2 19.6 %all-to-all-start.2 = ((bf16[32,64,512]{2,1,0:T(8,128)(2,1)}), bf16[32,64,512]{2,1,0:T(8,128)(2,1)S(1)}, u32[]{:S(2)}, u32[]{:S(2)}) async-start(bf16[32,64,512]{2,1,0:T(8,128)(2,1)} %shard_map.105), calls=%async_computation.2 | async-start | bytes 4194304 | tf_op jit(solution)/shard_map/all_to_all | solution.py:418
  65.7 2.8 %collective-permute-start.3 = (bf16[3,224,512]{2,1,0:T(8,128)(2,1)S(1)}, bf16[3,224,512]{2,1,0:T(8,128)(2,1)S(1)}, u32[]{:S(2)}, u32[]{:S(2)}) collective-permute-start(bf16[3,224,512]{2,1,0:T(8,128)(2,1)S(1)} %get-tuple-element.56.refs_4_.refs_2_), channel_id=1, source_target_pairs={{0,96},{32,0},{64,32},{96,64},{1,97},{33,1},{65,33},{97,65},{2,98}... | collective-permute-start | bytes 2064392 | tf_op jit(solution)/shard_map/ppermute | solution.py:410
  68.6 0.8 collective-permute-start.6
  69.3 2.5 %collective-permute-start.5 = (bf16[3,224,512]{2,1,0:T(8,128)(2,1)}, bf16[3,224,512]{2,1,0:T(8,128)(2,1)S(1)}, u32[]{:S(2)}, u32[]{:S(2)}) collective-permute-start(bf16[3,224,512]{2,1,0:T(8,128)(2,1)} %collective-permute-done.refs_3_.refs_1_), channel_id=1, source_target_pairs={{0,96},{32,0},{64,32},{96,64},{1,97},{33,1},{65,33},{97,65},{2,98}... | collective-permute-start | bytes 2064392 | tf_op jit(solution)/shard_map/ppermute | solution.py:410
  71.9 12.5 %collective-permute-done.3.refs_3_ = bf16[3,224,512]{2,1,0:T(8,128)(2,1)S(1)} collective-permute-done((bf16[3,224,512]{2,1,0:T(8,128)(2,1)S(1)}, bf16[3,224,512]{2,1,0:T(8,128)(2,1)S(1)}, u32[]{:S(2)}, u32[]{:S(2)}) %collective-permute-start.3) | collective-permute-done | bytes 688160 | tf_op jit(solution)/shard_map/ppermute | solution.py:410
  84.4 3.7 %collective-permute-start.4 = (bf16[3,224,512]{2,1,0:T(8,128)(2,1)S(1)}, bf16[3,224,512]{2,1,0:T(8,128)(2,1)S(1)}, u32[]{:S(2)}, u32[]{:S(2)}) collective-permute-start(bf16[3,224,512]{2,1,0:T(8,128)(2,1)S(1)} %collective-permute-done.3.refs_3_), channel_id=1, source_target_pairs={{0,96},{32,0},{64,32},{96,64},{1,97},{33,1},{65,33},{97,65},{2,98}... | collective-permute-start | bytes 2064392 | tf_op jit(solution)/shard_map/ppermute | solution.py:410
  88.1 0.2 collective-permute-done.1.refs_2_
  88.3 14.7 %collective-permute-done.6.refs_4_ = bf16[3,224,512]{2,1,0:T(8,128)(2,1)S(1)} collective-permute-done((bf16[3,224,512]{2,1,0:T(8,128)(2,1)S(1)}, bf16[3,224,512]{2,1,0:T(8,128)(2,1)S(1)}, u32[]{:S(2)}, u32[]{:S(2)}) %collective-permute-start.6) | collective-permute-done | bytes 688160 | tf_op jit(solution)/shard_map/ppermute | solution.py:410
  103.0 0.9 copy-done.12
  103.9 0.8 copy-done.13
  104.7 1.6 copy-done.1
  106.3 12.4 %shard_map.103 = (f32[3,896,512]{2,1,0:T(8,128)}, f32[2,512,512]{2,1,0:T(8,128)}, f32[2,8,512]{2,1,0:T(8,128)S(1)}) custom-call(bf16[32,64,512]{2,1,0:T(8,128)(2,1)S(1)} %copy-done.1, bf16[3,224,512]{2,1,0:T(8,128)(2,1)} %copy-done.13, bf16[3,224,512]{2,1,0:T(8,128)(2,1)} %copy-done.11, bf16[3,224,512]{2,1,0:T(8,128)(2,1)} %copy-done.10, ...), custom_call_target="tpu_custom_call" | custom-call | tf_op jit(solution)/shard_map/pallas_call | solution.py:266
  118.8 0.8 copy-done.14
  119.6 0.2 copy-done.15
  119.8 14.8 %shard_map.104 = (f32[3,896,512]{2,1,0:T(8,128)}, bf16[32,32,512]{2,1,0:T(8,128)(2,1)}, f32[2,8,512]{2,1,0:T(8,128)S(1)}) custom-call(bf16[32,64,512]{2,1,0:T(8,128)(2,1)S(1)} %copy-done.1, bf16[3,224,512]{2,1,0:T(8,128)(2,1)} %copy-done.15, bf16[3,224,512]{2,1,0:T(8,128)(2,1)} %copy-done.14, bf16[3,224,512]{2,1,0:T(8,128)(2,1)} %collective-permute-done.refs_3_.refs_1_, ...), custom_call_target="tpu_custom_call" | custom-call | tf_op jit(solution)/shard_map/pallas_call | solution.py:266
  134.6 8.8 %shard_map.106 = (bf16[3,224,512]{2,1,0:T(8,128)(2,1)}, bf16[3,224,512]{2,1,0:T(8,128)(2,1)}, f32[2,512,512]{2,1,0:T(8,128)}, f32[2,8,512]{2,1,0:T(8,128)S(1)}) custom-call(bf16[32,64,512]{2,1,0:T(8,128)(2,1)S(1)} %all-to-all-done.2.refs_0_, bf16[3,224,512]{2,1,0:T(8,128)(2,1)} %copy-done.15, bf16[3,224,512]{2,1,0:T(8,128)(2,1)} %copy-done.14, ...), custom_call_target="tpu_custom_call" | custom-call | tf_op jit(solution)/shard_map/pallas_call | solution.py:266
  143.4 0.1 collective-permute-start.7
  143.5 7.4 %all-to-all-start.1 = ((bf16[32,32,512]{2,1,0:T(8,128)(2,1)}), bf16[32,32,512]{2,1,0:T(8,128)(2,1)S(1)}, u32[]{:S(2)}, u32[]{:S(2)}) async-start(bf16[32,32,512]{2,1,0:T(8,128)(2,1)} %get-tuple-element.31), calls=%async_computation.1 | async-start | bytes 2097152 | tf_op jit(solution)/shard_map/all_to_all | solution.py:418
  151.0 3.3 %collective-permute-start.12 = (bf16[3,224,512]{2,1,0:T(8,128)(2,1)}, bf16[3,224,512]{2,1,0:T(8,128)(2,1)}, u32[]{:S(2)}, u32[]{:S(2)}) collective-permute-start(bf16[3,224,512]{2,1,0:T(8,128)(2,1)} %get-tuple-element.49), channel_id=1, source_target_pairs={{0,96},{32,0},{64,32},{96,64},{1,97},{33,1},{65,33},{97,65},{2,98}... | collective-permute-start | bytes 2064392 | tf_op jit(solution)/shard_map/ppermute | solution.py:410
  154.2 14.8 %shard_map.107 = (bf16[3,224,512]{2,1,0:T(8,128)(2,1)}, bf16[3,224,512]{2,1,0:T(8,128)(2,1)}, bf16[3,224,512]{2,1,0:T(8,128)(2,1)}, bf16[3,224,512]{2,1,0:T(8,12...) custom-call(bf16[32,64,512]{2,1,0:T(8,128)(2,1)S(1)} %all-to-all-done.2.refs_0_, ...), custom_call_target="tpu_custom_call" | custom-call | tf_op jit(solution)/shard_map/pallas_call | solution.py:266
  169.1 0.3 collective-permute-start.9
  169.4 2.4 add_convert_fusion.2
  171.8 2.0 collective-permute-start.8
  173.8 9.2 %shard_map.108 = (bf16[3,224,512]{2,1,0:T(8,128)(2,1)}, bf16[3,224,512]{2,1,0:T(8,128)(2,1)}, bf16[32,40,512]{2,1,0:T(8,128)(2,1)}) custom-call(bf16[32,64,512]{2,1,0:T(8,128)(2,1)S(1)} %all-to-all-done.2.refs_0_, bf16[3,224,512]{2,1,0:T(8,128)(2,1)} %collective-permute-done.refs_3_.refs_1_, bf16[3,224,512]{2,1,0:T(8,128)(2,1)} %copy-done.9, ...), custom_call_target="tpu_custom_call" | custom-call | tf_op jit(solution)/shard_map/pallas_call | solution.py:266
  183.0 1.0 copy-done.2
  183.9 7.4 %all-to-all-start.3 = ((bf16[32,40,512]{2,1,0:T(8,128)(2,1)}), bf16[32,40,512]{2,1,0:T(8,128)(2,1)S(1)}, u32[]{:S(2)}, u32[]{:S(2)}) async-start(bf16[32,40,512]{2,1,0:T(8,128)(2,1)} %get-tuple-element.39), calls=%async_computation.3 | async-start | bytes 2621440 | tf_op jit(solution)/shard_map/all_to_all | solution.py:418
  191.5 2.2 add_convert_fusion
  193.7 3.1 %collective-permute-start.13 = (bf16[3,224,512]{2,1,0:T(8,128)(2,1)}, bf16[3,224,512]{2,1,0:T(8,128)(2,1)}, u32[]{:S(2)}, u32[]{:S(2)}) collective-permute-start(bf16[3,224,512]{2,1,0:T(8,128)(2,1)} %add_convert_fusion), channel_id=1, source_target_pairs={{0,96},{32,0},{64,32},{96,64},{1,97},{33,1},{65,33},{97,65},{2,98}... | collective-permute-start | bytes 2064392 | tf_op jit(solution)/shard_map/ppermute | solution.py:410
  196.9 2.5 %add_convert_fusion.1 = bf16[3,224,512]{2,1,0:T(8,128)(2,1)} fusion(bf16[3,224,512]{2,1,0:T(8,128)(2,1)} %collective-permute-done.9, bf16[3,224,512]{2,1,0:T(8,128)(2,1)} %collective-permute-done.8, bf16[3,224,512]{2,1,0:T(8,128)(2,1)S(1)} %copy-done.17), kind=kLoop, calls=%fused_computation.3 | loop fusion | flops 2064384 | bytes 2752512 | tf_op jit(solution)/shard_map/convert_element_type | solution.py:422
  199.4 3.3 %collective-permute-start.10 = (bf16[3,224,512]{2,1,0:T(8,128)(2,1)}, bf16[3,224,512]{2,1,0:T(8,128)(2,1)}, u32[]{:S(2)}, u32[]{:S(2)}) collective-permute-start(bf16[3,224,512]{2,1,0:T(8,128)(2,1)} %add_convert_fusion.1), channel_id=1, source_target_pairs={{0,16},{16,0},{1,17},{17,1},{2,18},{18,2},{3,19},{19,3},{4,20},{20... | collective-permute-start | bytes 2064392 | tf_op jit(solution)/shard_map/ppermute | solution.py:414
  202.7 1.5 combine_first.1.part
  204.2 6.5 %all-to-all-done.3.back = bf16[32,40,512]{2,1,0:T(8,128)(2,1)S(1)} async-done(((bf16[32,40,512]{2,1,0:T(8,128)(2,1)}), bf16[32,40,512]{2,1,0:T(8,128)(2,1)S(1)}, u32[]{:S(2)}, u32[]{:S(2)}) %all-to-all-start.3) | async-done | bytes 1310752 | tf_op jit(solution)/shard_map/all_to_all | solution.py:418
  210.7 3.7 %combine_last.1 = (bf16[128,4096]{1,0:T(8,128)(2,1)}, f32[8,1024]{1,0:T(8,128)S(1)}) custom-call(f32[8,1024]{1,0:T(8,128)S(1)} %maximum_bitcast_fusion.table, f32[1024,512]{1,0:T(8,128)S(1)} %combine_first.1.part, bf16[32,40,512]{2,1,0:T(8,128)(2,1)S(1)} %all-to-all-done.3.back), custom_call_target="tpu_custom_call" | custom-call | tf_op jit(solution)/shard_map/combine_last/pallas_call | solution.py:347
  214.4 0.6 slice_bitcast_fusion
  215.1 2.4 final_own.1
  217.5 7.1 %collective-permute-done.10.other = bf16[3,224,512]{2,1,0:T(8,128)(2,1)} collective-permute-done((bf16[3,224,512]{2,1,0:T(8,128)(2,1)}, bf16[3,224,512]{2,1,0:T(8,128)(2,1)}, u32[]{:S(2)}, u32[]{:S(2)}) %collective-permute-start.10) | collective-permute-done | bytes 688160 | tf_op jit(solution)/shard_map/ppermute | solution.py:414
  224.6 22.0 %final_other.1 = (bf16[2,2,224,512]{3,2,1,0:T(8,128)(2,1)}, bf16[2,224,512]{2,1,0:T(8,128)(2,1)}) custom-call(s32[1]{0:T(128)} %bitcast.8.which, bf16[3,224,512]{2,1,0:T(8,128)(2,1)} %collective-permute-done.10.other, bf16[2,2,224,512]{3,2,1,0:T(8,128)(2,1)} %get-tuple-element.50._in, ...), custom_call_target="tpu_custom_call", output_to_operand_aliasing={{0}: (2, {}), {1}: (3, {})} | custom-call | tf_op jit(solution)/shard_map/final_other/pallas_call | solution.py:397
  (46 shorter events, 0.2 us)
Async XLA Ops:
  2.2 1.2 copy-start.4
  3.4 1.2 copy-start.6
  8.5 8.6 %copy-start.18 = (bf16[2,224,512]{2,1,0:T(8,128)(2,1)S(1)}, bf16[2,224,512]{2,1,0:T(8,128)(2,1)}, u32[]{:S(2)}) copy-start(bf16[2,224,512]{2,1,0:T(8,128)(2,1)} %param.13) | copy-start | bytes 1376260
  8.5 36.3 %all-to-all-start = ((bf16[32,64,512]{2,1,0:T(8,128)(2,1)}), bf16[32,64,512]{2,1,0:T(8,128)(2,1)S(1)}, u32[]{:S(2)}, u32[]{:S(2)}) async-start(bf16[32,64,512]{2,1,0:T(8,128)(2,1)} %shard_map.102), calls=%async_computation | async-start | bytes 4194304 | tf_op jit(solution)/shard_map/all_to_all | solution.py:418
  17.1 5.8 %copy-start.5 = (bf16[128,4096]{1,0:T(8,128)(2,1)S(1)}, bf16[128,4096]{1,0:T(8,128)(2,1)}, u32[]{:S(2)}) copy-start(bf16[128,4096]{1,0:T(8,128)(2,1)} %tok.3) | copy-start | bytes 3145732
  17.1 5.8 %copy-start.7 = (bf16[128,4096]{1,0:T(8,128)(2,1)S(1)}, bf16[128,4096]{1,0:T(8,128)(2,1)}, u32[]{:S(2)}) copy-start(bf16[128,4096]{1,0:T(8,128)(2,1)} %cot.3) | copy-start | bytes 3145732
  19.5 49.0 %copy-start.9 = (bf16[3,224,512]{2,1,0:T(8,128)(2,1)}, bf16[3,224,512]{2,1,0:T(8,128)(2,1)S(1)}, u32[]{:S(2)}) copy-start(bf16[3,224,512]{2,1,0:T(8,128)(2,1)S(1)} %get-tuple-element.56.refs_4_.refs_2_) | copy-start | bytes 2064388
  19.5 49.0 %collective-permute-start = (bf16[3,224,512]{2,1,0:T(8,128)(2,1)}, bf16[3,224,512]{2,1,0:T(8,128)(2,1)}, u32[]{:S(2)}, u32[]{:S(2)}) collective-permute-start(bf16[3,224,512]{2,1,0:T(8,128)(2,1)} %get-tuple-element.57), channel_id=1, source_target_pairs={{0,16},{16,0},{1,17},{17,1},{2,18},{18,2},{3,19},{19,3},{4,20},{20... | collective-permute-start | bytes 2064392 | tf_op jit(solution)/shard_map/ppermute | solution.py:414
  44.8 1.3 copy-start
  46.2 88.5 %all-to-all-start.2 = ((bf16[32,64,512]{2,1,0:T(8,128)(2,1)}), bf16[32,64,512]{2,1,0:T(8,128)(2,1)S(1)}, u32[]{:S(2)}, u32[]{:S(2)}) async-start(bf16[32,64,512]{2,1,0:T(8,128)(2,1)} %shard_map.105), calls=%async_computation.2 | async-start | bytes 4194304 | tf_op jit(solution)/shard_map/all_to_all | solution.py:418
  65.7 18.6 %collective-permute-start.3 = (bf16[3,224,512]{2,1,0:T(8,128)(2,1)S(1)}, bf16[3,224,512]{2,1,0:T(8,128)(2,1)S(1)}, u32[]{:S(2)}, u32[]{:S(2)}) collective-permute-start(bf16[3,224,512]{2,1,0:T(8,128)(2,1)S(1)} %get-tuple-element.56.refs_4_.refs_2_), channel_id=1, source_target_pairs={{0,96},{32,0},{64,32},{96,64},{1,97},{33,1},{65,33},{97,65},{2,98}... | collective-permute-start | bytes 2064392 | tf_op jit(solution)/shard_map/ppermute | solution.py:410
  68.6 19.7 %collective-permute-start.1 = (bf16[3,224,512]{2,1,0:T(8,128)(2,1)}, bf16[3,224,512]{2,1,0:T(8,128)(2,1)S(1)}, u32[]{:S(2)}, u32[]{:S(2)}) collective-permute-start(bf16[3,224,512]{2,1,0:T(8,128)(2,1)} %collective-permute-done.refs_3_.refs_1_), channel_id=1, source_target_pairs={{0,32},{32,64},{64,96},{96,0},{1,33},{33,65},{65,97},{97,1},{2,34}... | collective-permute-start | bytes 2064392 | tf_op jit(solution)/shard_map/ppermute | solution.py:410
  68.6 34.5 %collective-permute-start.6 = (bf16[3,224,512]{2,1,0:T(8,128)(2,1)S(1)}, bf16[3,224,512]{2,1,0:T(8,128)(2,1)S(1)}, u32[]{:S(2)}, u32[]{:S(2)}) collective-permute-start(bf16[3,224,512]{2,1,0:T(8,128)(2,1)S(1)} %get-tuple-element.56.refs_4_.refs_2_), channel_id=1, source_target_pairs={{0,32},{32,64},{64,96},{96,0},{1,33},{33,65},{65,97},{97,1},{2,34}... | collective-permute-start | bytes 2064392 | tf_op jit(solution)/shard_map/ppermute | solution.py:410
  69.3 33.7 %collective-permute-start.5 = (bf16[3,224,512]{2,1,0:T(8,128)(2,1)}, bf16[3,224,512]{2,1,0:T(8,128)(2,1)S(1)}, u32[]{:S(2)}, u32[]{:S(2)}) collective-permute-start(bf16[3,224,512]{2,1,0:T(8,128)(2,1)} %collective-permute-done.refs_3_.refs_1_), channel_id=1, source_target_pairs={{0,96},{32,0},{64,32},{96,64},{1,97},{33,1},{65,33},{97,65},{2,98}... | collective-permute-start | bytes 2064392 | tf_op jit(solution)/shard_map/ppermute | solution.py:410
  84.4 18.7 %copy-start.10 = (bf16[3,224,512]{2,1,0:T(8,128)(2,1)}, bf16[3,224,512]{2,1,0:T(8,128)(2,1)S(1)}, u32[]{:S(2)}) copy-start(bf16[3,224,512]{2,1,0:T(8,128)(2,1)S(1)} %collective-permute-done.3.refs_3_) | copy-start | bytes 2064388
  84.4 34.4 %collective-permute-start.4 = (bf16[3,224,512]{2,1,0:T(8,128)(2,1)S(1)}, bf16[3,224,512]{2,1,0:T(8,128)(2,1)S(1)}, u32[]{:S(2)}, u32[]{:S(2)}) collective-permute-start(bf16[3,224,512]{2,1,0:T(8,128)(2,1)S(1)} %collective-permute-done.3.refs_3_), channel_id=1, source_target_pairs={{0,96},{32,0},{64,32},{96,64},{1,97},{33,1},{65,33},{97,65},{2,98}... | collective-permute-start | bytes 2064392 | tf_op jit(solution)/shard_map/ppermute | solution.py:410
  88.3 14.8 %copy-start.11 = (bf16[3,224,512]{2,1,0:T(8,128)(2,1)}, bf16[3,224,512]{2,1,0:T(8,128)(2,1)S(1)}, u32[]{:S(2)}) copy-start(bf16[3,224,512]{2,1,0:T(8,128)(2,1)S(1)} %collective-permute-done.1.refs_2_) | copy-start | bytes 2064388
  88.3 30.5 %collective-permute-start.2 = (bf16[3,224,512]{2,1,0:T(8,128)(2,1)S(1)}, bf16[3,224,512]{2,1,0:T(8,128)(2,1)S(1)}, u32[]{:S(2)}, u32[]{:S(2)}) collective-permute-start(bf16[3,224,512]{2,1,0:T(8,128)(2,1)S(1)} %collective-permute-done.1.refs_2_), channel_id=1, source_target_pairs={{0,32},{32,64},{64,96},{96,0},{1,33},{33,65},{65,97},{97,1},{2,34}... | collective-permute-start | bytes 2064392 | tf_op jit(solution)/shard_map/ppermute | solution.py:410
  103.0 0.9 copy-start.12
  103.9 0.8 copy-start.13
  104.7 1.6 copy-start.1
  118.8 0.9 copy-start.14
  118.8 1.1 copy-start.15
  143.4 26.0 %collective-permute-start.7 = (bf16[3,224,512]{2,1,0:T(8,128)(2,1)}, bf16[3,224,512]{2,1,0:T(8,128)(2,1)}, u32[]{:S(2)}, u32[]{:S(2)}) collective-permute-start(bf16[3,224,512]{2,1,0:T(8,128)(2,1)} %get-tuple-element.44), channel_id=1, source_target_pairs={{0,32},{32,64},{64,96},{96,0},{1,33},{33,65},{65,97},{97,1},{2,34}... | collective-permute-start | bytes 2064392 | tf_op jit(solution)/shard_map/ppermute | solution.py:410
  143.5 39.4 %all-to-all-start.1 = ((bf16[32,32,512]{2,1,0:T(8,128)(2,1)}), bf16[32,32,512]{2,1,0:T(8,128)(2,1)S(1)}, u32[]{:S(2)}, u32[]{:S(2)}) async-start(bf16[32,32,512]{2,1,0:T(8,128)(2,1)} %get-tuple-element.31), calls=%async_computation.1 | async-start | bytes 2097152 | tf_op jit(solution)/shard_map/all_to_all | solution.py:418
  151.0 40.5 %collective-permute-start.12 = (bf16[3,224,512]{2,1,0:T(8,128)(2,1)}, bf16[3,224,512]{2,1,0:T(8,128)(2,1)}, u32[]{:S(2)}, u32[]{:S(2)}) collective-permute-start(bf16[3,224,512]{2,1,0:T(8,128)(2,1)} %get-tuple-element.49), channel_id=1, source_target_pairs={{0,96},{32,0},{64,32},{96,64},{1,97},{33,1},{65,33},{97,65},{2,98}... | collective-permute-start | bytes 2064392 | tf_op jit(solution)/shard_map/ppermute | solution.py:410
  169.1 27.8 %collective-permute-start.9 = (bf16[3,224,512]{2,1,0:T(8,128)(2,1)}, bf16[3,224,512]{2,1,0:T(8,128)(2,1)}, u32[]{:S(2)}, u32[]{:S(2)}) collective-permute-start(bf16[3,224,512]{2,1,0:T(8,128)(2,1)} %get-tuple-element.45), channel_id=1, source_target_pairs={{0,96},{32,0},{64,32},{96,64},{1,97},{33,1},{65,33},{97,65},{2,98}... | collective-permute-start | bytes 2064392 | tf_op jit(solution)/shard_map/ppermute | solution.py:410
  171.8 25.1 %collective-permute-start.8 = (bf16[3,224,512]{2,1,0:T(8,128)(2,1)}, bf16[3,224,512]{2,1,0:T(8,128)(2,1)}, u32[]{:S(2)}, u32[]{:S(2)}) collective-permute-start(bf16[3,224,512]{2,1,0:T(8,128)(2,1)} %add_convert_fusion.2), channel_id=1, source_target_pairs={{0,32},{32,64},{64,96},{96,0},{1,33},{33,65},{65,97},{97,1},{2,34}... | collective-permute-start | bytes 2064392 | tf_op jit(solution)/shard_map/ppermute | solution.py:410
  182.9 8.5 %copy-start.16 = (bf16[3,224,512]{2,1,0:T(8,128)(2,1)S(1)}, bf16[3,224,512]{2,1,0:T(8,128)(2,1)}, u32[]{:S(2)}) copy-start(bf16[3,224,512]{2,1,0:T(8,128)(2,1)} %get-tuple-element.48) | copy-start | bytes 2064388
  183.0 1.0 copy-start.2
  183.9 26.8 %all-to-all-start.3 = ((bf16[32,40,512]{2,1,0:T(8,128)(2,1)}), bf16[32,40,512]{2,1,0:T(8,128)(2,1)S(1)}, u32[]{:S(2)}, u32[]{:S(2)}) async-start(bf16[32,40,512]{2,1,0:T(8,128)(2,1)} %get-tuple-element.39), calls=%async_computation.3 | async-start | bytes 2621440 | tf_op jit(solution)/shard_map/all_to_all | solution.py:418
  191.3 5.5 %copy-start.17 = (bf16[3,224,512]{2,1,0:T(8,128)(2,1)S(1)}, bf16[3,224,512]{2,1,0:T(8,128)(2,1)}, u32[]{:S(2)}) copy-start(bf16[3,224,512]{2,1,0:T(8,128)(2,1)} %get-tuple-element.42) | copy-start | bytes 2064388
  191.4 23.7 %collective-permute-start.11 = (bf16[3,224,512]{2,1,0:T(8,128)(2,1)}, bf16[3,224,512]{2,1,0:T(8,128)(2,1)}, u32[]{:S(2)}, u32[]{:S(2)}) collective-permute-start(bf16[3,224,512]{2,1,0:T(8,128)(2,1)} %get-tuple-element.47), channel_id=1, source_target_pairs={{0,32},{32,64},{64,96},{96,0},{1,33},{33,65},{65,97},{97,1},{2,34}... | collective-permute-start | bytes 2064392 | tf_op jit(solution)/shard_map/ppermute | solution.py:410
  193.7 21.4 %collective-permute-start.13 = (bf16[3,224,512]{2,1,0:T(8,128)(2,1)}, bf16[3,224,512]{2,1,0:T(8,128)(2,1)}, u32[]{:S(2)}, u32[]{:S(2)}) collective-permute-start(bf16[3,224,512]{2,1,0:T(8,128)(2,1)} %add_convert_fusion), channel_id=1, source_target_pairs={{0,96},{32,0},{64,32},{96,64},{1,97},{33,1},{65,33},{97,65},{2,98}... | collective-permute-start | bytes 2064392 | tf_op jit(solution)/shard_map/ppermute | solution.py:410
  196.9 5.9 %copy-start.3 = (bf16[32,32,512]{2,1,0:T(8,128)(2,1)S(1)}, bf16[32,32,512]{2,1,0:T(8,128)(2,1)}, u32[]{:S(2)}) copy-start(bf16[32,32,512]{2,1,0:T(8,128)(2,1)} %copy-done.2) | copy-start | bytes 3145732
  199.4 25.2 %collective-permute-start.10 = (bf16[3,224,512]{2,1,0:T(8,128)(2,1)}, bf16[3,224,512]{2,1,0:T(8,128)(2,1)}, u32[]{:S(2)}, u32[]{:S(2)}) collective-permute-start(bf16[3,224,512]{2,1,0:T(8,128)(2,1)} %add_convert_fusion.1), channel_id=1, source_target_pairs={{0,16},{16,0},{1,17},{17,1},{2,18},{18,2},{3,19},{19,3},{4,20},{20... | collective-permute-start | bytes 2064392 | tf_op jit(solution)/shard_map/ppermute | solution.py:414
  210.7 4.3 %copy-start.8 = (bf16[3,224,512]{2,1,0:T(8,128)(2,1)S(1)}, bf16[3,224,512]{2,1,0:T(8,128)(2,1)}, u32[]{:S(2)}) copy-start(bf16[3,224,512]{2,1,0:T(8,128)(2,1)} %get-tuple-element.46.own0) | copy-start | bytes 2064388

commit v3 on v1

--- a/solution.py
+++ b/solution.py
@@ -10,6 +10,7 @@
 
 H = 8
 DS = 512
+CAP = 64
 PEERS = 32
 SLOTS = (32, 32)
 GROUP = 8
@@ -95,7 +96,7 @@
 UNITS = 2 * SH
 
 
-def router_rows(back, slots, router_first, router):
+def router_rows(back, at, router_first, router):
     table = jnp.zeros((PEERS, 128), F32)
     for part, value in ((0, router_first), (1, router)):
         count = SLOTS[part]
@@ -108,25 +109,26 @@
         lane = lax.broadcasted_iota(jnp.int32, (total, 128), 1)
         place = jnp.where(slot == lane, 1.0, 0.0).astype(BF)
         table = table + contract(spread, place, 1, 0)
-    back[:, slots : slots + EXTRA, 0:128] = jnp.broadcast_to(
+    back[:, at : at + EXTRA, 0:128] = jnp.broadcast_to(
         table.astype(BF)[:, None, :], (PEERS, EXTRA, 128)
     )
-    back[:, slots : slots + EXTRA, 128:DS] = jnp.zeros((PEERS, EXTRA, DS - 128), BF)
+    back[:, at : at + EXTRA, 128:DS] = jnp.zeros((PEERS, EXTRA, DS - 128), BF)
 
 
 def expert_kernel(*refs, part, end):
     slots = SLOTS[part]
+    last = part == 1 and end
     refs = list(refs)
     take = lambda n: [refs.pop(0) for _ in range(n)]
-    (z,) = take(1)
+    (z_in,) = take(1)
     weights = take(4)
     before = take(1)[0] if part else None
     acc_in, router_in = take(2) if end else (None, None)
-    router_first = take(1)[0] if part and end else None
+    router_first = take(2)[0] if last else None
     outs = take(4 if part else 1)
     (dx_out,) = take(1)
-    router_out = None if part and end else take(1)[0]
-    acc, wbuf, stage, obuf, asem, wsem, bsem, ssem = refs
+    router_out = None if last else take(1)[0]
+    z, acc, wbuf, stage, obuf, dbuf, zsem, asem, wsem, bsem, ssem = refs
 
     def units(p):
         return pl.ds(pl.multiple_of(p * UNITS, UNITS), UNITS)
@@ -148,6 +150,8 @@
             obuf.at[p, :, half * SH : (half + 1) * SH, :], outs[2 * p + half], ssem.at[p, half]
         )
 
+    z_load = pltpu.make_async_copy(z_in, z, zsem)
+    z_load.start()
     for k in range(4):
         fetch(k, k // 2).start()
     if part:
@@ -159,6 +163,7 @@
     else:
         acc[...] = jnp.zeros_like(acc)
     router = jnp.zeros((8, PEERS * slots), F32) if not end else router_in[...]
+    z_load.wait()
 
     def block(p, router):
         fetch(0, p).wait()
@@ -189,13 +194,15 @@
 
     router = lax.fori_loop(0, 2, block, router)
     if end:
-        dx_out[:, 0:slots, :] = acc[...].astype(BF).reshape(PEERS, slots, DS)
+        dbuf[:, 0:slots, :] = acc[...].astype(BF).reshape(PEERS, slots, DS)
+        if last:
+            router_rows(dbuf, slots, router_first[...], router)
+        here = pl.ds(part * SLOTS[0], slots + part * EXTRA)
+        save = pltpu.make_async_copy(dbuf, dx_out.at[:, here, :], asem)
     else:
-        acc_save = pltpu.make_async_copy(acc, dx_out, asem)
-        acc_save.start()
-    if router_out is None:
-        router_rows(dx_out, slots, router_first[...], router)
-    else:
+        save = pltpu.make_async_copy(acc, dx_out, asem)
+    save.start()
+    if not last:
         router_out[...] = router
     for p in range(2):
         if part:
@@ -203,38 +210,35 @@
             store(p, 1).wait()
         else:
             store_wide(p).wait()
-    if not end:
-        acc_save.wait()
-
-
-def expert_part(part, z, weights, before=None, carry=None, router_first=None):
+    save.wait()
+
+
+def expert_part(part, z, weights, before=None, carry=None, first=None):
     end = carry is not None
+    last = part == 1 and end
     slots = SLOTS[part]
     rows = PEERS * slots
-    args = [z, *[in_hbm(w) for w in weights]]
-    in_specs = [WHOLE] + [HBM] * 4
+    args = [z if part else in_hbm(z), *[in_hbm(w) for w in weights]]
+    in_specs = [pl.BlockSpec(memory_space=pl.ANY) if part else HBM] + [HBM] * 4
     if part:
         args += [in_hbm(before)]
         in_specs += [HBM]
     if end:
         args += [in_hbm(carry[0]), carry[1]]
         in_specs += [HBM, WHOLE]
-    if part and end:
-        args += [router_first]
-        in_specs += [WHOLE]
+    if last:
+        args += [first[1], in_hbm(first[0])]
+        in_specs += [WHOLE, HBM]
     if part:
         out_shape = [pltpu.HBM((3, SH, DS), BF)] * 4
-        out_specs = [HBM] * 4
     else:
         out_shape = [pltpu.HBM((3, 4 * SH, DS), F32)]
-        out_specs = [HBM]
     if end:
-        out_shape += [pltpu.HBM((PEERS, slots + part * EXTRA, DS), BF)]
-        out_specs += [WHOLE]
+        out_shape += [pltpu.HBM((PEERS, CAP + EXTRA, DS), BF)]
     else:
         out_shape += [pltpu.HBM((rows, DS), F32)]
-        out_specs += [HBM]
-    if not (part and end):
+    out_specs = [HBM] * len(out_shape)
+    if not last:
         out_shape += [jax.ShapeDtypeStruct((8, rows), F32)]
         out_specs += [WHOLE]
     return pl.pallas_call(
@@ -242,11 +246,15 @@
         in_specs=in_specs,
         out_specs=out_specs,
         out_shape=out_shape,
+        input_output_aliases={len(args) - 1: 4} if last else {},
         scratch_shapes=[
+            pltpu.VMEM((PEERS, 2 * slots, DS), BF),
             pltpu.VMEM((rows, DS), F32),
             pltpu.VMEM((2, 3, UNITS, DS), BF),
             pltpu.VMEM((2, 3, UNITS, DS), F32),
             pltpu.VMEM((2, 3, UNITS, DS) if part else (8, 128), BF),
+            pltpu.VMEM((PEERS, slots + part * EXTRA, DS) if end else (8, 128), BF),
+            pltpu.SemaphoreType.DMA,
             pltpu.SemaphoreType.DMA,
             pltpu.SemaphoreType.DMA((2, 2)),
             pltpu.SemaphoreType.DMA((2,)),
@@ -269,28 +277,21 @@
     return (whole(0), whole(1)), (cols[:, 2:3], cols[:, 3:4]), (whole(4), whole(5)), (whole(6), whole(7))
 
 
-def combine_first_kernel(table, back, out):
-    codes = columns(table)[0]
-    rows = back[...].reshape(PEERS * SLOTS[0], DS)
-    count = 256
-    for b in range(SUBS // count):
-        out[b * count : (b + 1) * count, :] = contract(
-            picks(codes, 0, b * count, count), rows, 1, 0
-        )
-
-
-def combine_last_kernel(table, part, back, out, probs):
+def combine_kernel(table, back, out, probs):
     codes, weight, peer, slot = columns(table)
-    rows = back[:, 0 : SLOTS[1], :].reshape(PEERS * SLOTS[1], DS)
+    rows = [
+        back[:, 0 : SLOTS[0], :].reshape(PEERS * SLOTS[0], DS),
+        back[:, SLOTS[0] : CAP, :].reshape(PEERS * SLOTS[1], DS),
+    ]
     count = 256
     n = count // 128
     for b in range(SUBS // count):
-        got = contract(picks(codes, 1, b * count, count), rows, 1, 0)
-        got = (got + part[b * count : (b + 1) * count, :]).astype(BF)
+        got = contract(picks(codes, 0, b * count, count), rows[0], 1, 0)
+        got = (got + contract(picks(codes, 1, b * count, count), rows[1], 1, 0)).astype(BF)
         for k in range(n):
             h = b * n + k
             out[:, h * DS : (h + 1) * DS] = got[k * 128 : (k + 1) * 128]
-    routers = back[:, SLOTS[1] : SLOTS[1] + EXTRA, 0:128].reshape(PEERS * EXTRA, 128)
+    routers = back[:, CAP : CAP + EXTRA, 0:128].reshape(PEERS * EXTRA, 128)
     source = lax.broadcasted_iota(jnp.int32, (SUBS, PEERS * EXTRA), 1)
     lane = lax.broadcasted_iota(jnp.int32, (SUBS, 128), 1)
     found = []
@@ -303,53 +304,62 @@
     probs[...] = jnp.transpose(both)[0:8, :]
 
 
-def combine_first(table, back):
+def combine(table, back):
     return pl.pallas_call(
-        combine_first_kernel,
-        out_shape=jax.ShapeDtypeStruct((SUBS, DS), F32),
-        compiler_params=params(),
-        name="combine_first",
-    )(table, back)
-
-
-def combine_last(table, part, back):
-    return pl.pallas_call(
-        combine_last_kernel,
+        combine_kernel,
         out_shape=[
             jax.ShapeDtypeStruct((SUBS // H, H * DS), BF),
             jax.ShapeDtypeStruct((8, SUBS), F32),
         ],
         compiler_params=params(),
-        name="combine_last",
-    )(table, part, back)
-
-
-def final_kernel(which, own0, own1, own2, other, grad_in, grad_out):
-    a = which[0]
-    b = 1 - a
+        name="combine",
+    )(table, back)
+
+
+def place(source, grad_in, grad_out, at, sems):
+    copies = (
+        pltpu.make_async_copy(source.at[0:2], grad_in.at[at], sems.at[0]),
+        pltpu.make_async_copy(source.at[2], grad_out.at[at], sems.at[1]),
+    )
+    for c in copies:
+        c.start()
+    for c in copies:
+        c.wait()
+
+
+def final_own_kernel(which, own0, own1, own2, grad_in, grad_out, total, sems):
     for k in range(3):
-        total = own0[k].astype(F32) + own1[k].astype(F32) + own2[k].astype(F32)
-        total = total.astype(BF)
-        if k < 2:
-            grad_in[a, k] = total
-            grad_in[b, k] = other[k]
-        else:
-            grad_out[a] = total
-            grad_out[b] = other[k]
+        value = own0[k].astype(F32) + own1[k].astype(F32) + own2[k].astype(F32)
+        total[k] = value.astype(BF)
+    place(total, grad_in, grad_out, which[0], sems)
+
+
+def final_other_kernel(which, other, _in, _out, grad_in, grad_out, sems):
+    place(other, grad_in, grad_out, 1 - which[0], sems)
 
 
 def final(which, own, other):
-    vmem = pl.BlockSpec(memory_space=pltpu.VMEM)
+    smem = pl.BlockSpec(memory_space=pltpu.SMEM)
+    out_shape = [pltpu.HBM((2, 2, SH, DS), BF), pltpu.HBM((2, SH, DS), BF)]
+    grads = pl.pallas_call(
+        final_own_kernel,
+        in_specs=[smem] + [WHOLE] * 3,
+        out_specs=[HBM, HBM],
+        out_shape=out_shape,
+        scratch_shapes=[pltpu.VMEM((3, SH, DS), BF), pltpu.SemaphoreType.DMA((2,))],
+        compiler_params=params(),
+        name="final_own",
+    )(which, *own)
     return pl.pallas_call(
-        final_kernel,
-        in_specs=[pl.BlockSpec(memory_space=pltpu.SMEM)] + [vmem] * 4,
-        out_shape=[
-            jax.ShapeDtypeStruct((2, 2, SH, DS), BF),
-            jax.ShapeDtypeStruct((2, SH, DS), BF),
-        ],
+        final_other_kernel,
+        in_specs=[smem, WHOLE, HBM, HBM],
+        out_specs=[HBM, HBM],
+        out_shape=out_shape,
+        input_output_aliases={2: 0, 3: 1},
+        scratch_shapes=[pltpu.SemaphoreType.DMA((2,))],
         compiler_params=params(),
-        name="final",
-    )(which, *own, other)
+        name="final_other",
+    )(which, other, *[in_hbm(g) for g in grads])
 
 
 def ring(a, step):
@@ -371,9 +381,8 @@
 def layer(tokens, cotangent, expert_ids, slot_ids, route_probs, weights_in, weights_out):
     yh = lax.axis_index("yh")
     both = jnp.concatenate([weights_in, weights_out[:, None]], axis=1)
-    theirs = jnp.where(yh == 0, both[1], both[0])
+    w_p = swap(jnp.where(yh == 0, both[1], both[0]))
     w_o = jnp.where(yh == 0, both[0], both[1])
-    w_p = swap(theirs)
     w_o_m = ring(w_o, 1)
     w_o_p = ring(w_o, -1)
     w_p_m = ring(w_p, 1)
@@ -394,25 +403,23 @@
     z1 = exchange(dispatch(table, tokens, cotangent, 0))
     z2 = exchange(dispatch(table, tokens, cotangent, 1))
 
-    w_p = [w_p_2, w_p_p, w_p_m, w_p]
-    w_o = [w_o_2, w_o_p, w_o_m, w_o]
-    dw_p, *carry = expert_part(0, z1, w_p)
-    dw_o, back1, router1 = expert_part(0, z1, w_o, carry=carry)
-    back1 = exchange(back1)
-    p_2, p_p, p_m, p_0, *carry = expert_part(1, z2, w_p, dw_p)
+    far = [w_p_2, w_o_2, w_p_p, w_p_m]
+    rest = [w_o_p, w_o_m, w_p, w_o]
+    dw_rest, *carry = expert_part(0, z1, rest)
+    dw_far, *first = expert_part(0, z1, far, carry=carry)
+    p_2, o_2, p_p, p_m, *carry = expert_part(1, z2, far, dw_far)
     p_2 = ring(p_2, 1)
+    o_2 = ring(o_2, -1)
     p_m = ring(p_m, -1)
-    o_2, o_p, o_m, o_0, back2 = expert_part(1, z2, w_o, dw_o, carry, router1)
-    back2 = exchange(back2)
-    o_2 = ring(o_2, -1)
+    o_p, o_m, p_0, o_0, back = expert_part(1, z2, rest, dw_rest, carry, first)
+    back = exchange(back)
     p_p = ring(add(p_p, p_2), 1)
+    o_m = ring(add(o_m, o_2), -1)
     o_p = ring(o_p, 1)
-    o_m = ring(add(o_m, o_2), -1)
     other = swap(add(p_0, p_p, p_m))
     grad_in, grad_out = final(yh.astype(jnp.int32).reshape(1), (o_0, o_p, o_m), other)
 
-    part = combine_first(table, back1)
-    grad_tokens, probs = combine_last(table, part, back2)
+    grad_tokens, probs = combine(table, back)
     grad_probs = jnp.transpose(probs[0:2].reshape(2, H, SUBS // H), (2, 1, 0))
     return grad_tokens, grad_probs, grad_in, grad_out
 

time: 223 us -> 223 us (level)
  waiting for transfers between devices: 69.8 us -> 82.6 us
  starting transfers between devices: 67.4 us -> 61.6 us
  other arithmetic: 11 us -> 5.72 us
  Pallas kernels: 68.7 us -> 65 us
    ppermute x12, waiting for transfers between devices: 45.3 us -> 61.5 us  [ring(): return lax.ppermute(a, 'x', [(i, (i + step) % 4) for i in range(4)])]
    all_to_all x4 -> x3, starting transfers between devices: 42.9 us -> 35.7 us  [exchange(): return lax.all_to_all(a, PLANE, 0, 0, tiled=True)]
    convert_element_type x3, other arithmetic: 7.03 us -> 1.74 us  [add(): return sum((a.astype(F32) for a in arrays)).astype(BF)]
    ppermute x2, waiting for transfers between devices: 6.4 us -> 2.89 us  [swap(): return lax.ppermute(a, 'yh', [(0, 1), (1, 0)])]
    pallas_call x4, Pallas kernels: 53 us -> 50.6 us  [expert_part(): pl.pallas_call(functools.partial(expert_kernel, part=part, end=end), in_s...]
    unnamed x28 -> x38, local copies, waits for them, and re-layouts: 3.34 us -> 5.51 us
    all_to_all x4 -> x3, waiting for transfers between devices: 18.1 us -> 18.2 us  [exchange(): return lax.all_to_all(a, PLANE, 0, 0, tiled=True)]
  transfers between devices with their start and end apart: 18 -> 17, of which waited for: 8 -> 9; matrix products, arithmetic and copies ran while one was open for 5% -> 2% of each run, Pallas kernels for 28% -> 20%
where the time goes in v3:
time: 223 us; the launch traced here: 222 us
  waiting for transfers between devices  82.6 us (37%)
  Pallas kernels  65 us (29%)
  starting transfers between devices  61.6 us (28%)
  local copies, waits for them, and re-layouts  6.13 us (3%)
  other arithmetic  5.72 us (3%)
    ppermute x12, waiting for transfers between devices, ring(): return lax.ppermute(a, 'x', [(i, (i + step) % 4) for i in range(4)])  61.5 us
    pallas_call x4, Pallas kernels, expert_part(): pl.pallas_call(functools.partial(expert_kernel, part=part, end=end), in_s...  50.6 us
    all_to_all x3, starting transfers between devices, exchange(): return lax.all_to_all(a, PLANE, 0, 0, tiled=True)  35.7 us
    ppermute x12, starting transfers between devices, ring(): return lax.ppermute(a, 'x', [(i, (i + step) % 4) for i in range(4)])  19.2 us
    all_to_all x3, waiting for transfers between devices, exchange(): return lax.all_to_all(a, PLANE, 0, 0, tiled=True)  18.2 us
    pallas_call x2, Pallas kernels, dispatch(): pl.pallas_call(functools.partial(dispatch_kernel, part=part), grid=(PEERS...  7.63 us
    ppermute x2, starting transfers between devices, swap(): return lax.ppermute(a, 'yh', [(0, 1), (1, 0)])  6.68 us
    unnamed x38, local copies, waits for them, and re-layouts  5.51 us
  transfers between devices with their start and end apart: 17, of which 9 were waited for; matrix products, arithmetic and copies ran while one was open for 2% of the time, Pallas kernels for 20%

profile of v3, /device:TPU:0, one launch (start us, length us, event | category | flops | bytes accessed | tf_op | source)
XLA Modules:
  0.0 221.9 jit_solution(13365503910588947585)
XLA Ops:
  0.6 0.7 convert_element_type.43
  1.3 0.8 fusion.1
  2.2 1.2 copy-done
  3.4 1.2 copy-done.2
  4.6 3.8 %shard_map.103 = bf16[32,64,512]{2,1,0:T(8,128)(2,1)} custom-call(f32[8,1024]{1,0:T(8,128)S(1)} %maximum_bitcast_fusion.table, bf16[128,4096]{1,0:T(8,128)(2,1)S(1)} %copy-done, bf16[128,4096]{1,0:T(8,128)(2,1)S(1)} %copy-done.2), custom_call_target="tpu_custom_call" | custom-call | tf_op jit(solution)/shard_map/pallas_call | solution.py:60
  8.5 8.6 %all-to-all-start.1 = ((bf16[32,64,512]{2,1,0:T(8,128)(2,1)}), bf16[32,64,512]{2,1,0:T(8,128)(2,1)S(1)}, u32[]{:S(2)}, u32[]{:S(2)}) async-start(bf16[32,64,512]{2,1,0:T(8,128)(2,1)} %shard_map.103), calls=%async_computation.1 | async-start | bytes 4194304 | tf_op jit(solution)/shard_map/all_to_all | solution.py:374
  17.1 0.0 copy-start.3
  17.1 2.4 %select_bitcast_fusion = (bf16[3,224,512]{2,1,0:T(8,128)(2,1)}, bf16[3,224,512]{2,1,0:T(8,128)(2,1)S(1)}) fusion(pred[]{:T(512)S(6)} %eq.6, bf16[2,1,224,512]{3,2,1,0:T(8,128)(2,1)S(1)} %bitcast.14, bf16[2,2,224,512]{3,2,1,0:T(8,128)(2,1)} %param.12), kind=kLoop, calls=%fused_computation.7 | loop fusion | flops 1720320 | bytes 2752513 | tf_op jit(solution)/shard_map/jit(_where)/select_n | solution.py:384
  19.5 3.3 %collective-permute-start.2 = (bf16[3,224,512]{2,1,0:T(8,128)(2,1)}, bf16[3,224,512]{2,1,0:T(8,128)(2,1)S(1)}, u32[]{:S(2)}, u32[]{:S(2)}) collective-permute-start(bf16[3,224,512]{2,1,0:T(8,128)(2,1)} %get-tuple-element.52), channel_id=1, source_target_pairs={{0,16},{16,0},{1,17},{17,1},{2,18},{18,2},{3,19},{19,3},{4,20},{20... | collective-permute-start | bytes 2064392 | tf_op jit(solution)/shard_map/ppermute | solution.py:370
  22.9 3.8 %shard_map.102 = bf16[32,64,512]{2,1,0:T(8,128)(2,1)} custom-call(f32[8,1024]{1,0:T(8,128)S(1)} %maximum_bitcast_fusion.table, bf16[128,4096]{1,0:T(8,128)(2,1)S(1)} %copy-done.1, bf16[128,4096]{1,0:T(8,128)(2,1)S(1)} %copy-done.3), custom_call_target="tpu_custom_call" | custom-call | tf_op jit(solution)/shard_map/pallas_call | solution.py:60
  26.7 18.2 %all-to-all-done.1.refs_0_ = bf16[32,64,512]{2,1,0:T(8,128)(2,1)S(1)} async-done(((bf16[32,64,512]{2,1,0:T(8,128)(2,1)}), bf16[32,64,512]{2,1,0:T(8,128)(2,1)S(1)}, u32[]{:S(2)}, u32[]{:S(2)}) %all-to-all-start.1) | async-done | bytes 2097184 | tf_op jit(solution)/shard_map/all_to_all | solution.py:374
  44.8 1.3 copy-done.5
  46.1 19.6 %all-to-all-start = ((bf16[32,64,512]{2,1,0:T(8,128)(2,1)}), bf16[32,64,512]{2,1,0:T(8,128)(2,1)S(1)}, u32[]{:S(2)}, u32[]{:S(2)}) async-start(bf16[32,64,512]{2,1,0:T(8,128)(2,1)} %shard_map.102), calls=%async_computation | async-start | bytes 4194304 | tf_op jit(solution)/shard_map/all_to_all | solution.py:374
  65.7 2.8 %collective-permute-start = (bf16[3,224,512]{2,1,0:T(8,128)(2,1)S(1)}, bf16[3,224,512]{2,1,0:T(8,128)(2,1)S(1)}, u32[]{:S(2)}, u32[]{:S(2)}) collective-permute-start(bf16[3,224,512]{2,1,0:T(8,128)(2,1)S(1)} %get-tuple-element.53.refs_4_), channel_id=1, source_target_pairs={{0,96},{32,0},{64,32},{96,64},{1,97},{33,1},{65,33},{97,65},{2,98}... | collective-permute-start | bytes 2064392 | tf_op jit(solution)/shard_map/ppermute | solution.py:366
  68.6 0.8 collective-permute-start.1
  69.3 2.6 %collective-permute-start.6 = (bf16[3,224,512]{2,1,0:T(8,128)(2,1)S(1)}, bf16[3,224,512]{2,1,0:T(8,128)(2,1)S(1)}, u32[]{:S(2)}, u32[]{:S(2)}) collective-permute-start(bf16[3,224,512]{2,1,0:T(8,128)(2,1)S(1)} %collective-permute-done.2.refs_3_), channel_id=1, source_target_pairs={{0,96},{32,0},{64,32},{96,64},{1,97},{33,1},{65,33},{97,65},{2,98}... | collective-permute-start | bytes 2064392 | tf_op jit(solution)/shard_map/ppermute | solution.py:366
  71.9 12.5 %collective-permute-done.refs_1_ = bf16[3,224,512]{2,1,0:T(8,128)(2,1)S(1)} collective-permute-done((bf16[3,224,512]{2,1,0:T(8,128)(2,1)S(1)}, bf16[3,224,512]{2,1,0:T(8,128)(2,1)S(1)}, u32[]{:S(2)}, u32[]{:S(2)}) %collective-permute-start) | collective-permute-done | bytes 688160 | tf_op jit(solution)/shard_map/ppermute | solution.py:366
  84.4 3.7 %collective-permute-start.5 = (bf16[3,224,512]{2,1,0:T(8,128)(2,1)S(1)}, bf16[3,224,512]{2,1,0:T(8,128)(2,1)S(1)}, u32[]{:S(2)}, u32[]{:S(2)}) collective-permute-start(bf16[3,224,512]{2,1,0:T(8,128)(2,1)S(1)} %collective-permute-done.refs_1_), channel_id=1, source_target_pairs={{0,96},{32,0},{64,32},{96,64},{1,97},{33,1},{65,33},{97,65},{2,98}... | collective-permute-start | bytes 2064392 | tf_op jit(solution)/shard_map/ppermute | solution.py:366
  88.1 14.7 %collective-permute-done.1.refs_2_ = bf16[3,224,512]{2,1,0:T(8,128)(2,1)S(1)} collective-permute-done((bf16[3,224,512]{2,1,0:T(8,128)(2,1)S(1)}, bf16[3,224,512]{2,1,0:T(8,128)(2,1)S(1)}, u32[]{:S(2)}, u32[]{:S(2)}) %collective-permute-start.1) | collective-permute-done | bytes 688160 | tf_op jit(solution)/shard_map/ppermute | solution.py:366
  102.8 0.8 copy-done.9
  103.7 12.4 %shard_map.104 = (f32[3,896,512]{2,1,0:T(8,128)}, f32[1024,512]{1,0:T(8,128)}, f32[8,1024]{1,0:T(8,128)S(1)}) custom-call(bf16[32,64,512]{2,1,0:T(8,128)(2,1)} %copy-done.5, bf16[3,224,512]{2,1,0:T(8,128)(2,1)} %copy-done.8, bf16[3,224,512]{2,1,0:T(8,128)(2,1)} %copy-done.9, bf16[3,224,512]{2,1,0:T(8,128)(2,1)} %copy-done.7, bf16[3,224,512]{2,1,0:T(8,128)(2,1)} %copy-done.6), custom_call_target="tpu_custom_call" | custom-call | tf_op jit(solution)/shard_map/pallas_call | solution.py:244
  116.2 0.4 collective-permute-done.4.refs_1_
  116.6 0.4 copy-done.11
  117.0 0.2 copy-done.12
  117.2 0.2 copy-done.13
  117.4 12.7 %shard_map.105 = (f32[3,896,512]{2,1,0:T(8,128)}, bf16[32,72,512]{2,1,0:T(8,128)(2,1)}, f32[8,1024]{1,0:T(8,128)S(1)}) custom-call(bf16[32,64,512]{2,1,0:T(8,128)(2,1)} %copy-done.5, bf16[3,224,512]{2,1,0:T(8,128)(2,1)} %copy-done.13, bf16[3,224,512]{2,1,0:T(8,128)(2,1)} %copy-done.12, bf16[3,224,512]{2,1,0:T(8,128)(2,1)} %copy-done.11, ...), custom_call_target="tpu_custom_call" | custom-call | tf_op jit(solution)/shard_map/pallas_call | solution.py:244
  130.1 12.8 %shard_map.106 = (bf16[3,224,512]{2,1,0:T(8,128)(2,1)}, bf16[3,224,512]{2,1,0:T(8,128)(2,1)}, bf16[3,224,512]{2,1,0:T(8,128)(2,1)}, bf16[3,224,512]{2,1,0:T(8,12...) custom-call(bf16[32,64,512]{2,1,0:T(8,128)(2,1)S(1)} %all-to-all-done.refs_0_, bf16[3,224,512]{2,1,0:T(8,128)(2,1)} %copy-done.13, ...), custom_call_target="tpu_custom_call" | custom-call | tf_op jit(solution)/shard_map/pallas_call | solution.py:244
  142.9 0.3 collective-permute-start.7
  143.2 12.7 %shard_map.107 = (bf16[3,224,512]{2,1,0:T(8,128)(2,1)}, bf16[3,224,512]{2,1,0:T(8,128)(2,1)}, bf16[3,224,512]{2,1,0:T(8,128)(2,1)}, bf16[3,224,512]{2,1,0:T(8,128)(2,1)}, bf16[32,72,512]{2,1,0:T(8,128)(2,1)}) custom-call(bf16[32,64,512]{2,1,0:T(8,128)(2,1)S(1)} %all-to-all-done.refs_0_, ...), custom_call_target="tpu_custom_call", output_to_operand_aliasing={{4}: (9, {})} | custom-call | tf_op jit(solution)/shard_map/pallas_call | solution.py:244
  155.9 7.5 %all-to-all-start.2 = ((bf16[32,72,512]{2,1,0:T(8,128)(2,1)}), bf16[32,72,512]{2,1,0:T(8,128)(2,1)S(1)}, u32[]{:S(2)}, u32[]{:S(2)}) async-start(bf16[32,72,512]{2,1,0:T(8,128)(2,1)} %get-tuple-element.35), calls=%async_computation.2 | async-start | bytes 4718592 | tf_op jit(solution)/shard_map/all_to_all | solution.py:374
  163.5 3.3 %collective-permute-start.12 = (bf16[3,224,512]{2,1,0:T(8,128)(2,1)}, bf16[3,224,512]{2,1,0:T(8,128)(2,1)S(1)}, u32[]{:S(2)}, u32[]{:S(2)}) collective-permute-start(bf16[3,224,512]{2,1,0:T(8,128)(2,1)} %get-tuple-element.45), channel_id=1, source_target_pairs={{0,96},{32,0},{64,32},{96,64},{1,97},{33,1},{65,33},{97,65},{2,98}... | collective-permute-start | bytes 2064392 | tf_op jit(solution)/shard_map/ppermute | solution.py:366
  166.8 0.1 collective-permute-start.9
  166.9 1.3 add_convert_fusion.2
  168.2 2.0 collective-permute-start.8
  170.2 0.1 collective-permute-start.11
  170.3 12.7 %collective-permute-done.12 = bf16[3,224,512]{2,1,0:T(8,128)(2,1)S(1)} collective-permute-done((bf16[3,224,512]{2,1,0:T(8,128)(2,1)}, bf16[3,224,512]{2,1,0:T(8,128)(2,1)S(1)}, u32[]{:S(2)}, u32[]{:S(2)}) %collective-permute-start.12) | collective-permute-done | bytes 688160 | tf_op jit(solution)/shard_map/ppermute | solution.py:366
  182.9 0.2 add_convert_fusion
  183.1 3.7 %collective-permute-start.13 = (bf16[3,224,512]{2,1,0:T(8,128)(2,1)S(1)}, bf16[3,224,512]{2,1,0:T(8,128)(2,1)S(1)}, u32[]{:S(2)}, u32[]{:S(2)}) collective-permute-start(bf16[3,224,512]{2,1,0:T(8,128)(2,1)S(1)} %add_convert_fusion), channel_id=1, source_target_pairs={{0,96},{32,0},{64,32},{96,64},{1,97},{33,1},{65,33},{97,65},{2,98}... | collective-permute-start | bytes 2064392 | tf_op jit(solution)/shard_map/ppermute | solution.py:366
  186.8 10.9 %collective-permute-done.9 = bf16[3,224,512]{2,1,0:T(8,128)(2,1)S(1)} collective-permute-done((bf16[3,224,512]{2,1,0:T(8,128)(2,1)}, bf16[3,224,512]{2,1,0:T(8,128)(2,1)S(1)}, u32[]{:S(2)}, u32[]{:S(2)}) %collective-permute-start.9) | collective-permute-done | bytes 688160 | tf_op jit(solution)/shard_map/ppermute | solution.py:366
  197.7 0.3 add_convert_fusion.1
  198.0 3.4 %collective-permute-start.10 = (bf16[3,224,512]{2,1,0:T(8,128)(2,1)S(1)}, bf16[3,224,512]{2,1,0:T(8,128)(2,1)S(1)}, u32[]{:S(2)}, u32[]{:S(2)}) collective-permute-start(bf16[3,224,512]{2,1,0:T(8,128)(2,1)S(1)} %add_convert_fusion.1), channel_id=1, source_target_pairs={{0,16},{16,0},{1,17},{17,1},{2,18},{18,2},{3,19},{19,3},{4,20},{20... | collective-permute-start | bytes 2064392 | tf_op jit(solution)/shard_map/ppermute | solution.py:370
  201.3 0.2 collective-permute-done.11.own1
  201.5 10.1 %collective-permute-done.13.own2 = bf16[3,224,512]{2,1,0:T(8,128)(2,1)S(1)} collective-permute-done((bf16[3,224,512]{2,1,0:T(8,128)(2,1)S(1)}, bf16[3,224,512]{2,1,0:T(8,128)(2,1)S(1)}, u32[]{:S(2)}, u32[]{:S(2)}) %collective-permute-start.13) | collective-permute-done | bytes 688160 | tf_op jit(solution)/shard_map/ppermute | solution.py:366
  211.6 1.1 final_own.1
  212.7 2.9 %collective-permute-done.10.other = bf16[3,224,512]{2,1,0:T(8,128)(2,1)S(1)} collective-permute-done((bf16[3,224,512]{2,1,0:T(8,128)(2,1)S(1)}, bf16[3,224,512]{2,1,0:T(8,128)(2,1)S(1)}, u32[]{:S(2)}, u32[]{:S(2)}) %collective-permute-start.10) | collective-permute-done | bytes 688160 | tf_op jit(solution)/shard_map/ppermute | solution.py:370
  215.6 0.9 final_other.1
  216.5 4.8 %combine.1 = (bf16[128,4096]{1,0:T(8,128)(2,1)}, f32[8,1024]{1,0:T(8,128)S(1)}) custom-call(f32[8,1024]{1,0:T(8,128)S(1)} %maximum_bitcast_fusion.table, bf16[32,72,512]{2,1,0:T(8,128)(2,1)S(1)} %all-to-all-done.2.back), custom_call_target="tpu_custom_call" | custom-call | tf_op jit(solution)/shard_map/combine/pallas_call | solution.py:308
  221.3 0.6 slice_bitcast_fusion
  (42 shorter events, 0.1 us)
Async XLA Ops:
  2.2 1.2 copy-start
  3.4 1.2 copy-start.2
  8.5 8.6 %copy-start.17 = (bf16[2,224,512]{2,1,0:T(8,128)(2,1)S(1)}, bf16[2,224,512]{2,1,0:T(8,128)(2,1)}, u32[]{:S(2)}) copy-start(bf16[2,224,512]{2,1,0:T(8,128)(2,1)} %param.13) | copy-start | bytes 1376260
  8.5 36.4 %all-to-all-start.1 = ((bf16[32,64,512]{2,1,0:T(8,128)(2,1)}), bf16[32,64,512]{2,1,0:T(8,128)(2,1)S(1)}, u32[]{:S(2)}, u32[]{:S(2)}) async-start(bf16[32,64,512]{2,1,0:T(8,128)(2,1)} %shard_map.103), calls=%async_computation.1 | async-start | bytes 4194304 | tf_op jit(solution)/shard_map/all_to_all | solution.py:374
  17.1 5.8 %copy-start.1 = (bf16[128,4096]{1,0:T(8,128)(2,1)S(1)}, bf16[128,4096]{1,0:T(8,128)(2,1)}, u32[]{:S(2)}) copy-start(bf16[128,4096]{1,0:T(8,128)(2,1)} %tok.3) | copy-start | bytes 3145732
  17.1 5.8 %copy-start.3 = (bf16[128,4096]{1,0:T(8,128)(2,1)S(1)}, bf16[128,4096]{1,0:T(8,128)(2,1)}, u32[]{:S(2)}) copy-start(bf16[128,4096]{1,0:T(8,128)(2,1)} %cot.3) | copy-start | bytes 3145732
  19.5 49.0 %copy-start.6 = (bf16[3,224,512]{2,1,0:T(8,128)(2,1)}, bf16[3,224,512]{2,1,0:T(8,128)(2,1)S(1)}, u32[]{:S(2)}) copy-start(bf16[3,224,512]{2,1,0:T(8,128)(2,1)S(1)} %get-tuple-element.53.refs_4_) | copy-start | bytes 2064388
  19.5 49.0 %collective-permute-start.2 = (bf16[3,224,512]{2,1,0:T(8,128)(2,1)}, bf16[3,224,512]{2,1,0:T(8,128)(2,1)S(1)}, u32[]{:S(2)}, u32[]{:S(2)}) collective-permute-start(bf16[3,224,512]{2,1,0:T(8,128)(2,1)} %get-tuple-element.52), channel_id=1, source_target_pairs={{0,16},{16,0},{1,17},{17,1},{2,18},{18,2},{3,19},{19,3},{4,20},{20... | collective-permute-start | bytes 2064392 | tf_op jit(solution)/shard_map/ppermute | solution.py:370
  44.8 1.3 copy-start.5
  46.1 84.0 %all-to-all-start = ((bf16[32,64,512]{2,1,0:T(8,128)(2,1)}), bf16[32,64,512]{2,1,0:T(8,128)(2,1)S(1)}, u32[]{:S(2)}, u32[]{:S(2)}) async-start(bf16[32,64,512]{2,1,0:T(8,128)(2,1)} %shard_map.102), calls=%async_computation | async-start | bytes 4194304 | tf_op jit(solution)/shard_map/all_to_all | solution.py:374
  65.7 18.7 %collective-permute-start = (bf16[3,224,512]{2,1,0:T(8,128)(2,1)S(1)}, bf16[3,224,512]{2,1,0:T(8,128)(2,1)S(1)}, u32[]{:S(2)}, u32[]{:S(2)}) collective-permute-start(bf16[3,224,512]{2,1,0:T(8,128)(2,1)S(1)} %get-tuple-element.53.refs_4_), channel_id=1, source_target_pairs={{0,96},{32,0},{64,32},{96,64},{1,97},{33,1},{65,33},{97,65},{2,98}... | collective-permute-start | bytes 2064392 | tf_op jit(solution)/shard_map/ppermute | solution.py:366
  68.5 34.3 %copy-start.7 = (bf16[3,224,512]{2,1,0:T(8,128)(2,1)}, bf16[3,224,512]{2,1,0:T(8,128)(2,1)S(1)}, u32[]{:S(2)}) copy-start(bf16[3,224,512]{2,1,0:T(8,128)(2,1)S(1)} %collective-permute-done.2.refs_3_) | copy-start | bytes 2064388
  68.5 19.5 %collective-permute-start.3 = (bf16[3,224,512]{2,1,0:T(8,128)(2,1)S(1)}, bf16[3,224,512]{2,1,0:T(8,128)(2,1)S(1)}, u32[]{:S(2)}, u32[]{:S(2)}) collective-permute-start(bf16[3,224,512]{2,1,0:T(8,128)(2,1)S(1)} %collective-permute-done.2.refs_3_), channel_id=1, source_target_pairs={{0,32},{32,64},{64,96},{96,0},{1,33},{33,65},{65,97},{97,1},{2,34}... | collective-permute-start | bytes 2064392 | tf_op jit(solution)/shard_map/ppermute | solution.py:366
  68.6 34.2 %collective-permute-start.1 = (bf16[3,224,512]{2,1,0:T(8,128)(2,1)S(1)}, bf16[3,224,512]{2,1,0:T(8,128)(2,1)S(1)}, u32[]{:S(2)}, u32[]{:S(2)}) collective-permute-start(bf16[3,224,512]{2,1,0:T(8,128)(2,1)S(1)} %get-tuple-element.53.refs_4_), channel_id=1, source_target_pairs={{0,32},{32,64},{64,96},{96,0},{1,33},{33,65},{65,97},{97,1},{2,34}... | collective-permute-start | bytes 2064392 | tf_op jit(solution)/shard_map/ppermute | solution.py:366
  69.3 46.8 %collective-permute-start.6 = (bf16[3,224,512]{2,1,0:T(8,128)(2,1)S(1)}, bf16[3,224,512]{2,1,0:T(8,128)(2,1)S(1)}, u32[]{:S(2)}, u32[]{:S(2)}) collective-permute-start(bf16[3,224,512]{2,1,0:T(8,128)(2,1)S(1)} %collective-permute-done.2.refs_3_), channel_id=1, source_target_pairs={{0,96},{32,0},{64,32},{96,64},{1,97},{33,1},{65,33},{97,65},{2,98}... | collective-permute-start | bytes 2064392 | tf_op jit(solution)/shard_map/ppermute | solution.py:366
  84.4 18.4 %copy-start.8 = (bf16[3,224,512]{2,1,0:T(8,128)(2,1)}, bf16[3,224,512]{2,1,0:T(8,128)(2,1)S(1)}, u32[]{:S(2)}) copy-start(bf16[3,224,512]{2,1,0:T(8,128)(2,1)S(1)} %collective-permute-done.refs_1_) | copy-start | bytes 2064388
  84.4 31.8 %collective-permute-start.5 = (bf16[3,224,512]{2,1,0:T(8,128)(2,1)S(1)}, bf16[3,224,512]{2,1,0:T(8,128)(2,1)S(1)}, u32[]{:S(2)}, u32[]{:S(2)}) collective-permute-start(bf16[3,224,512]{2,1,0:T(8,128)(2,1)S(1)} %collective-permute-done.refs_1_), channel_id=1, source_target_pairs={{0,96},{32,0},{64,32},{96,64},{1,97},{33,1},{65,33},{97,65},{2,98}... | collective-permute-start | bytes 2064392 | tf_op jit(solution)/shard_map/ppermute | solution.py:366
  88.1 28.5 %copy-start.10 = (bf16[3,224,512]{2,1,0:T(8,128)(2,1)}, bf16[3,224,512]{2,1,0:T(8,128)(2,1)S(1)}, u32[]{:S(2)}) copy-start(bf16[3,224,512]{2,1,0:T(8,128)(2,1)S(1)} %collective-permute-done.3.refs_4_) | copy-start | bytes 2064388
  88.1 28.5 %collective-permute-start.4 = (bf16[3,224,512]{2,1,0:T(8,128)(2,1)S(1)}, bf16[3,224,512]{2,1,0:T(8,128)(2,1)S(1)}, u32[]{:S(2)}, u32[]{:S(2)}) collective-permute-start(bf16[3,224,512]{2,1,0:T(8,128)(2,1)S(1)} %collective-permute-done.3.refs_4_), channel_id=1, source_target_pairs={{0,32},{32,64},{64,96},{96,0},{1,33},{33,65},{65,97},{97,1},{2,34}... | collective-permute-start | bytes 2064392 | tf_op jit(solution)/shard_map/ppermute | solution.py:366
  102.8 0.8 copy-start.9
  116.1 0.8 copy-start.11
  116.1 1.1 copy-start.12
  116.6 0.8 copy-start.13
  142.9 23.9 %collective-permute-start.7 = (bf16[3,224,512]{2,1,0:T(8,128)(2,1)}, bf16[3,224,512]{2,1,0:T(8,128)(2,1)}, u32[]{:S(2)}, u32[]{:S(2)}) collective-permute-start(bf16[3,224,512]{2,1,0:T(8,128)(2,1)} %get-tuple-element.40), channel_id=1, source_target_pairs={{0,32},{32,64},{64,96},{96,0},{1,33},{33,65},{65,97},{97,1},{2,34}... | collective-permute-start | bytes 2064392 | tf_op jit(solution)/shard_map/ppermute | solution.py:366
  155.9 10.9 %copy-start.16 = (bf16[3,224,512]{2,1,0:T(8,128)(2,1)S(1)}, bf16[3,224,512]{2,1,0:T(8,128)(2,1)}, u32[]{:S(2)}) copy-start(bf16[3,224,512]{2,1,0:T(8,128)(2,1)} %get-tuple-element.39) | copy-start | bytes 2064388
  155.9 60.5 %all-to-all-start.2 = ((bf16[32,72,512]{2,1,0:T(8,128)(2,1)}), bf16[32,72,512]{2,1,0:T(8,128)(2,1)S(1)}, u32[]{:S(2)}, u32[]{:S(2)}) async-start(bf16[32,72,512]{2,1,0:T(8,128)(2,1)} %get-tuple-element.35), calls=%async_computation.2 | async-start | bytes 4718592 | tf_op jit(solution)/shard_map/all_to_all | solution.py:374
  163.5 6.7 %copy-start.18 = (bf16[3,224,512]{2,1,0:T(8,128)(2,1)S(1)}, bf16[3,224,512]{2,1,0:T(8,128)(2,1)}, u32[]{:S(2)}) copy-start(bf16[3,224,512]{2,1,0:T(8,128)(2,1)} %get-tuple-element.43) | copy-start | bytes 2064388
  163.5 19.4 %copy-start.15 = (bf16[3,224,512]{2,1,0:T(8,128)(2,1)S(1)}, bf16[3,224,512]{2,1,0:T(8,128)(2,1)}, u32[]{:S(2)}) copy-start(bf16[3,224,512]{2,1,0:T(8,128)(2,1)} %get-tuple-element.44) | copy-start | bytes 2064388
  163.5 19.4 %collective-permute-start.12 = (bf16[3,224,512]{2,1,0:T(8,128)(2,1)}, bf16[3,224,512]{2,1,0:T(8,128)(2,1)S(1)}, u32[]{:S(2)}, u32[]{:S(2)}) collective-permute-start(bf16[3,224,512]{2,1,0:T(8,128)(2,1)} %get-tuple-element.45), channel_id=1, source_target_pairs={{0,96},{32,0},{64,32},{96,64},{1,97},{33,1},{65,33},{97,65},{2,98}... | collective-permute-start | bytes 2064392 | tf_op jit(solution)/shard_map/ppermute | solution.py:366
  166.8 30.9 %collective-permute-start.9 = (bf16[3,224,512]{2,1,0:T(8,128)(2,1)}, bf16[3,224,512]{2,1,0:T(8,128)(2,1)S(1)}, u32[]{:S(2)}, u32[]{:S(2)}) collective-permute-start(bf16[3,224,512]{2,1,0:T(8,128)(2,1)} %get-tuple-element.41), channel_id=1, source_target_pairs={{0,96},{32,0},{64,32},{96,64},{1,97},{33,1},{65,33},{97,65},{2,98}... | collective-permute-start | bytes 2064392 | tf_op jit(solution)/shard_map/ppermute | solution.py:366
  168.1 29.5 %copy-start.14 = (bf16[3,224,512]{2,1,0:T(8,128)(2,1)S(1)}, bf16[3,224,512]{2,1,0:T(8,128)(2,1)}, u32[]{:S(2)}) copy-start(bf16[3,224,512]{2,1,0:T(8,128)(2,1)} %get-tuple-element.38) | copy-start | bytes 2064388
  168.2 29.5 %collective-permute-start.8 = (bf16[3,224,512]{2,1,0:T(8,128)(2,1)S(1)}, bf16[3,224,512]{2,1,0:T(8,128)(2,1)S(1)}, u32[]{:S(2)}, u32[]{:S(2)}) collective-permute-start(bf16[3,224,512]{2,1,0:T(8,128)(2,1)S(1)} %add_convert_fusion.2), channel_id=1, source_target_pairs={{0,32},{32,64},{64,96},{96,0},{1,33},{33,65},{65,97},{97,1},{2,34}... | collective-permute-start | bytes 2064392 | tf_op jit(solution)/shard_map/ppermute | solution.py:366
  170.2 31.3 %collective-permute-start.11 = (bf16[3,224,512]{2,1,0:T(8,128)(2,1)S(1)}, bf16[3,224,512]{2,1,0:T(8,128)(2,1)S(1)}, u32[]{:S(2)}, u32[]{:S(2)}) collective-permute-start(bf16[3,224,512]{2,1,0:T(8,128)(2,1)S(1)} %copy-done.18), channel_id=1, source_target_pairs={{0,32},{32,64},{64,96},{96,0},{1,33},{33,65},{65,97},{97,1},{2,34}... | collective-permute-start | bytes 2064392 | tf_op jit(solution)/shard_map/ppermute | solution.py:366
  183.1 28.5 %collective-permute-start.13 = (bf16[3,224,512]{2,1,0:T(8,128)(2,1)S(1)}, bf16[3,224,512]{2,1,0:T(8,128)(2,1)S(1)}, u32[]{:S(2)}, u32[]{:S(2)}) collective-permute-start(bf16[3,224,512]{2,1,0:T(8,128)(2,1)S(1)} %add_convert_fusion), channel_id=1, source_target_pairs={{0,96},{32,0},{64,32},{96,64},{1,97},{33,1},{65,33},{97,65},{2,98}... | collective-permute-start | bytes 2064392 | tf_op jit(solution)/shard_map/ppermute | solution.py:366
  197.7 13.9 %copy-start.4 = (bf16[3,224,512]{2,1,0:T(8,128)(2,1)S(1)}, bf16[3,224,512]{2,1,0:T(8,128)(2,1)}, u32[]{:S(2)}) copy-start(bf16[3,224,512]{2,1,0:T(8,128)(2,1)} %get-tuple-element.42.own0) | copy-start | bytes 2064388
  198.0 17.7 %collective-permute-start.10 = (bf16[3,224,512]{2,1,0:T(8,128)(2,1)S(1)}, bf16[3,224,512]{2,1,0:T(8,128)(2,1)S(1)}, u32[]{:S(2)}, u32[]{:S(2)}) collective-permute-start(bf16[3,224,512]{2,1,0:T(8,128)(2,1)S(1)} %add_convert_fusion.1), channel_id=1, source_target_pairs={{0,16},{16,0},{1,17},{17,1},{2,18},{18,2},{3,19},{19,3},{4,20},{20... | collective-permute-start | bytes 2064392 | tf_op jit(solution)/shard_map/ppermute | solution.py:370
